TPU v7x, 32 devices: a whole 2x2x4 slice. The times are simulated.
32 devices in a mesh: dp: 8 (over y, x, core), tensor: 4 (over z).
Axes of the slice: x: 2, y: 2, z: 4, core: 2. Of those that a mesh axis runs over, the one named last changes fastest.
Arguments:
- block_input: bfloat16 [8192, 2048], P('dp'), may hold values from -6 to 6
- image_starts: int32 [8, 2], P('dp'), may hold values from 0 to 768, as said below
- norm_gain: bfloat16 [2048], replicated, may hold values from 0.5 to 1.5
- q_down: bfloat16 [2048, 1024], replicated, may hold values from -0.125 to 0.125
- q_gain: bfloat16 [1024], replicated, may hold values from 0.5 to 1.5
- q_up: bfloat16 [1024, 4096], P(None, 'tensor'), may hold values from -0.1875 to 0.1875
- k_proj: bfloat16 [2048, 256], replicated, may hold values from -0.25 to 0.25
- v_proj: bfloat16 [2048, 256], replicated, may hold values from -0.125 to 0.125
- out_proj: bfloat16 [4096, 2048], P('tensor'), may hold values from -0.75 to 0.75
- mlp_gain: bfloat16 [2048], replicated, may hold values from 0.5 to 1.5
- w_gate: bfloat16 [2048, 5632], P(None, 'tensor'), may hold values from -0.125 to 0.125
- w_up: bfloat16 [2048, 5632], P(None, 'tensor'), may hold values from -0.125 to 0.125
- w_down: bfloat16 [5632, 2048], P('tensor'), may hold values from -0.078125 to 0.078125
- d_output: bfloat16 [8192, 2048], P('dp'), may hold values from -6 to 6
Outputs:
- block_output: bfloat16 [8192, 2048], P('dp')
- grad_input: bfloat16 [8192, 2048], P('dp')
- grad_norm_gain: float32 [2048], P(('dp', 'tensor'))
- grad_q_down: float32 [2048, 1024], P(('dp', 'tensor'))
- grad_q_gain: float32 [1024], P(('dp', 'tensor'))
- grad_q_up: float32 [1024, 4096], P('dp', 'tensor')
- grad_k_proj: float32 [2048, 256], P(('dp', 'tensor'))
- grad_v_proj: float32 [2048, 256], P(('dp', 'tensor'))
- grad_out_proj: float32 [4096, 2048], P('tensor', 'dp')
- grad_mlp_gain: float32 [2048], P(('dp', 'tensor'))
- grad_w_gate: float32 [2048, 5632], P('dp', 'tensor')
- grad_w_up: float32 [2048, 5632], P('dp', 'tensor')
- grad_w_down: float32 [5632, 2048], P('tensor', 'dp')
Inputs may be any that keep to these rules, and one draw needn't show every extreme that they name: `image_starts`: each row holds the ascending starts of 2 image pieces of 256 positions of one sequence; the pieces lie inside the sequence and never intersect.
All inputs are finite; a program needn't handle non-finite values.
Results may differ from a plain program's by a relative error of at most 0.017.
The roundings to bfloat16 on the way count: a program that leaves them out, or rounds other values in their place, can miss the bound.
Values sent between devices are 32-bit elements; how exact they have to be, the bound alone decides.
A program may use at most 256 MiB of HBM per device.

v0:
```python
import jax
import jax.numpy as jnp
from jax import lax
from jax.sharding import PartitionSpec as P

PIECE = 256


epsilon = 1e-06
masked_score = -1e30


def normalize(values):
    scale_rows = lax.rsqrt(jnp.mean(values * values, axis=-1, keepdims=True) + epsilon)
    return (values * scale_rows, scale_rows)


def norm_back(grad_normed, normed, scale_rows):
    return scale_rows * (
        grad_normed - normed * jnp.mean(grad_normed * normed, axis=-1, keepdims=True)
    )


def left_dot(left, right):
    return lax.dot_general(
        left, right, (((0,), (0,)), ((), ())), preferred_element_type=jnp.float32
    )


def right_dot(left, right):
    return lax.dot_general(
        left, right, (((1,), (1,)), ((), ())), preferred_element_type=jnp.float32
    )


def rotate(values, cos_tab, sin_tab):
    half = values.shape[-1] // 2
    first_half = values[..., :half]
    second_half = values[..., half:]
    return jnp.concatenate(
        [
            first_half * cos_tab - second_half * sin_tab,
            second_half * cos_tab + first_half * sin_tab,
        ],
        axis=-1,
    )


def unrotate(grads, cos_tab, sin_tab):
    half = grads.shape[-1] // 2
    first_half = grads[..., :half]
    second_half = grads[..., half:]
    return jnp.concatenate(
        [
            first_half * cos_tab + second_half * sin_tab,
            second_half * cos_tab - first_half * sin_tab,
        ],
        axis=-1,
    )


def shards(
    block_input,
    image_starts,
    norm_gain,
    q_down,
    q_gain,
    q_up,
    k_proj,
    v_proj,
    out_proj,
    mlp_gain,
    w_gate,
    w_up,
    w_down,
    d_output,
):
    row_count, model_width = block_input.shape
    seq_count = image_starts.shape[0]
    seq_len = row_count // seq_count
    head_dim = k_proj.shape[1]
    head_count = q_up.shape[1] // head_dim
    block_rows = min(512, seq_len)
    block_count = seq_len // block_rows
    score_scale = head_dim ** (-0.5)
    positions = jnp.arange(seq_len, dtype=jnp.float32)
    inv_freq = 10000.0 ** (-(jnp.arange(head_dim // 2, dtype=jnp.float32) * 2.0) / head_dim)
    angles = positions[:, None] * inv_freq[None, :]
    cos_all = jnp.tile(jnp.cos(angles), (seq_count, 1))
    sin_all = jnp.tile(jnp.sin(angles), (seq_count, 1))
    pos_int = jnp.arange(seq_len, dtype=jnp.int32)
    inside = (pos_int[None, :, None] >= image_starts[:, None, :]) & (
        pos_int[None, :, None] < image_starts[:, None, :] + PIECE
    )
    labels = jnp.arange(1, image_starts.shape[1] + 1, dtype=jnp.int32)
    piece_ids = jnp.sum(jnp.where(inside, labels, 0), axis=2)

    def block_scores(q_block, key_rows, seq_ids, row_start):
        raw = (
            jnp.einsum("qhd,kd->hqk", q_block, key_rows, preferred_element_type=jnp.float32)
            * score_scale
        )
        query_pos = row_start + jnp.arange(block_rows, dtype=jnp.int32)
        query_ids = lax.dynamic_slice_in_dim(seq_ids, row_start, block_rows)
        visible = (pos_int[None, :] <= query_pos[:, None]) | (
            query_ids[:, None] == seq_ids[None, :]
        ) & (query_ids[:, None] > 0)
        return jnp.where(visible[None], raw, masked_score)

    input_f32 = block_input.astype(jnp.float32)
    gain_attn = norm_gain.astype(jnp.float32)
    gain_query = q_gain.astype(jnp.float32)
    gain_mlp = mlp_gain.astype(jnp.float32)
    cotan_f32 = d_output.astype(jnp.float32)
    normed_one, scale_one = normalize(input_f32)
    normed_in = (normed_one * gain_attn).astype(jnp.bfloat16)
    q_latent = jnp.dot(normed_in, q_down, preferred_element_type=jnp.float32)
    q_unit, q_scale = normalize(q_latent)
    q_normed = (q_unit * gain_query).astype(jnp.bfloat16)
    q_raw = jnp.dot(q_normed, q_up, preferred_element_type=jnp.float32).reshape(
        row_count, head_count, head_dim
    )
    queries = rotate(q_raw, cos_all[:, None, :], sin_all[:, None, :]).astype(jnp.bfloat16)
    key_rows = rotate(
        jnp.dot(normed_in, k_proj, preferred_element_type=jnp.float32), cos_all, sin_all
    ).astype(jnp.bfloat16)
    val_rows = jnp.dot(normed_in, v_proj, preferred_element_type=jnp.float32).astype(jnp.bfloat16)
    query_seq = queries.reshape(seq_count, block_count, block_rows, head_count, head_dim)
    key_seq = key_rows.reshape(seq_count, seq_len, head_dim)
    val_seq = val_rows.reshape(seq_count, seq_len, head_dim)
    block_ids = jnp.arange(block_count, dtype=jnp.int32)

    def forward_seq(seq_item):
        q_all, seq_keys, seq_vals, seq_ids = seq_item

        def forward_block(block_item):
            q_block, blk_index = block_item
            scores = block_scores(q_block, seq_keys, seq_ids, blk_index * block_rows)
            row_max = jnp.max(scores, axis=-1, keepdims=True)
            exp_terms = jnp.exp(scores - row_max)
            row_sum = jnp.sum(exp_terms, axis=-1, keepdims=True)
            attn_probs = (exp_terms / row_sum).astype(jnp.bfloat16)
            mixed_block = jnp.einsum(
                "hqk,kd->qhd", attn_probs, seq_vals, preferred_element_type=jnp.float32
            )
            return (mixed_block.astype(jnp.bfloat16), (row_max + jnp.log(row_sum))[..., 0])

        return lax.map(forward_block, (q_all, block_ids))

    mixed_seq, log_norm = lax.map(forward_seq, (query_seq, key_seq, val_seq, piece_ids))
    mixed_heads = mixed_seq.reshape(row_count, head_count * head_dim)
    attn_out = lax.psum(
        jnp.dot(mixed_heads, out_proj, preferred_element_type=jnp.float32), "tensor"
    )
    hidden_in = input_f32 + attn_out
    normed_two, scale_two = normalize(hidden_in)
    normed_mid = (normed_two * gain_mlp).astype(jnp.bfloat16)
    gate_pre = jnp.dot(normed_mid, w_gate, preferred_element_type=jnp.float32)
    up_pre = jnp.dot(normed_mid, w_up, preferred_element_type=jnp.float32)
    gate_sig = jax.nn.sigmoid(gate_pre)
    hidden_act = (gate_pre * gate_sig * up_pre).astype(jnp.bfloat16)
    mlp_out = lax.psum(jnp.dot(hidden_act, w_down, preferred_element_type=jnp.float32), "tensor")
    block_output = (hidden_in + mlp_out).astype(jnp.bfloat16)
    grad_down = left_dot(hidden_act, d_output)
    d_act = right_dot(d_output, w_down)
    d_gate = (d_act * up_pre * gate_sig * (1.0 + gate_pre * (1.0 - gate_sig))).astype(jnp.bfloat16)
    d_up = (d_act * gate_pre * gate_sig).astype(jnp.bfloat16)
    grad_gate = left_dot(normed_mid, d_gate)
    grad_up = left_dot(normed_mid, d_up)
    d_mid = lax.psum(right_dot(d_gate, w_gate) + right_dot(d_up, w_up), "tensor")
    grad_gain_mlp = jnp.sum(d_mid * normed_two, axis=0)
    d_hidden = cotan_f32 + norm_back(d_mid * gain_mlp, normed_two, scale_two)
    d_hidden_low = d_hidden.astype(jnp.bfloat16)
    grad_out = left_dot(mixed_heads, d_hidden_low)
    d_mixed = right_dot(d_hidden_low, out_proj).astype(jnp.bfloat16)
    d_mixed_seq = d_mixed.reshape(seq_count, block_count, block_rows, head_count, head_dim)

    def backward_seq(seq_item):
        q_all, dm_all, norm_all, seq_keys, seq_vals, seq_ids = seq_item

        def backward_block(sums_pair, block_item):
            key_sum, val_sum = sums_pair
            q_block, dm_block, norm_block, blk_index = block_item
            scores = block_scores(q_block, seq_keys, seq_ids, blk_index * block_rows)
            attn_probs = jnp.exp(scores - norm_block[..., None])
            d_probs = jnp.einsum(
                "qhd,kd->hqk", dm_block, seq_vals, preferred_element_type=jnp.float32
            )
            d_scores = (
                attn_probs * (d_probs - jnp.sum(attn_probs * d_probs, axis=-1, keepdims=True))
            ).astype(jnp.bfloat16)
            d_query = (
                jnp.einsum("hqk,kd->qhd", d_scores, seq_keys, preferred_element_type=jnp.float32)
                * score_scale
            )
            key_sum = (
                key_sum
                + jnp.einsum("hqk,qhd->kd", d_scores, q_block, preferred_element_type=jnp.float32)
                * score_scale
            )
            val_sum = val_sum + jnp.einsum(
                "hqk,qhd->kd",
                attn_probs.astype(jnp.bfloat16),
                dm_block,
                preferred_element_type=jnp.float32,
            )
            return ((key_sum, val_sum), d_query)

        zero_rows = jnp.zeros((seq_len, head_dim), jnp.float32)
        (key_sum, val_sum), d_query = lax.scan(
            backward_block, (zero_rows, zero_rows), (q_all, dm_all, norm_all, block_ids)
        )
        return (key_sum, val_sum, d_query)

    key_grad, val_grad, query_grad = lax.map(
        backward_seq, (query_seq, d_mixed_seq, log_norm, key_seq, val_seq, piece_ids)
    )
    d_q_raw = unrotate(
        query_grad.reshape(row_count, head_count, head_dim),
        cos_all[:, None, :],
        sin_all[:, None, :],
    )
    d_q_raw = d_q_raw.reshape(row_count, head_count * head_dim).astype(jnp.bfloat16)
    key_val_part = jnp.concatenate(
        [key_grad.reshape(row_count, head_dim), val_grad.reshape(row_count, head_dim)], axis=1
    )
    grad_query_up = left_dot(q_normed, d_q_raw)
    d_bq_part = right_dot(d_q_raw, q_up)
    d_q_normed, key_val_full = lax.psum((d_bq_part, key_val_part), "tensor")
    d_key_low = unrotate(key_val_full[:, :head_dim], cos_all, sin_all).astype(jnp.bfloat16)
    d_val_low = key_val_full[:, head_dim:].astype(jnp.bfloat16)
    grad_gain_query = jnp.sum(d_q_normed * q_unit, axis=0)
    d_latent = norm_back(d_q_normed * gain_query, q_unit, q_scale).astype(jnp.bfloat16)
    d_normed_in = (
        right_dot(d_latent, q_down) + right_dot(d_key_low, k_proj) + right_dot(d_val_low, v_proj)
    )
    grad_gain_attn = jnp.sum(d_normed_in * normed_one, axis=0)
    grad_input = (d_hidden + norm_back(d_normed_in * gain_attn, normed_one, scale_one)).astype(
        jnp.bfloat16
    )
    grad_query_up, grad_out, grad_gate, grad_up, grad_down = (
        lax.psum_scatter(grad_query_up, "dp", scatter_dimension=0, tiled=True),
        lax.psum_scatter(grad_out, "dp", scatter_dimension=1, tiled=True),
        lax.psum_scatter(grad_gate, "dp", scatter_dimension=0, tiled=True),
        lax.psum_scatter(grad_up, "dp", scatter_dimension=0, tiled=True),
        lax.psum_scatter(grad_down, "dp", scatter_dimension=1, tiled=True),
    )
    tp_count = lax.axis_size("tensor")
    tp_index = lax.axis_index("tensor")
    summed = (
        lax.psum_scatter(left_dot(normed_in, d_latent), "dp", scatter_dimension=0, tiled=True),
        lax.psum_scatter(left_dot(normed_in, d_key_low), "dp", scatter_dimension=0, tiled=True),
        lax.psum_scatter(left_dot(normed_in, d_val_low), "dp", scatter_dimension=0, tiled=True),
        lax.psum_scatter(grad_gain_attn, "dp", scatter_dimension=0, tiled=True),
        lax.psum_scatter(grad_gain_query, "dp", scatter_dimension=0, tiled=True),
        lax.psum_scatter(grad_gain_mlp, "dp", scatter_dimension=0, tiled=True),
    )

    def pick_rows(summed_rows):
        own_count = summed_rows.shape[0] // tp_count
        return lax.dynamic_slice_in_dim(summed_rows, tp_index * own_count, own_count, 0)

    grad_qd, grad_key, grad_val, grad_g1, grad_gq, grad_g2 = tuple(
        (pick_rows(item) for item in summed)
    )
    return (
        block_output,
        grad_input,
        grad_g1,
        grad_qd,
        grad_gq,
        grad_query_up,
        grad_key,
        grad_val,
        grad_out,
        grad_g2,
        grad_gate,
        grad_up,
        grad_down,
    )


def solution(mesh):
    placed = (
        P("dp", None),
        P("dp", None),
        P(),
        P(),
        P(),
        P(None, "tensor"),
        P(),
        P(),
        P("tensor", None),
        P(),
        P(None, "tensor"),
        P(None, "tensor"),
        P("tensor", None),
        P("dp", None),
    )
    return jax.shard_map(
        shards,
        mesh=mesh,
        in_specs=placed,
        out_specs=(
            P("dp", None),
            P("dp", None),
            P(("dp", "tensor")),
            P(("dp", "tensor"), None),
            P(("dp", "tensor")),
            P("dp", "tensor"),
            P(("dp", "tensor"), None),
            P(("dp", "tensor"), None),
            P("tensor", "dp"),
            P(("dp", "tensor")),
            P("dp", "tensor"),
            P("dp", "tensor"),
            P("tensor", "dp"),
        ),
        check_vma=False,
    )
```

profile of v0, /device:TPU:0, one launch (start us, length us, event | category | flops | bytes accessed | tf_op | source)
XLA Modules:
  0.0 1899.2 jit_solution(2587256044341212786)
XLA Ops:
  9.3 3.1 fusion.59
  17.0 3.2 subtract_convert_fusion.3
  26.3 7.7 multiply_reduce_fusion.5
  44.7 3.0 subtract_convert_fusion.1
  49.5 25.1 %while.48 = (s32[]{:T(128)}, bf16[2,512,4,256]{3,2,1,0:T(4,128)(2,1)}, f32[2,4,512]{2,1,0:T(4,128)S(1)}, s32[2]{0:T(128)S(1)}, s32[1024]{0:T(1024)S(1)}, /*index...) while((s32[]{:T(128)}, ...), condition=%wide.region_6.7_spmd.clone, body=%wide.region_3.6_spmd.clone.sunk | while | flops 2175269888 | bytes 49364228 | solution.py:148
  78.1 6.8 fusion.79
  85.6 293.1 %all-reduce.9.cloned.1.call-done = f32[1024,2048]{1,0:T(8,128)} async-done(((f32[1024,2048]{1,0:T(8,128)}), f32[1024,2048]{1,0:T(8,128)}) %all-reduce.9.cloned.1.call-update) | async-done | bytes 8388624 | tf_op jit(solution)/shard_map/psum | solution.py:152
  378.6 5.7 multiply_reduce_fusion.2
  387.6 11.8 fusion.81
  399.4 10.4 fusion.80
  409.8 14.7 multiply_convert_fusion.1
  424.6 9.8 fusion.83
  434.4 11.0 convolution_add_fusion
  445.6 11.6 fusion.82
  457.2 278.3 %all-reduce.11.cloned.1.call-done = f32[1024,2048]{1,0:T(8,128)} async-done(((f32[1024,2048]{1,0:T(8,128)}), f32[1024,2048]{1,0:T(8,128)}) %all-reduce.11.cloned.1.call-update) | async-done | bytes 8388624 | tf_op jit(solution)/shard_map/psum | solution.py:170
  735.5 7.7 multiply_reduce_fusion
  744.9 4.6 multiply_add_fusion
  749.5 3.3 copy-done.6
  752.8 7.9 fusion.64
  760.8 4.5 squeeze.42
  765.3 41.3 %while.49 = (s32[]{:T(128)}, f32[1024,256]{1,0:T(8,128)}, f32[1024,256]{1,0:T(8,128)}, f32[2,512,4,256]{3,1,0,2:T(8,128)}, s32[2]{0:T(128)S(1)}, /*index=5*/s32[...) while((s32[]{:T(128)}, f32[1024,256]{1,0:T(8,128)}, ...), condition=%wide.region_14.15_spmd.clone, body=%wide.region_12.14_spmd.clone.sunk | while | flops 5404097536 | bytes 137960912 | solution.py:210
  774.9 3.4 fusion.162
  795.3 3.4 fusion.162
  806.6 3.0 add_convert_fusion.1
  811.1 4.1 copy.98
  819.4 6.0 fusion.89
  826.9 492.9 %all-reduce.13.cloned.1.call-done = (f32[1024,2048]{1,0:T(8,128)}, f32[1024,1024]{0,1:T(8,128)}, f32[1024,512]{0,1:T(8,128)}) async-done(((f32[1024,2048]{1,0:T(8,128)}, f32[1024,1024]{0,1:T(8,128)}, f32[1024,512]{0,1:T(8,128)}), (f32[1024,2048]{1,0:T(8,128)}, f32[1024,1024]{0,1:T(8,128)}, f32[1024,512]{0,1:T(8,128)})) %all-reduce.13.cloned.1.call-update) | async-done | bytes 14680080 | tf_op jit(solution)/shard_map/psum | solution.py:162
  1319.8 3.7 add_convert_fusion.3
  1324.2 4.8 fusion.69
  1329.1 5.2 fusion.71
  1334.5 5.1 multiply_reduce_fusion.3
  1344.1 7.0 fusion.85
  1351.3 7.3 fusion.75
  1358.6 11.6 fusion.88
  1370.3 11.9 fusion.87
  1382.2 12.1 fusion.86
  1394.7 12.0 fusion.60
  1412.1 6.9 fusion.84
  1419.1 8.7 fusion.58
  1427.8 25.4 %all-reduce.3 = (f32[2048]{0:T(1024)S(1)}, f32[1024]{0:T(1024)S(1)}, f32[2048]{0:T(1024)S(1)}) all-reduce(f32[2048]{0:T(1024)S(1)} %get-tuple-element.346, f32[1024]{0:T(1024)S(1)} %get-tuple-element.348, f32[2048]{0:T(1024)S(1)} %copy-done.42), channel_id=2, replica_groups=mesh['dp'=8,'tensor'=4] {'dp'}, use_global_device_ids=true, to_apply=%region_20.21.clone | all-reduce | flops 5120 | bytes 40960
  1455.0 9.8 add_convert_fusion
  1464.7 9.1 fusion.57
  1476.8 11.7 reduce-scatter.9.cloned.1.call-done
  1490.2 53.4 %reduce-scatter.11.cloned.1.call-done = f32[128,1024]{1,0:T(8,128)} async-done(((f32[1024,1024]{1,0:T(8,128)}), f32[128,1024]{1,0:T(8,128)}) %reduce-scatter.11.cloned.1.call-update) | async-done | bytes 524304 | tf_op jit(solution)/shard_map/reduce_scatter | solution.py:242
  1543.6 90.9 %reduce-scatter.23.cloned.1.call-done = f32[1408,256]{1,0:T(8,128)} async-done(((f32[1408,2048]{1,0:T(8,128)}), f32[1408,256]{1,0:T(8,128)}) %reduce-scatter.23.cloned.1.call-update) | async-done | bytes 1441808 | tf_op jit(solution)/shard_map/reduce_scatter | solution.py:246
  1634.5 91.2 %reduce-scatter.21.cloned.1.call-done = f32[256,1408]{1,0:T(8,128)} async-done(((f32[2048,1408]{1,0:T(8,128)}), f32[256,1408]{1,0:T(8,128)}) %reduce-scatter.21.cloned.1.call-update) | async-done | bytes 1441808 | tf_op jit(solution)/shard_map/reduce_scatter | solution.py:245
  1725.8 91.1 %reduce-scatter.19.cloned.1.call-done = f32[256,1408]{1,0:T(8,128)} async-done(((f32[2048,1408]{1,0:T(8,128)}), f32[256,1408]{1,0:T(8,128)}) %reduce-scatter.19.cloned.1.call-update) | async-done | bytes 1441808 | tf_op jit(solution)/shard_map/reduce_scatter | solution.py:244
  1816.8 75.4 %reduce-scatter.17.cloned.1.call-done = f32[1024,256]{1,0:T(8,128)} async-done(((f32[1024,2048]{1,0:T(8,128)}), f32[1024,256]{1,0:T(8,128)}) %reduce-scatter.17.cloned.1.call-update) | async-done | bytes 1048592 | tf_op jit(solution)/shard_map/reduce_scatter | solution.py:243
  (234 shorter events, 113.6 us)
Async XLA Ops:
  7.2 26.8 %copy-start = (bf16[1024,1024]{1,0:T(8,128)(2,1)S(1)}, bf16[1024,1024]{1,0:T(8,128)(2,1)}, u32[]{:S(2)}) copy-start(bf16[1024,1024]{1,0:T(8,128)(2,1)} %param.23) | copy-start | bytes 6291460
  7.2 5.2 copy-start.43
  7.2 371.4 %all-reduce.9.cloned.1.call-start = ((), (), s32[]{:S(2)}) async-start(), calls=%async_computation.8 | async-start | bytes 16777216 | tf_op jit(solution)/shard_map/psum | solution.py:152
  7.3 9.7 copy-start.45
  7.3 5.1 copy-start.2
  9.3 24.7 %copy-start.38 = (f32[1024]{0:T(1024)}, f32[1024]{0:T(1024)S(1)}, u32[]{:S(2)}) copy-start(f32[1024]{0:T(1024)S(1)} %convert_element_type.78) | copy-start | bytes 12292
  13.7 3.3 copy-start.8
  34.0 2.6 copy-start.10
  57.4 2.7 copy-start.21
  69.6 2.7 copy-start.21
  74.6 3.5 copy-start.48
  84.9 650.6 %all-reduce.11.cloned.1.call-start = ((), (), s32[]{:S(2)}) async-start(), calls=%async_computation.9 | async-start | bytes 16777216 | tf_op jit(solution)/shard_map/psum | solution.py:170
  384.3 3.3 copy-start.1
  387.6 11.8 copy-start.16
  399.4 10.4 copy-start.14
  424.6 9.8 copy-start.51
  424.6 9.8 copy-start.52
  445.5 874.3 %all-reduce.13.cloned.1.call-start = ((), (), s32[]{:S(2)}) async-start(), calls=%async_computation.18 | async-start | bytes 29360128 | tf_op jit(solution)/shard_map/psum | solution.py:162
  735.5 8.2 copy-start.5
  735.5 9.4 copy-start.15
  749.5 3.3 copy-start.6
  769.3 2.6 copy-start.29
  774.8 3.4 copy-start.30
  789.7 2.6 copy-start.29
  795.3 3.4 copy-start.30
  819.4 6.0 copy-start.19
  826.8 493.0 %copy-start.46 = (f32[128]{0:T(128)S(1)}, f32[128]{0:T(128)}, u32[]{:S(2)}) copy-start(f32[128]{0:T(128)} %copy-done.45) | copy-start | bytes 1540
  826.9 647.0 %reduce-scatter.13.cloned.1.call-start = ((), (), s32[]{:S(2)}) async-start(), calls=%async_computation.12 | async-start | bytes 2359296 | tf_op jit(solution)/shard_map/reduce_scatter | solution.py:252
  1329.1 5.4 copy-start.39
  1329.1 5.4 copy-start.41
  1329.1 146.3 %reduce-scatter.15.cloned.1.call-start = ((), (), s32[]{:S(2)}) async-start(), calls=%async_computation.13 | async-start | bytes 2359296 | tf_op jit(solution)/shard_map/reduce_scatter | solution.py:253
  1334.4 154.1 %reduce-scatter.9.cloned.1.call-start = ((), (), s32[]{:S(2)}) async-start(), calls=%async_computation.10 | async-start | bytes 9437184 | tf_op jit(solution)/shard_map/reduce_scatter | solution.py:251
  1334.5 5.3 copy-start.11
  1334.5 6.7 copy-start.12
  1341.2 3.0 copy-start.9
  1351.2 192.4 %reduce-scatter.11.cloned.1.call-start = ((), (), s32[]{:S(2)}) async-start(), calls=%async_computation.11 | async-start | bytes 4718592 | tf_op jit(solution)/shard_map/reduce_scatter | solution.py:242
  1358.6 276.0 %reduce-scatter.23.cloned.1.call-start = ((), (), s32[]{:S(2)}) async-start(), calls=%async_computation.17 | async-start | bytes 12976128 | tf_op jit(solution)/shard_map/reduce_scatter | solution.py:246
  1370.2 355.5 %reduce-scatter.21.cloned.1.call-start = ((), (), s32[]{:S(2)}) async-start(), calls=%async_computation.16 | async-start | bytes 12976128 | tf_op jit(solution)/shard_map/reduce_scatter | solution.py:245
  1382.2 434.6 %reduce-scatter.19.cloned.1.call-start = ((), (), s32[]{:S(2)}) async-start(), calls=%async_computation.15 | async-start | bytes 12976128 | tf_op jit(solution)/shard_map/reduce_scatter | solution.py:244
  1394.4 497.8 %reduce-scatter.17.cloned.1.call-start = ((), (), s32[]{:S(2)}) async-start(), calls=%async_computation.14 | async-start | bytes 9437184 | tf_op jit(solution)/shard_map/reduce_scatter | solution.py:243
  1409.2 2.9 copy-start.49
  1412.1 6.9 copy-start.3
  1412.1 6.9 copy-start.13
  1412.1 6.9 copy-start.28
  1412.1 6.9 copy-start.35
  1412.1 6.9 copy-start.37
  1419.1 8.8 copy-start.42
  1455.0 9.8 copy-start.4
  (25 other events, 42.5 us)
Sparse Core Ops, SparseCore 0:
  85.0 293.5 all-reduce.8
  445.6 289.8 all-reduce.10
  827.0 492.7 all-reduce.12
  1329.2 39.9 reduce-scatter.12
  1372.3 41.0 reduce-scatter.14
  1416.8 71.6 reduce-scatter.8
  1492.4 51.1 reduce-scatter.10
  1547.7 86.8 reduce-scatter.22
  1638.6 87.0 reduce-scatter.20
  1729.7 87.0 reduce-scatter.18
  1820.9 71.2 reduce-scatter.16
where the time goes:
time: 1910 us; the launch traced here: 1900 us
  waiting for transfers between devices  1480 us (77%)
  matrix products  228 us (12%)
  other arithmetic  79.1 us (4%)
  local copies, waits for them, and re-layouts  67.9 us (4%)
  blocking collectives  25.4 us (1%)
    psum x1, waiting for transfers between devices, shards(): lax.psum(jnp.dot(hidden_act, w_down, preferred_element_type=jnp.float32),...  493 us
    psum x1, waiting for transfers between devices, shards(): lax.psum(jnp.dot(mixed_heads, out_proj, preferred_element_type=jnp.float3...  293 us
    psum x1, waiting for transfers between devices, shards(): lax.psum(right_dot(d_gate, w_gate) + right_dot(d_up, w_up), 'tensor')  278 us
    reduce_scatter x1, waiting for transfers between devices, shards(): lax.psum_scatter(grad_up, 'dp', scatter_dimension=0, tiled=True)  91.2 us
    reduce_scatter x1, waiting for transfers between devices, shards(): lax.psum_scatter(grad_gate, 'dp', scatter_dimension=0, tiled=True)  91.1 us
    reduce_scatter x1, waiting for transfers between devices, shards(): lax.psum_scatter(grad_down, 'dp', scatter_dimension=1, tiled=True)  90.9 us
    reduce_scatter x1, waiting for transfers between devices, shards(): lax.psum_scatter(grad_out, 'dp', scatter_dimension=1, tiled=True)  75.4 us
    dot_general x8, matrix products, left_dot(): lax.dot_general(left, right, (((0,), (0,)), ((), ())), preferred_element_...  71.9 us
  transfers between devices with their start and end apart: 11, of which 9 were waited for; matrix products, arithmetic and copies ran while one was open for 7% of the time, Pallas kernels for 0%

commit v1 on v0

--- a/solution.py
+++ b/solution.py
@@ -1,7 +1,14 @@
+import functools
+
 import jax
 import jax.numpy as jnp
 from jax import lax
+from jax.experimental import pallas as pl
+from jax.experimental.pallas import tpu as pltpu
 from jax.sharding import PartitionSpec as P
+
+
+MESH = pl.DeviceIdType.MESH
 
 PIECE = 256
 
@@ -57,6 +64,113 @@
         ],
         axis=-1,
     )
+
+
+def line_kernel(axis, n, chunks, K, x_ref, o_ref, red, s_red, r_red, s_fin, r_fin):
+    me = lax.axis_index(axis)
+    rows = x_ref.shape[0] // (2 * chunks)
+    barrier = pltpu.get_barrier_semaphore()
+
+    @pl.when(me > 0)
+    def _():
+        pl.semaphore_signal(barrier, inc=1, device_id={axis: me - 1}, device_id_type=MESH)
+
+    @pl.when(me < n - 1)
+    def _():
+        pl.semaphore_signal(barrier, inc=1, device_id={axis: me + 1}, device_id_type=MESH)
+
+    @pl.when((me == 0) | (me == n - 1))
+    def _():
+        pl.semaphore_wait(barrier, 1)
+
+    @pl.when((me > 0) & (me < n - 1))
+    def _():
+        pl.semaphore_wait(barrier, 2)
+
+    def at(half, c):
+        return pl.ds(pl.multiple_of((half * chunks + c) * rows, rows), rows)
+
+    def down(half):
+        return me - 1 if half == 0 else me + 1
+
+    def up(half):
+        return me + 1 if half == 0 else me - 1
+
+    def sum_copy(src, half, c):
+        return pltpu.make_async_remote_copy(
+            src_ref=src.at[at(half, c)], dst_ref=red.at[at(half, c)],
+            send_sem=s_red.at[half, c], recv_sem=r_red.at[half, c],
+            device_id={axis: down(half)}, device_id_type=MESH)
+
+    def fin_copy(half, c):
+        return pltpu.make_async_remote_copy(
+            src_ref=o_ref.at[at(half, c)], dst_ref=o_ref.at[at(half, c)],
+            send_sem=s_fin.at[half, c], recv_sem=r_fin.at[half, c],
+            device_id={axis: up(half)}, device_id_type=MESH)
+
+    def step(s, carry):
+        for half in (0, 1):
+            hop = (n - 1 - me) if half == 0 else me
+            c = s - K * hop
+            ok = (c >= 0) & (c < chunks)
+
+            @pl.when(ok & (hop == 0))
+            def _():
+                sum_copy(x_ref, half, c).start()
+
+            @pl.when(ok & (hop > 0) & (hop < n - 1))
+            def _():
+                sum_copy(x_ref, half, c).wait_recv()
+                red[at(half, c)] = red[at(half, c)] + x_ref[at(half, c)]
+                sum_copy(red, half, c).start()
+
+            @pl.when(ok & (hop == n - 1))
+            def _():
+                sum_copy(x_ref, half, c).wait_recv()
+                o_ref[at(half, c)] = red[at(half, c)] + x_ref[at(half, c)]
+                fin_copy(half, c).start()
+        for half in (0, 1):
+            back = me if half == 0 else (n - 1 - me)
+            c = s - K * (n - 1) - K * back
+            ok = (c >= 0) & (c < chunks)
+
+            @pl.when(ok & (back > 0))
+            def _():
+                fin_copy(half, c).wait_recv()
+
+            @pl.when(ok & (back > 0) & (back < n - 1))
+            def _():
+                fin_copy(half, c).start()
+        return carry
+
+    lax.fori_loop(0, chunks + 2 * K * (n - 1), step, 0)
+
+    def drain(c, carry):
+        for half in (0, 1):
+            hop = (n - 1 - me) if half == 0 else me
+
+            @pl.when(hop < n - 1)
+            def _():
+                sum_copy(x_ref, half, c).wait_send()
+
+            @pl.when(hop > 0)
+            def _():
+                fin_copy(half, c).wait_send()
+        return carry
+
+    lax.fori_loop(0, chunks, drain, 0)
+
+
+def line_sum(x, axis, n, chunks, cid, K=1):
+    return pl.pallas_call(
+        functools.partial(line_kernel, axis, n, chunks, K),
+        out_shape=jax.ShapeDtypeStruct(x.shape, x.dtype),
+        in_specs=[pl.BlockSpec(memory_space=pltpu.VMEM)],
+        out_specs=pl.BlockSpec(memory_space=pltpu.VMEM),
+        scratch_shapes=[pltpu.VMEM(x.shape, x.dtype)] + [pltpu.SemaphoreType.DMA((2, chunks))] * 4,
+        compiler_params=pltpu.CompilerParams(collective_id=cid, has_side_effects=True, vmem_limit_bytes=48 << 20),
+        name="line_sum",
+    )(x)
 
 
 def shards(
@@ -76,6 +190,22 @@
     d_output,
 ):
     row_count, model_width = block_input.shape
+    dp_count = lax.axis_size("dp")
+    tp_count = lax.axis_size("tensor")
+    tp_index = lax.axis_index("tensor")
+
+    def sum_parts(part):
+        chunks = row_count // 32
+        while row_count % (16 * chunks):
+            chunks -= 1
+        return line_sum(part, "tensor", tp_count, chunks, 1 if part.shape[1] == model_width else 2, 2)
+
+    def own_part(values, axis):
+        split = values.shape[axis] // (dp_count * tp_count)
+        shape = values.shape[:axis] + (dp_count, tp_count, split) + values.shape[axis + 1 :]
+        picked = lax.dynamic_index_in_dim(values.reshape(shape), tp_index, axis + 1, keepdims=False)
+        return picked
+
     seq_count = image_starts.shape[0]
     seq_len = row_count // seq_count
     head_dim = k_proj.shape[1]
@@ -149,9 +279,7 @@
 
     mixed_seq, log_norm = lax.map(forward_seq, (query_seq, key_seq, val_seq, piece_ids))
     mixed_heads = mixed_seq.reshape(row_count, head_count * head_dim)
-    attn_out = lax.psum(
-        jnp.dot(mixed_heads, out_proj, preferred_element_type=jnp.float32), "tensor"
-    )
+    attn_out = sum_parts(jnp.dot(mixed_heads, out_proj, preferred_element_type=jnp.float32))
     hidden_in = input_f32 + attn_out
     normed_two, scale_two = normalize(hidden_in)
     normed_mid = (normed_two * gain_mlp).astype(jnp.bfloat16)
@@ -159,15 +287,21 @@
     up_pre = jnp.dot(normed_mid, w_up, preferred_element_type=jnp.float32)
     gate_sig = jax.nn.sigmoid(gate_pre)
     hidden_act = (gate_pre * gate_sig * up_pre).astype(jnp.bfloat16)
-    mlp_out = lax.psum(jnp.dot(hidden_act, w_down, preferred_element_type=jnp.float32), "tensor")
-    block_output = (hidden_in + mlp_out).astype(jnp.bfloat16)
+    mlp_part = jnp.dot(hidden_act, w_down, preferred_element_type=jnp.float32)
     grad_down = left_dot(hidden_act, d_output)
     d_act = right_dot(d_output, w_down)
     d_gate = (d_act * up_pre * gate_sig * (1.0 + gate_pre * (1.0 - gate_sig))).astype(jnp.bfloat16)
     d_up = (d_act * gate_pre * gate_sig).astype(jnp.bfloat16)
     grad_gate = left_dot(normed_mid, d_gate)
     grad_up = left_dot(normed_mid, d_up)
-    d_mid = lax.psum(right_dot(d_gate, w_gate) + right_dot(d_up, w_up), "tensor")
+    d_mid_part = right_dot(d_gate, w_gate) + right_dot(d_up, w_up)
+    d_mid_part, grad_down, grad_gate, grad_up = lax.optimization_barrier(
+        (d_mid_part, grad_down, grad_gate, grad_up)
+    )
+    grad_gate = lax.psum_scatter(grad_gate, "dp", scatter_dimension=0, tiled=True)
+    grad_up = lax.psum_scatter(grad_up, "dp", scatter_dimension=0, tiled=True)
+    grad_down = lax.psum_scatter(grad_down, "dp", scatter_dimension=1, tiled=True)
+    d_mid = sum_parts(d_mid_part)
     grad_gain_mlp = jnp.sum(d_mid * normed_two, axis=0)
     d_hidden = cotan_f32 + norm_back(d_mid * gain_mlp, normed_two, scale_two)
     d_hidden_low = d_hidden.astype(jnp.bfloat16)
@@ -226,7 +360,12 @@
     )
     grad_query_up = left_dot(q_normed, d_q_raw)
     d_bq_part = right_dot(d_q_raw, q_up)
-    d_q_normed, key_val_full = lax.psum((d_bq_part, key_val_part), "tensor")
+    mlp_part, d_bq_part = lax.optimization_barrier((mlp_part, d_bq_part))
+    mlp_out = sum_parts(mlp_part)
+    block_output = (hidden_in + mlp_out).astype(jnp.bfloat16)
+    query_key_val = sum_parts(jnp.concatenate([d_bq_part, key_val_part], axis=1))
+    d_q_normed = query_key_val[:, : q_gain.shape[0]]
+    key_val_full = query_key_val[:, q_gain.shape[0] :]
     d_key_low = unrotate(key_val_full[:, :head_dim], cos_all, sin_all).astype(jnp.bfloat16)
     d_val_low = key_val_full[:, head_dim:].astype(jnp.bfloat16)
     grad_gain_query = jnp.sum(d_q_normed * q_unit, axis=0)
@@ -238,31 +377,27 @@
     grad_input = (d_hidden + norm_back(d_normed_in * gain_attn, normed_one, scale_one)).astype(
         jnp.bfloat16
     )
-    grad_query_up, grad_out, grad_gate, grad_up, grad_down = (
-        lax.psum_scatter(grad_query_up, "dp", scatter_dimension=0, tiled=True),
-        lax.psum_scatter(grad_out, "dp", scatter_dimension=1, tiled=True),
-        lax.psum_scatter(grad_gate, "dp", scatter_dimension=0, tiled=True),
-        lax.psum_scatter(grad_up, "dp", scatter_dimension=0, tiled=True),
-        lax.psum_scatter(grad_down, "dp", scatter_dimension=1, tiled=True),
-    )
-    tp_count = lax.axis_size("tensor")
-    tp_index = lax.axis_index("tensor")
-    summed = (
-        lax.psum_scatter(left_dot(normed_in, d_latent), "dp", scatter_dimension=0, tiled=True),
-        lax.psum_scatter(left_dot(normed_in, d_key_low), "dp", scatter_dimension=0, tiled=True),
-        lax.psum_scatter(left_dot(normed_in, d_val_low), "dp", scatter_dimension=0, tiled=True),
-        lax.psum_scatter(grad_gain_attn, "dp", scatter_dimension=0, tiled=True),
-        lax.psum_scatter(grad_gain_query, "dp", scatter_dimension=0, tiled=True),
-        lax.psum_scatter(grad_gain_mlp, "dp", scatter_dimension=0, tiled=True),
-    )
-
-    def pick_rows(summed_rows):
-        own_count = summed_rows.shape[0] // tp_count
-        return lax.dynamic_slice_in_dim(summed_rows, tp_index * own_count, own_count, 0)
-
-    grad_qd, grad_key, grad_val, grad_g1, grad_gq, grad_g2 = tuple(
-        (pick_rows(item) for item in summed)
-    )
+    grad_query_up = lax.psum_scatter(grad_query_up, "dp", scatter_dimension=0, tiled=True)
+    grad_out = lax.psum_scatter(grad_out, "dp", scatter_dimension=1, tiled=True)
+    own_in = own_part(normed_in, 1).reshape(row_count, -1)
+    own_grads = left_dot(own_in, jnp.concatenate([d_latent, d_key_low, d_val_low], axis=1))
+    own_rows = own_grads.shape[0]
+    gain_one = own_part(grad_gain_attn, 0).reshape(own_rows, 1)
+    gain_two = own_part(grad_gain_mlp, 0).reshape(own_rows, 1)
+    gain_mid = own_part(grad_gain_query, 0)
+    own_mid = gain_mid.shape[1]
+    gain_mid = jnp.pad(gain_mid, ((0, 0), (0, own_rows // dp_count - own_mid))).reshape(own_rows, 1)
+    gain_cols = jnp.concatenate([gain_one, gain_two, gain_mid], axis=1)
+    own_grads = jnp.concatenate([own_grads, jnp.pad(gain_cols, ((0, 0), (0, 125)))], axis=1)
+    own_sum = lax.psum_scatter(own_grads, "dp", scatter_dimension=0, tiled=True)
+    rank = q_down.shape[1]
+    grad_qd = own_sum[:, :rank]
+    grad_key = own_sum[:, rank : rank + head_dim]
+    grad_val = own_sum[:, rank + head_dim : rank + 2 * head_dim]
+    gain_at = rank + 2 * head_dim
+    grad_g1 = own_sum[:, gain_at]
+    grad_g2 = own_sum[:, gain_at + 1]
+    grad_gq = own_sum[:own_mid, gain_at + 2]
     return (
         block_output,
         grad_input,
@@ -297,6 +432,7 @@
         P("tensor", None),
         P("dp", None),
     )
+
     return jax.shard_map(
         shards,
         mesh=mesh,

time: 1910 us -> 1370 us (0.72)
  waiting for transfers between devices: 1480 us -> 205 us
  Pallas kernels: 0 us -> 768 us
  blocking collectives: 25.4 us -> 0 us
    psum x3 -> x0, waiting for transfers between devices: 1060 us -> none  [the longest x1 493 us: shards(): lax.psum(jnp.dot(hidden_act, w_down, preferred_element_type=jnp.float32),...]
    pallas_call x0 -> x4, Pallas kernels: none -> 768 us  [line_sum(): pl.pallas_call(functools.partial(line_kernel, axis, n, chunks, K), out_sh...]
    reduce_scatter x5 -> x3, waiting for transfers between devices: 178 us -> 91.1 us  [the longest x1 91.1 us: shards(): grad_up = lax.psum_scatter(grad_up, 'dp', scatter_dimension=0, tiled=True)]
    reduce_scatter x1, waiting for transfers between devices: 91.1 us -> 21.5 us  [shards(): lax.psum_scatter(grad_gate, 'dp', scatter_dimension=0, tiled=True)]
    reduce_scatter x1, waiting for transfers between devices: 53.4 us -> 0.01 us  [shards(): lax.psum_scatter(grad_query_up, 'dp', scatter_dimension=0, tiled=True)]
    unnamed x1 -> x0, blocking collectives: 25.4 us -> none
    dot_general x8 -> x6, matrix products: 71.9 us -> 54.6 us  [left_dot(): lax.dot_general(left, right, (((0,), (0,)), ((), ())), preferred_element_...]
  transfers between devices with their start and end apart: 11 -> 6, of which waited for: 9 -> 3; matrix products, arithmetic and copies ran while one was open for 7% -> 3% of each run, Pallas kernels for 0% -> 15%
where the time goes in v1:
time: 1370 us
  Pallas kernels  768 us (56%)
  matrix products  221 us (16%)
  waiting for transfers between devices  205 us (15%)
  other arithmetic  88.2 us (6%)
  local copies, waits for them, and re-layouts  67.2 us (5%)
  between operations  15 us (1%)
    pallas_call x4, Pallas kernels, line_sum(): pl.pallas_call(functools.partial(line_kernel, axis, n, chunks, K), out_sh...  768 us
    reduce_scatter x1, waiting for transfers between devices, shards(): grad_up = lax.psum_scatter(grad_up, 'dp', scatter_dimension=0, tiled=True)  91.1 us
    reduce_scatter x1, waiting for transfers between devices, shards(): lax.psum_scatter(grad_down, 'dp', scatter_dimension=1, tiled=True)  90.8 us
    dot_general x8, matrix products, right_dot(): lax.dot_general(left, right, (((1,), (1,)), ((), ())), preferred_element_...  74.5 us
    dot_general x6, matrix products, left_dot(): lax.dot_general(left, right, (((0,), (0,)), ((), ())), preferred_element_...  54.6 us
  transfers between devices with their start and end apart: 6, of which 3 were waited for; matrix products, arithmetic and copies ran while one was open for 3% of the time, Pallas kernels for 15%

profile of v1, /device:TPU:0, one launch (start us, length us, event | category | flops | bytes accessed | tf_op | source)
XLA Modules:
  0.0 1368.7 jit_solution(11573206589873726733)
XLA Ops:
  9.3 3.1 fusion.59
  13.0 3.0 fusion.52
  16.1 6.9 copy.96
  23.0 3.9 convolution_convert_fusion
  29.3 6.1 multiply_reduce_fusion.5
  35.4 5.3 copy.85
  40.7 4.8 fusion.85
  53.6 3.6 subtract_convert_fusion.3
  57.2 3.1 subtract_convert_fusion.1
  62.3 24.7 %while.48 = (s32[]{:T(128)}, bf16[2,512,4,256]{3,2,1,0:T(4,128)(2,1)}, f32[2,4,512]{2,1,0:T(4,128)S(1)}, s32[2]{0:T(128)S(1)}, s32[1024]{0:T(1024)S(1)}, /*index...) while((s32[]{:T(128)}, ...), condition=%wide.region_6.7_spmd.clone, body=%wide.region_3.6_spmd.clone.sunk | while | flops 2175269888 | bytes 49364228 | solution.py:278
  90.9 6.8 fusion.90.x_ref
  97.7 208.6 %line_sum.4 = f32[1024,2048]{1,0:T(8,128)} custom-call(f32[1024,2048]{1,0:T(8,128)} %fusion.90.x_ref), custom_call_target="tpu_custom_call" | custom-call | tf_op jit(solution)/shard_map/line_sum/pallas_call | solution.py:165
  306.3 5.7 multiply_reduce_fusion.2
  315.4 11.8 fusion.92
  327.2 10.4 fusion.91
  337.6 14.7 %multiply_convert_fusion.1 = (bf16[1024,1408]{1,0:T(8,128)(2,1)}, bf16[1024,1408]{1,0:T(8,128)(2,1)}, bf16[1024,1408]{1,0:T(8,128)(2,1)S(1)}) fusion(f32[1024,1408]{1,0:T(8,128)} %fusion.91, f32[1024,1408]{1,0:T(8,128)} %fusion.92, bf16[1024,2048]{1,0:T(8,128)(2,1)S(1)} %copy-done.15, bf16[1408,2048]{1,0:T(8,128)(2,1)} %param.30), kind=kOutput, calls=%fused_computation.84 | convolution fusion | flops 5928648704 | bytes 30146560 | tf_op jit(solution)/shard_map/dot_general | solution.py:38
  352.3 11.2 fusion.93.x_ref
  363.5 9.0 fusion.95
  372.5 11.8 fusion.94
  384.3 9.6 fusion.96
  393.9 12.1 fusion.97
  405.9 12.9 convolution_add_fusion.x_ref
  418.8 203.8 %line_sum.5 = f32[1024,2048]{1,0:T(8,128)} custom-call(f32[1024,2048]{1,0:T(8,128)} %convolution_add_fusion.x_ref), custom_call_target="tpu_custom_call" | custom-call | tf_op jit(solution)/shard_map/line_sum/pallas_call | solution.py:165
  622.6 8.4 multiply_reduce_fusion
  633.3 4.4 multiply_add_fusion
  637.7 10.5 fusion.72
  648.2 4.6 squeeze.60
  652.9 41.4 %while.49 = (s32[]{:T(128)}, f32[1024,256]{1,0:T(8,128)}, f32[1024,256]{1,0:T(8,128)}, f32[2,512,4,256]{3,1,0,2:T(8,128)}, s32[2]{0:T(128)S(1)}, /*index=5*/s32[...) while((s32[]{:T(128)}, f32[1024,256]{1,0:T(8,128)}, ...), condition=%wide.region_11.12_spmd.clone, body=%wide.region_9.11_spmd.clone.sunk | while | flops 5404097536 | bytes 137960912 | solution.py:344
  662.5 3.4 fusion.169
  683.0 3.4 fusion.169
  698.8 4.0 copy.95
  702.8 4.1 fusion.98
  707.0 3.4 pad_maximum_fusion.x_ref
  710.4 155.4 %line_sum.7 = f32[1024,1536]{1,0:T(8,128)} custom-call(f32[1024,1536]{1,0:T(8,128)} %pad_maximum_fusion.x_ref), custom_call_target="tpu_custom_call" | custom-call | tf_op jit(solution)/shard_map/line_sum/pallas_call | solution.py:165
  865.9 3.3 multiply_reduce_fusion.3
  869.2 4.1 add_convert_fusion.3
  876.9 4.9 multiply_convert_fusion.4
  882.0 10.8 fusion.99
  895.3 8.3 fusion.58
  904.7 3.7 fusion.60
  910.6 7.6 fusion.84
  918.3 12.7 fusion.68
  932.8 200.4 %line_sum.6 = f32[1024,2048]{1,0:T(8,128)} custom-call(f32[1024,2048]{1,0:T(8,128)} %fusion.93.x_ref), custom_call_target="tpu_custom_call" | custom-call | tf_op jit(solution)/shard_map/line_sum/pallas_call | solution.py:165
  1133.2 9.8 add_convert_fusion
  1142.9 9.3 fusion.57
  1158.3 21.5 %reduce-scatter.13.cloned.1.call-done = f32[256,1408]{1,0:T(8,128)} async-done(((f32[2048,1408]{1,0:T(8,128)}), f32[256,1408]{1,0:T(8,128)}) %reduce-scatter.13.cloned.1.call-update) | async-done | bytes 1441808 | tf_op jit(solution)/shard_map/reduce_scatter | solution.py:301
  1179.8 91.1 %reduce-scatter.15.cloned.1.call-done = f32[256,1408]{1,0:T(8,128)} async-done(((f32[2048,1408]{1,0:T(8,128)}), f32[256,1408]{1,0:T(8,128)}) %reduce-scatter.15.cloned.1.call-update) | async-done | bytes 1441808 | tf_op jit(solution)/shard_map/reduce_scatter | solution.py:302
  1270.9 90.8 %reduce-scatter.17.cloned.1.call-done = f32[1408,256]{1,0:T(8,128)} async-done(((f32[1408,2048]{1,0:T(8,128)}), f32[1408,256]{1,0:T(8,128)}) %reduce-scatter.17.cloned.1.call-update) | async-done | bytes 1441808 | tf_op jit(solution)/shard_map/reduce_scatter | solution.py:303
  (240 shorter events, 102.3 us)
Async XLA Ops:
  7.2 33.5 %copy-start = (bf16[1024,1024]{1,0:T(8,128)(2,1)S(1)}, bf16[1024,1024]{1,0:T(8,128)(2,1)}, u32[]{:S(2)}) copy-start(bf16[1024,1024]{1,0:T(8,128)(2,1)} %param.23) | copy-start | bytes 6291460
  7.2 5.2 copy-start.48
  7.2 5.2 copy-start.49
  7.2 1145.0 %reduce-scatter.7.cloned.1.call-start = ((), (), s32[]{:S(2)}) async-start(), calls=%async_computation.6 | async-start | bytes 3833856 | tf_op jit(solution)/shard_map/reduce_scatter | solution.py:392
  7.3 46.3 %copy-start.50 = (f32[128]{0:T(128)}, f32[128]{0:T(128)S(1)}, u32[]{:S(2)}) copy-start(f32[128]{0:T(128)S(1)} %multiply_power_fusion) | copy-start | bytes 1540
  7.3 5.7 copy-start.2
  9.3 31.4 %copy-start.43 = (f32[1024]{0:T(1024)}, f32[1024]{0:T(1024)S(1)}, u32[]{:S(2)}) copy-start(f32[1024]{0:T(1024)S(1)} %convert_element_type.82) | copy-start | bytes 12292
  23.0 3.9 copy-start.10
  23.0 4.1 copy-start.26
  35.4 5.4 copy-start.45
  57.2 3.5 copy-start.13
  57.2 3.4 copy-start.14
  87.1 10.6 copy-start.8
  87.1 10.6 copy-start.11
  87.1 10.6 copy-start.24
  87.1 10.6 copy-start.39
  87.1 3.8 copy-start.53
  312.1 3.3 copy-start.1
  315.4 11.8 copy-start.17
  327.2 10.4 copy-start.15
  372.5 11.8 copy-start.18
  372.5 11.8 copy-start.55
  418.8 212.2 %slice-start = ((s8[8388608]{0:T(1024)(128)(4,1)}), s8[4194304]{0:T(1024)(128)(4,1)S(1)}, s32[]{:S(2)}) async-start(s8[8388608]{0:T(1024)(128)(4,1)} %bitcast.206), calls=%async_computation.12 | async-start | bytes 8388608
  622.6 8.4 slice-start.1
  622.6 9.5 copy-start.5
  622.6 10.7 copy-start.16
  648.2 4.6 copy-start.9
  648.2 4.6 copy-start.12
  648.2 4.6 copy-start.25
  648.2 4.7 copy-start.40
  662.5 3.4 copy-start.30
  682.9 3.4 copy-start.30
  702.8 4.1 copy-start.31
  702.8 4.1 copy-start.34
  710.4 155.4 %copy-start.6 = (f32[1024,1024]{1,0:T(8,128)S(1)}, f32[1024,1024]{1,0:T(8,128)}, u32[]{:S(2)}) copy-start(f32[1024,1024]{1,0:T(8,128)} %copy.85) | copy-start | bytes 12582916
  710.4 155.4 %copy-start.44 = (f32[1024]{0:T(1024)S(1)}, f32[1024]{0:T(1024)}, u32[]{:S(2)}) copy-start(f32[1024]{0:T(1024)} %copy-done.43) | copy-start | bytes 12292
  710.4 155.4 %copy-start.46 = (f32[1024]{0:T(1024)S(1)}, f32[1024]{0:T(1024)}, u32[]{:S(2)}) copy-start(f32[1024]{0:T(1024)} %copy-done.45) | copy-start | bytes 12292
  865.8 3.3 copy-start.51
  865.8 9.5 copy-start.47
  882.0 10.9 copy-start.27
  882.0 10.9 copy-start.35
  904.7 3.7 copy-start.36
  910.4 248.0 %reduce-scatter.9.cloned.1.call-start = ((), (), s32[]{:S(2)}) async-start(), calls=%async_computation.7 | async-start | bytes 4718592 | tf_op jit(solution)/shard_map/reduce_scatter | solution.py:380
  918.3 240.1 %reduce-scatter.11.cloned.1.call-start = ((), (), s32[]{:S(2)}) async-start(), calls=%async_computation.8 | async-start | bytes 9437184 | tf_op jit(solution)/shard_map/reduce_scatter | solution.py:381
  931.0 248.8 %reduce-scatter.13.cloned.1.call-start = ((), (), s32[]{:S(2)}) async-start(), calls=%async_computation.9 | async-start | bytes 12976128 | tf_op jit(solution)/shard_map/reduce_scatter | solution.py:301
  931.6 339.3 %reduce-scatter.15.cloned.1.call-start = ((), (), s32[]{:S(2)}) async-start(), calls=%async_computation.10 | async-start | bytes 12976128 | tf_op jit(solution)/shard_map/reduce_scatter | solution.py:302
  932.2 429.5 %reduce-scatter.17.cloned.1.call-start = ((), (), s32[]{:S(2)}) async-start(), calls=%async_computation.11 | async-start | bytes 12976128 | tf_op jit(solution)/shard_map/reduce_scatter | solution.py:303
  1133.1 9.8 copy-start.4
  (25 other events, 50.1 us)
Sparse Core Ops, SparseCore 0:
  910.5 47.6 reduce-scatter.6
  962.1 51.1 reduce-scatter.8
  1017.4 71.3 reduce-scatter.10
  1092.6 87.1 reduce-scatter.12
  1183.7 87.0 reduce-scatter.14
  1274.8 86.8 reduce-scatter.16

commit v2 on v1

--- a/solution.py
+++ b/solution.py
@@ -66,9 +66,10 @@
     )
 
 
-def line_kernel(axis, n, chunks, K, x_ref, o_ref, red, s_red, r_red, s_fin, r_fin):
+def line_steps(axis, n, chunks, lag, x_ref, held, red, sems, finish, job, job_count):
     me = lax.axis_index(axis)
     rows = x_ref.shape[0] // (2 * chunks)
+    s_red, r_red, s_fin, r_fin = sems
     barrier = pltpu.get_barrier_semaphore()
 
     @pl.when(me > 0)
@@ -90,28 +91,32 @@
     def at(half, c):
         return pl.ds(pl.multiple_of((half * chunks + c) * rows, rows), rows)
 
-    def down(half):
-        return me - 1 if half == 0 else me + 1
-
-    def up(half):
-        return me + 1 if half == 0 else me - 1
-
     def sum_copy(src, half, c):
         return pltpu.make_async_remote_copy(
-            src_ref=src.at[at(half, c)], dst_ref=red.at[at(half, c)],
-            send_sem=s_red.at[half, c], recv_sem=r_red.at[half, c],
-            device_id={axis: down(half)}, device_id_type=MESH)
+            src_ref=src.at[at(half, c)],
+            dst_ref=red.at[at(half, c)],
+            send_sem=s_red.at[half, c],
+            recv_sem=r_red.at[half, c],
+            device_id={axis: me - 1 if half == 0 else me + 1},
+            device_id_type=MESH,
+        )
 
     def fin_copy(half, c):
         return pltpu.make_async_remote_copy(
-            src_ref=o_ref.at[at(half, c)], dst_ref=o_ref.at[at(half, c)],
-            send_sem=s_fin.at[half, c], recv_sem=r_fin.at[half, c],
-            device_id={axis: up(half)}, device_id_type=MESH)
+            src_ref=held.at[at(half, c)],
+            dst_ref=held.at[at(half, c)],
+            send_sem=s_fin.at[half, c],
+            recv_sem=r_fin.at[half, c],
+            device_id={axis: me + 1 if half == 0 else me - 1},
+            device_id_type=MESH,
+        )
+
+    steps = chunks + 2 * lag * (n - 1)
 
     def step(s, carry):
         for half in (0, 1):
             hop = (n - 1 - me) if half == 0 else me
-            c = s - K * hop
+            c = s - lag * hop
             ok = (c >= 0) & (c < chunks)
 
             @pl.when(ok & (hop == 0))
@@ -127,11 +132,13 @@
             @pl.when(ok & (hop == n - 1))
             def _():
                 sum_copy(x_ref, half, c).wait_recv()
-                o_ref[at(half, c)] = red[at(half, c)] + x_ref[at(half, c)]
+                held[at(half, c)] = red[at(half, c)] + x_ref[at(half, c)]
                 fin_copy(half, c).start()
+                finish(at(half, c))
+
         for half in (0, 1):
             back = me if half == 0 else (n - 1 - me)
-            c = s - K * (n - 1) - K * back
+            c = s - lag * (n - 1) - lag * back
             ok = (c >= 0) & (c < chunks)
 
             @pl.when(ok & (back > 0))
@@ -141,9 +148,16 @@
             @pl.when(ok & (back > 0) & (back < n - 1))
             def _():
                 fin_copy(half, c).start()
+
+            @pl.when(ok & (back > 0))
+            def _():
+                finish(at(half, c))
+
+        if job_count:
+            lax.fori_loop(s * job_count // steps, (s + 1) * job_count // steps, job, 0)
         return carry
 
-    lax.fori_loop(0, chunks + 2 * K * (n - 1), step, 0)
+    lax.fori_loop(0, steps, step, 0)
 
     def drain(c, carry):
         for half in (0, 1):
@@ -156,21 +170,155 @@
             @pl.when(hop > 0)
             def _():
                 fin_copy(half, c).wait_send()
+
         return carry
 
     lax.fori_loop(0, chunks, drain, 0)
 
 
-def line_sum(x, axis, n, chunks, cid, K=1):
+def line_kernel(axis, n, chunks, lag, x_ref, o_ref, red, *sems):
+    line_steps(axis, n, chunks, lag, x_ref, o_ref, red, sems, lambda at: None, None, 0)
+
+
+def line_low_kernel(axis, n, chunks, lag, x_ref, o_ref, red, held, *sems):
+    def finish(at):
+        o_ref[at] = held[at].astype(o_ref.dtype)
+
+    line_steps(axis, n, chunks, lag, x_ref, held, red, sems, finish, None, 0)
+
+
+def chunk_count(rows, most, tile):
+    chunks = most
+    while rows % (2 * chunks * tile):
+        chunks -= 1
+    return chunks
+
+
+def line_params(cid):
+    return pltpu.CompilerParams(
+        collective_id=cid, has_side_effects=True, vmem_limit_bytes=56 << 20
+    )
+
+
+def line_sum(x, axis, n, cid, low=False):
+    chunks = chunk_count(x.shape[0], 32, 16 if low else 8)
+    held = [pltpu.VMEM(x.shape, x.dtype)] if low else []
     return pl.pallas_call(
-        functools.partial(line_kernel, axis, n, chunks, K),
-        out_shape=jax.ShapeDtypeStruct(x.shape, x.dtype),
+        functools.partial(line_low_kernel if low else line_kernel, axis, n, chunks, 2),
+        out_shape=jax.ShapeDtypeStruct(x.shape, jnp.bfloat16 if low else x.dtype),
         in_specs=[pl.BlockSpec(memory_space=pltpu.VMEM)],
         out_specs=pl.BlockSpec(memory_space=pltpu.VMEM),
-        scratch_shapes=[pltpu.VMEM(x.shape, x.dtype)] + [pltpu.SemaphoreType.DMA((2, chunks))] * 4,
-        compiler_params=pltpu.CompilerParams(collective_id=cid, has_side_effects=True, vmem_limit_bytes=48 << 20),
+        scratch_shapes=[pltpu.VMEM(x.shape, x.dtype)]
+        + held
+        + [pltpu.SemaphoreType.DMA((2, chunks))] * 4,
+        compiler_params=line_params(cid),
         name="line_sum",
     )(x)
+
+
+def attend_back_kernel(
+    axis,
+    n,
+    chunks,
+    lag,
+    seq_len,
+    block,
+    x_ref,
+    q_ref,
+    dm_ref,
+    k_ref,
+    v_ref,
+    norm_ref,
+    own_ref,
+    all_ref,
+    cos_ref,
+    sin_ref,
+    o_ref,
+    dq_ref,
+    dkv_ref,
+    red,
+    held,
+    *sems,
+):
+    rows, head_dim = k_ref.shape
+    heads = q_ref.shape[1] // head_dim
+    half_dim = head_dim // 2
+    blocks = seq_len // block
+    scale = head_dim ** (-0.5)
+    dkv_ref[...] = jnp.zeros_like(dkv_ref)
+
+    def finish(at):
+        o_ref[at] = held[at].astype(o_ref.dtype)
+
+    def job(j, carry):
+        head = lax.rem(j, heads)
+        row_block = lax.div(j, heads)
+        seq = lax.div(row_block, blocks)
+        block_at = lax.rem(row_block, blocks)
+        own = pl.ds(pl.multiple_of(row_block * block, block), block)
+        cols = pl.ds(pl.multiple_of(head * head_dim, head_dim), head_dim)
+        low_cols = pl.ds(pl.multiple_of(head * head_dim, half_dim), half_dim)
+        high_cols = pl.ds(pl.multiple_of(head * head_dim + half_dim, half_dim), half_dim)
+
+        def run(reach):
+            keys = pl.ds(pl.multiple_of(seq * seq_len, seq_len), reach)
+            q = q_ref[own, cols]
+            dm = dm_ref[own, cols]
+            k = k_ref[keys, :]
+            v = v_ref[keys, :]
+            scores = right_dot(q, k) * scale
+            q_pos = block_at * block + lax.broadcasted_iota(jnp.int32, scores.shape, 0)
+            k_pos = lax.broadcasted_iota(jnp.int32, scores.shape, 1)
+            same = own_ref[own, :] == all_ref[:, keys]
+            probs = jnp.where(
+                (k_pos <= q_pos) | same, jnp.exp(scores - norm_ref[head, own, :]), 0.0
+            )
+            d_probs = right_dot(dm, v)
+            row_sum = jnp.sum(probs * d_probs, axis=1, keepdims=True)
+            d_scores = (probs * (d_probs - row_sum)).astype(jnp.bfloat16)
+            dkv_ref[keys, 0:head_dim] += left_dot(d_scores, q) * scale
+            dkv_ref[keys, head_dim : 2 * head_dim] += left_dot(probs.astype(jnp.bfloat16), dm)
+            dq = jnp.dot(d_scores, k, preferred_element_type=jnp.float32) * scale
+            first = dq[:, :half_dim]
+            second = dq[:, half_dim:]
+            cos_tab = cos_ref[own, :]
+            sin_tab = sin_ref[own, :]
+            dq_ref[own, low_cols] = (first * cos_tab + second * sin_tab).astype(dq_ref.dtype)
+            dq_ref[own, high_cols] = (second * cos_tab - first * sin_tab).astype(dq_ref.dtype)
+
+        reaches = [min(seq_len, (b + 1) * block + PIECE) for b in range(blocks)]
+        for reach in sorted(set(reaches)):
+            first = reaches.index(reach)
+            last = first + reaches.count(reach) - 1
+
+            @pl.when((block_at >= first) & (block_at <= last))
+            def _():
+                run(reach)
+
+        return carry
+
+    job_count = heads * (rows // block)
+    line_steps(axis, n, chunks, lag, x_ref, held, red, sems, finish, job, job_count)
+
+
+def attend_back(x, q, dm, k, v, norm, own_ids, all_ids, cos_tab, sin_tab, axis, n, seq_len, cid):
+    chunks = chunk_count(x.shape[0], 32, 16)
+    block = min(256, seq_len)
+    vmem = pl.BlockSpec(memory_space=pltpu.VMEM)
+    return pl.pallas_call(
+        functools.partial(attend_back_kernel, axis, n, chunks, 2, seq_len, block),
+        out_shape=(
+            jax.ShapeDtypeStruct(x.shape, jnp.bfloat16),
+            jax.ShapeDtypeStruct(q.shape, jnp.bfloat16),
+            jax.ShapeDtypeStruct((k.shape[0], 2 * k.shape[1]), jnp.float32),
+        ),
+        in_specs=[vmem] * 10,
+        out_specs=(vmem, vmem, vmem),
+        scratch_shapes=[pltpu.VMEM(x.shape, x.dtype)] * 2
+        + [pltpu.SemaphoreType.DMA((2, chunks))] * 4,
+        compiler_params=line_params(cid),
+        name="attend_back",
+    )(x, q, dm, k, v, norm, own_ids, all_ids, cos_tab, sin_tab)
 
 
 def shards(
@@ -189,16 +337,10 @@
     w_down,
     d_output,
 ):
-    row_count, model_width = block_input.shape
+    row_count, _ = block_input.shape
     dp_count = lax.axis_size("dp")
     tp_count = lax.axis_size("tensor")
     tp_index = lax.axis_index("tensor")
-
-    def sum_parts(part):
-        chunks = row_count // 32
-        while row_count % (16 * chunks):
-            chunks -= 1
-        return line_sum(part, "tensor", tp_count, chunks, 1 if part.shape[1] == model_width else 2, 2)
 
     def own_part(values, axis):
         split = values.shape[axis] // (dp_count * tp_count)
@@ -279,15 +421,23 @@
 
     mixed_seq, log_norm = lax.map(forward_seq, (query_seq, key_seq, val_seq, piece_ids))
     mixed_heads = mixed_seq.reshape(row_count, head_count * head_dim)
-    attn_out = sum_parts(jnp.dot(mixed_heads, out_proj, preferred_element_type=jnp.float32))
-    hidden_in = input_f32 + attn_out
+    first_here = (tp_index == 0).astype(jnp.float32)
+    hidden_part = (
+        jnp.dot(mixed_heads, out_proj, preferred_element_type=jnp.float32) + first_here * input_f32
+    )
+    hidden_in = line_sum(hidden_part, "tensor", tp_count, 1)
     normed_two, scale_two = normalize(hidden_in)
     normed_mid = (normed_two * gain_mlp).astype(jnp.bfloat16)
     gate_pre = jnp.dot(normed_mid, w_gate, preferred_element_type=jnp.float32)
     up_pre = jnp.dot(normed_mid, w_up, preferred_element_type=jnp.float32)
     gate_sig = jax.nn.sigmoid(gate_pre)
     hidden_act = (gate_pre * gate_sig * up_pre).astype(jnp.bfloat16)
-    mlp_part = jnp.dot(hidden_act, w_down, preferred_element_type=jnp.float32)
+    half_rows = row_count // 2
+    out_part_one, out_part_two = (
+        jnp.dot(hidden_act[at], w_down, preferred_element_type=jnp.float32)
+        + first_here * hidden_in[at]
+        for at in (slice(0, half_rows), slice(half_rows, row_count))
+    )
     grad_down = left_dot(hidden_act, d_output)
     d_act = right_dot(d_output, w_down)
     d_gate = (d_act * up_pre * gate_sig * (1.0 + gate_pre * (1.0 - gate_sig))).astype(jnp.bfloat16)
@@ -301,69 +451,38 @@
     grad_gate = lax.psum_scatter(grad_gate, "dp", scatter_dimension=0, tiled=True)
     grad_up = lax.psum_scatter(grad_up, "dp", scatter_dimension=0, tiled=True)
     grad_down = lax.psum_scatter(grad_down, "dp", scatter_dimension=1, tiled=True)
-    d_mid = sum_parts(d_mid_part)
+    d_mid = line_sum(d_mid_part, "tensor", tp_count, 1)
     grad_gain_mlp = jnp.sum(d_mid * normed_two, axis=0)
     d_hidden = cotan_f32 + norm_back(d_mid * gain_mlp, normed_two, scale_two)
     d_hidden_low = d_hidden.astype(jnp.bfloat16)
     grad_out = left_dot(mixed_heads, d_hidden_low)
     d_mixed = right_dot(d_hidden_low, out_proj).astype(jnp.bfloat16)
-    d_mixed_seq = d_mixed.reshape(seq_count, block_count, block_rows, head_count, head_dim)
-
-    def backward_seq(seq_item):
-        q_all, dm_all, norm_all, seq_keys, seq_vals, seq_ids = seq_item
-
-        def backward_block(sums_pair, block_item):
-            key_sum, val_sum = sums_pair
-            q_block, dm_block, norm_block, blk_index = block_item
-            scores = block_scores(q_block, seq_keys, seq_ids, blk_index * block_rows)
-            attn_probs = jnp.exp(scores - norm_block[..., None])
-            d_probs = jnp.einsum(
-                "qhd,kd->hqk", dm_block, seq_vals, preferred_element_type=jnp.float32
-            )
-            d_scores = (
-                attn_probs * (d_probs - jnp.sum(attn_probs * d_probs, axis=-1, keepdims=True))
-            ).astype(jnp.bfloat16)
-            d_query = (
-                jnp.einsum("hqk,kd->qhd", d_scores, seq_keys, preferred_element_type=jnp.float32)
-                * score_scale
-            )
-            key_sum = (
-                key_sum
-                + jnp.einsum("hqk,qhd->kd", d_scores, q_block, preferred_element_type=jnp.float32)
-                * score_scale
-            )
-            val_sum = val_sum + jnp.einsum(
-                "hqk,qhd->kd",
-                attn_probs.astype(jnp.bfloat16),
-                dm_block,
-                preferred_element_type=jnp.float32,
-            )
-            return ((key_sum, val_sum), d_query)
-
-        zero_rows = jnp.zeros((seq_len, head_dim), jnp.float32)
-        (key_sum, val_sum), d_query = lax.scan(
-            backward_block, (zero_rows, zero_rows), (q_all, dm_all, norm_all, block_ids)
-        )
-        return (key_sum, val_sum, d_query)
-
-    key_grad, val_grad, query_grad = lax.map(
-        backward_seq, (query_seq, d_mixed_seq, log_norm, key_seq, val_seq, piece_ids)
-    )
-    d_q_raw = unrotate(
-        query_grad.reshape(row_count, head_count, head_dim),
-        cos_all[:, None, :],
-        sin_all[:, None, :],
-    )
-    d_q_raw = d_q_raw.reshape(row_count, head_count * head_dim).astype(jnp.bfloat16)
-    key_val_part = jnp.concatenate(
-        [key_grad.reshape(row_count, head_dim), val_grad.reshape(row_count, head_dim)], axis=1
+    log_cols = jnp.transpose(log_norm, (2, 0, 1, 3)).reshape(head_count, row_count, 1)
+    out_part_one, grad_out = lax.optimization_barrier((out_part_one, grad_out))
+    grad_out = lax.psum_scatter(grad_out, "dp", scatter_dimension=1, tiled=True)
+    output_one, d_q_raw, key_val_part = attend_back(
+        out_part_one,
+        queries.reshape(row_count, head_count * head_dim),
+        d_mixed,
+        key_rows,
+        val_rows,
+        log_cols,
+        jnp.where(piece_ids > 0, piece_ids, -1).reshape(row_count, 1),
+        piece_ids.reshape(1, row_count),
+        cos_all,
+        sin_all,
+        "tensor",
+        tp_count,
+        seq_len,
+        3,
     )
     grad_query_up = left_dot(q_normed, d_q_raw)
     d_bq_part = right_dot(d_q_raw, q_up)
-    mlp_part, d_bq_part = lax.optimization_barrier((mlp_part, d_bq_part))
-    mlp_out = sum_parts(mlp_part)
-    block_output = (hidden_in + mlp_out).astype(jnp.bfloat16)
-    query_key_val = sum_parts(jnp.concatenate([d_bq_part, key_val_part], axis=1))
+    d_bq_part, grad_query_up = lax.optimization_barrier((d_bq_part, grad_query_up))
+    grad_query_up = lax.psum_scatter(grad_query_up, "dp", scatter_dimension=0, tiled=True)
+    query_key_val = line_sum(
+        jnp.concatenate([d_bq_part, key_val_part], axis=1), "tensor", tp_count, 2
+    )
     d_q_normed = query_key_val[:, : q_gain.shape[0]]
     key_val_full = query_key_val[:, q_gain.shape[0] :]
     d_key_low = unrotate(key_val_full[:, :head_dim], cos_all, sin_all).astype(jnp.bfloat16)
@@ -377,8 +496,6 @@
     grad_input = (d_hidden + norm_back(d_normed_in * gain_attn, normed_one, scale_one)).astype(
         jnp.bfloat16
     )
-    grad_query_up = lax.psum_scatter(grad_query_up, "dp", scatter_dimension=0, tiled=True)
-    grad_out = lax.psum_scatter(grad_out, "dp", scatter_dimension=1, tiled=True)
     own_in = own_part(normed_in, 1).reshape(row_count, -1)
     own_grads = left_dot(own_in, jnp.concatenate([d_latent, d_key_low, d_val_low], axis=1))
     own_rows = own_grads.shape[0]
@@ -390,6 +507,8 @@
     gain_cols = jnp.concatenate([gain_one, gain_two, gain_mid], axis=1)
     own_grads = jnp.concatenate([own_grads, jnp.pad(gain_cols, ((0, 0), (0, 125)))], axis=1)
     own_sum = lax.psum_scatter(own_grads, "dp", scatter_dimension=0, tiled=True)
+    output_two = line_sum(out_part_two, "tensor", tp_count, 4, low=True)
+    block_output = jnp.concatenate([output_one, output_two], axis=0)
     rank = q_down.shape[1]
     grad_qd = own_sum[:, :rank]
     grad_key = own_sum[:, rank : rank + head_dim]

time: 1370 us -> 1450 us (1.058)
  waiting for transfers between devices: 205 us -> 315 us
  matrix products: 221 us -> 201 us
  Pallas kernels: 768 us -> 786 us
  other arithmetic: 88.2 us -> 71.5 us
    reduce_scatter x1, waiting for transfers between devices: 21.5 us -> 91.1 us  [shards(): lax.psum_scatter(grad_gate, 'dp', scatter_dimension=0, tiled=True)]
    reduce_scatter x1, waiting for transfers between devices: 0.01 us -> 39.3 us  [shards(): grad_out = lax.psum_scatter(grad_out, 'dp', scatter_dimension=1, tiled=True)]
    pallas_call x4 -> x5, Pallas kernels: 768 us -> 786 us  [the longest x4 672 us: line_sum(): pl.pallas_call(functools.partial(line_low_kernel if low else line_kernel,...]
    convert_element_type x3 -> x0, other arithmetic: 14.5 us -> none  [the longest x1 9.77 us: shards(): block_output = (hidden_in + mlp_out).astype(jnp.bfloat16)]
    dot_general x9 -> x2, matrix products: 29.6 us -> 20.4 us  [shards(): jnp.dot(hidden_act[at], w_down, preferred_element_type=jnp.float32)]
  transfers between devices with their start and end apart: 6 -> 6, of which waited for: 3 -> 4; matrix products, arithmetic and copies ran while one was open for 3% -> 2% of each run, Pallas kernels for 15% -> 7%
where the time goes in v2:
time: 1450 us; the launch traced here: 1440 us
  Pallas kernels  786 us (54%)
  waiting for transfers between devices  315 us (22%)
  matrix products  201 us (14%)
  other arithmetic  71.5 us (5%)
  local copies, waits for them, and re-layouts  53.3 us (4%)
  between operations  15 us (1%)
    pallas_call x4, Pallas kernels, line_sum(): pl.pallas_call(functools.partial(line_low_kernel if low else line_kernel,...  672 us
    pallas_call x1, Pallas kernels, attend_back(): pl.pallas_call(functools.partial(attend_back_kernel, axis, n, chunks, 2,...  114 us
    reduce_scatter x1, waiting for transfers between devices, shards(): lax.psum_scatter(grad_gate, 'dp', scatter_dimension=0, tiled=True)  91.1 us
    reduce_scatter x1, waiting for transfers between devices, shards(): grad_up = lax.psum_scatter(grad_up, 'dp', scatter_dimension=0, tiled=True)  91.1 us
    reduce_scatter x1, waiting for transfers between devices, shards(): lax.psum_scatter(grad_down, 'dp', scatter_dimension=1, tiled=True)  90.8 us
    dot_general x8, matrix products, right_dot(): lax.dot_general(left, right, (((1,), (1,)), ((), ())), preferred_element_...  75.7 us
    dot_general x6, matrix products, left_dot(): lax.dot_general(left, right, (((0,), (0,)), ((), ())), preferred_element_...  47.3 us
    reduce_scatter x1, waiting for transfers between devices, shards(): grad_out = lax.psum_scatter(grad_out, 'dp', scatter_dimension=1, tiled=True)  39.3 us
  transfers between devices with their start and end apart: 6, of which 4 were waited for; matrix products, arithmetic and copies ran while one was open for 2% of the time, Pallas kernels for 7%

profile of v2, /device:TPU:0, one launch (start us, length us, event | category | flops | bytes accessed | tf_op | source)
XLA Modules:
  0.0 1443.2 jit_solution(16099447495769532738)
XLA Ops:
  9.3 3.1 fusion.27
  13.0 3.0 fusion.20
  16.1 6.9 copy.72
  23.0 4.4 convolution_convert_fusion.v_ref
  29.6 6.1 multiply_reduce_fusion.5
  35.7 5.3 copy.61
  41.1 4.8 fusion.56
  48.2 2.9 copy.79
  61.9 24.9 %while.22 = (s32[]{:T(128)}, bf16[2,512,4,256]{3,2,1,0:T(4,128)(2,1)}, f32[2,4,512]{2,1,0:T(4,128)S(1)}, s32[2]{0:T(128)S(1)}, s32[1024]{0:T(1024)S(1)}, /*index...) while((s32[]{:T(128)}, ...), condition=%wide.region_6.7_spmd.clone, body=%wide.region_3.6_spmd.clone.sunk | while | flops 2175269888 | bytes 49364228 | solution.py:420
  64.0 3.0 bitcast_reduce_fusion.2
  76.4 3.0 bitcast_reduce_fusion.2
  90.5 9.0 fusion.28.x_ref
  99.5 208.7 %line_sum.4 = f32[1024,2048]{1,0:T(8,128)} custom-call(f32[1024,2048]{1,0:T(8,128)} %fusion.28.x_ref), custom_call_target="tpu_custom_call" | custom-call | tf_op jit(solution)/shard_map/line_sum/pallas_call | solution.py:206
  308.2 4.1 multiply_reduce_fusion.2
  314.8 11.9 fusion.62
  326.6 8.4 fusion.61
  335.1 15.2 %multiply_convert_fusion.1 = (bf16[1024,1408]{1,0:T(8,128)(2,1)}, bf16[1024,1408]{1,0:T(8,128)(2,1)}, bf16[1024,1408]{1,0:T(8,128)(2,1)}) fusion(f32[1024,1408]{1,0:T(8,128)} %fusion.61, f32[1024,1408]{1,0:T(8,128)} %fusion.62, bf16[1024,2048]{1,0:T(8,128)(2,1)S(1)} %copy-done.14, bf16[1408,2048]{1,0:T(8,128)(2,1)} %param.28), kind=kOutput, calls=%fused_computation.47 | convolution fusion | flops 5928648704 | bytes 30146560 | tf_op jit(solution)/shard_map/dot_general | solution.py:38
  350.3 12.8 fusion.63
  363.1 9.6 fusion.65
  372.7 9.9 multiply_add_fusion.2.x_ref
  382.6 9.0 fusion.64
  391.6 12.1 fusion.66
  403.7 12.8 convolution_add_fusion.x_ref
  416.5 203.8 %line_sum.5 = f32[1024,2048]{1,0:T(8,128)} custom-call(f32[1024,2048]{1,0:T(8,128)} %convolution_add_fusion.x_ref), custom_call_target="tpu_custom_call" | custom-call | tf_op jit(solution)/shard_map/line_sum/pallas_call | solution.py:206
  620.3 8.0 multiply_reduce_fusion
  631.0 4.4 multiply_add_fusion
  635.4 10.7 fusion.41.dm_ref
  646.2 6.8 fusion.39
  656.1 3.2 copy.80
  659.3 113.7 %attend_back.1 = (bf16[512,2048]{1,0:T(8,128)(2,1)}, bf16[1024,1024]{1,0:T(8,128)(2,1)}, f32[1024,512]{1,0:T(8,128)}) custom-call(f32[512,2048]{1,0:T(8,128)} %multiply_add_fusion.2.x_ref, bf16[1024,1024]{1,0:T(8,128)(2,1)} %bitcast.116, bf16[1024,1024]{1,0:T(8,128)(2,1)} %fusion.41.dm_ref, bf16[1024,256]{1,0:T(8,128)(2,1)S(1)} %copy-done.19, ...), custom_call_target="tpu_custom_call" | custom-call | tf_op jit(solution)/shard_map/attend_back/pallas_call | solution.py:308
  773.0 6.1 fusion.55
  779.2 4.1 fusion.67
  783.3 3.2 pad_maximum_fusion.x_ref
  786.5 155.7 %line_sum.7 = f32[1024,1536]{1,0:T(8,128)} custom-call(f32[1024,1536]{1,0:T(8,128)} %pad_maximum_fusion.x_ref), custom_call_target="tpu_custom_call" | custom-call | tf_op jit(solution)/shard_map/line_sum/pallas_call | solution.py:206
  942.2 3.3 multiply_reduce_fusion.3
  945.5 4.1 add_convert_fusion.1
  953.2 4.9 multiply_convert_fusion.4
  958.3 10.7 fusion.68
  971.5 8.1 fusion.26
  980.7 3.7 fusion.29
  989.6 10.5 multiply_add_fusion.1.x_ref
  1000.1 103.8 %line_sum.6 = bf16[512,2048]{1,0:T(8,128)(2,1)} custom-call(f32[512,2048]{1,0:T(8,128)} %multiply_add_fusion.1.x_ref), custom_call_target="tpu_custom_call" | custom-call | tf_op jit(solution)/shard_map/line_sum/pallas_call | solution.py:206
  1104.0 4.8 pad_maximum_fusion.1
  1108.8 8.9 fusion.25
  1123.9 39.3 %reduce-scatter.11.cloned.1.call-done = f32[1024,256]{1,0:T(8,128)} async-done(((f32[1024,2048]{1,0:T(8,128)}), f32[1024,256]{1,0:T(8,128)}) %reduce-scatter.11.cloned.1.call-update) | async-done | bytes 1048592 | tf_op jit(solution)/shard_map/reduce_scatter | solution.py:462
  1163.2 91.1 %reduce-scatter.13.cloned.1.call-done = f32[256,1408]{1,0:T(8,128)} async-done(((f32[2048,1408]{1,0:T(8,128)}), f32[256,1408]{1,0:T(8,128)}) %reduce-scatter.13.cloned.1.call-update) | async-done | bytes 1441808 | tf_op jit(solution)/shard_map/reduce_scatter | solution.py:451
  1254.3 91.1 %reduce-scatter.15.cloned.1.call-done = f32[256,1408]{1,0:T(8,128)} async-done(((f32[2048,1408]{1,0:T(8,128)}), f32[256,1408]{1,0:T(8,128)}) %reduce-scatter.15.cloned.1.call-update) | async-done | bytes 1441808 | tf_op jit(solution)/shard_map/reduce_scatter | solution.py:452
  1345.4 90.8 %reduce-scatter.17.cloned.1.call-done = f32[1408,256]{1,0:T(8,128)} async-done(((f32[1408,2048]{1,0:T(8,128)}), f32[1408,256]{1,0:T(8,128)}) %reduce-scatter.17.cloned.1.call-update) | async-done | bytes 1441808 | tf_op jit(solution)/shard_map/reduce_scatter | solution.py:453
  (200 shorter events, 65.5 us)
Async XLA Ops:
  7.2 33.9 %copy-start = (bf16[1024,1024]{1,0:T(8,128)(2,1)S(1)}, bf16[1024,1024]{1,0:T(8,128)(2,1)}, u32[]{:S(2)}) copy-start(bf16[1024,1024]{1,0:T(8,128)(2,1)} %param.21) | copy-start | bytes 6291460
  7.2 5.2 copy-start.46
  7.2 5.2 copy-start.47
  7.2 1110.5 %reduce-scatter.7.cloned.1.call-start = ((), (), s32[]{:S(2)}) async-start(), calls=%async_computation.6 | async-start | bytes 3833856 | tf_op jit(solution)/shard_map/reduce_scatter | solution.py:509
  7.3 46.7 %copy-start.48 = (f32[128]{0:T(128)}, f32[128]{0:T(128)S(1)}, u32[]{:S(2)}) copy-start(f32[128]{0:T(128)S(1)} %multiply_power_fusion) | copy-start | bytes 1540
  7.3 5.7 copy-start.3
  9.3 31.8 %copy-start.40 = (f32[1024]{0:T(1024)}, f32[1024]{0:T(1024)S(1)}, u32[]{:S(2)}) copy-start(f32[1024]{0:T(1024)S(1)} %convert_element_type.76) | copy-start | bytes 12292
  16.1 6.9 copy-start.28
  23.0 4.4 copy-start.10
  23.0 4.4 copy-start.26
  35.7 5.4 copy-start.42
  86.7 12.7 copy-start.18
  86.7 12.7 copy-start.34
  86.7 12.7 copy-start.44
  86.7 3.7 copy-start.4
  308.2 5.8 copy-start.1
  313.9 12.7 slice-start.2
  314.7 48.3 %copy-start.17 = (bf16[1024,2048]{1,0:T(8,128)(2,1)}, bf16[1024,2048]{1,0:T(8,128)(2,1)S(1)}, u32[]{:S(2)}) copy-start(bf16[1024,2048]{1,0:T(8,128)(2,1)S(1)} %multiply_convert_fusion) | copy-start | bytes 12582916
  314.7 11.9 slice-start.3
  326.6 8.5 copy-start.14
  350.3 12.8 copy-start.53
  372.7 9.9 copy-start.15
  372.7 9.9 copy-start.52
  416.5 211.9 %slice-start = ((s8[8388608]{0:T(1024)(128)(4,1)}), s8[4194304]{0:T(1024)(128)(4,1)S(1)}, s32[]{:S(2)}) async-start(s8[8388608]{0:T(1024)(128)(4,1)} %bitcast.112), calls=%async_computation.12 | async-start | bytes 8388608
  620.3 8.1 slice-start.1
  620.3 9.5 copy-start.2
  620.3 10.7 copy-start.16
  635.4 10.7 copy-start.9
  635.4 10.7 copy-start.23
  646.2 6.8 copy-start.35
  646.2 7.9 copy-start.45
  653.0 6.2 copy-start.19
  654.1 5.2 copy-start.33
  659.2 113.8 %copy-start.7 = (f32[1024,1024]{1,0:T(8,128)S(1)}, f32[1024,1024]{1,0:T(8,128)}, u32[]{:S(2)}) copy-start(f32[1024,1024]{1,0:T(8,128)} %copy.61) | copy-start | bytes 12582916
  659.2 113.8 %copy-start.41 = (f32[1024]{0:T(1024)S(1)}, f32[1024]{0:T(1024)}, u32[]{:S(2)}) copy-start(f32[1024]{0:T(1024)} %copy-done.40) | copy-start | bytes 12292
  659.3 113.8 %copy-start.43 = (f32[1024]{0:T(1024)S(1)}, f32[1024]{0:T(1024)}, u32[]{:S(2)}) copy-start(f32[1024]{0:T(1024)} %copy-done.42) | copy-start | bytes 12292
  779.2 4.1 copy-start.25
  786.5 155.7 %copy-start.8 = (f32[1024,1024]{1,0:T(8,128)S(1)}, f32[1024,1024]{1,0:T(8,128)}, u32[]{:S(2)}) copy-start(f32[1024,1024]{1,0:T(8,128)} %copy.61) | copy-start | bytes 12582916
  958.3 10.7 copy-start.27
  958.3 10.7 copy-start.30
  980.7 3.7 copy-start.31
  986.4 137.6 %reduce-scatter.9.cloned.1.call-start = ((), (), s32[]{:S(2)}) async-start(), calls=%async_computation.7 | async-start | bytes 4718592 | tf_op jit(solution)/shard_map/reduce_scatter | solution.py:482
  987.1 176.1 %reduce-scatter.11.cloned.1.call-start = ((), (), s32[]{:S(2)}) async-start(), calls=%async_computation.8 | async-start | bytes 9437184 | tf_op jit(solution)/shard_map/reduce_scatter | solution.py:462
  987.8 266.5 %reduce-scatter.13.cloned.1.call-start = ((), (), s32[]{:S(2)}) async-start(), calls=%async_computation.9 | async-start | bytes 12976128 | tf_op jit(solution)/shard_map/reduce_scatter | solution.py:451
  988.4 357.0 %reduce-scatter.15.cloned.1.call-start = ((), (), s32[]{:S(2)}) async-start(), calls=%async_computation.10 | async-start | bytes 12976128 | tf_op jit(solution)/shard_map/reduce_scatter | solution.py:452
  989.0 447.2 %reduce-scatter.17.cloned.1.call-start = ((), (), s32[]{:S(2)}) async-start(), calls=%async_computation.11 | async-start | bytes 12976128 | tf_op jit(solution)/shard_map/reduce_scatter | solution.py:453
  1000.1 103.9 %copy-start.24 = (bf16[512,2048]{1,0:T(8,128)(2,1)S(1)}, bf16[512,2048]{1,0:T(8,128)(2,1)}, u32[]{:S(2)}) copy-start(bf16[512,2048]{1,0:T(8,128)(2,1)} %get-tuple-element.103) | copy-start | bytes 6291460
  1104.0 4.8 copy-start.6
  (18 other events, 39.5 us)
Sparse Core Ops, SparseCore 0:
  986.5 46.2 reduce-scatter.6
  1036.7 51.1 reduce-scatter.8
  1091.9 71.2 reduce-scatter.10
  1167.2 87.1 reduce-scatter.12
  1258.3 87.0 reduce-scatter.14
  1349.3 86.8 reduce-scatter.16

commit v3 on v2

--- a/solution.py
+++ b/solution.py
@@ -66,7 +66,7 @@
     )
 
 
-def line_steps(axis, n, chunks, lag, x_ref, held, red, sems, finish, job, job_count):
+def line_steps(axis, n, chunks, lag, x_ref, held, red, sems, finish, job, job_range):
     me = lax.axis_index(axis)
     rows = x_ref.shape[0] // (2 * chunks)
     s_red, r_red, s_fin, r_fin = sems
@@ -153,8 +153,8 @@
             def _():
                 finish(at(half, c))
 
-        if job_count:
-            lax.fori_loop(s * job_count // steps, (s + 1) * job_count // steps, job, 0)
+        if job is not None:
+            lax.fori_loop(*job_range(s, steps), job, 0)
         return carry
 
     lax.fori_loop(0, steps, step, 0)
@@ -177,14 +177,14 @@
 
 
 def line_kernel(axis, n, chunks, lag, x_ref, o_ref, red, *sems):
-    line_steps(axis, n, chunks, lag, x_ref, o_ref, red, sems, lambda at: None, None, 0)
+    line_steps(axis, n, chunks, lag, x_ref, o_ref, red, sems, lambda at: None, None, None)
 
 
 def line_low_kernel(axis, n, chunks, lag, x_ref, o_ref, red, held, *sems):
     def finish(at):
         o_ref[at] = held[at].astype(o_ref.dtype)
 
-    line_steps(axis, n, chunks, lag, x_ref, held, red, sems, finish, None, 0)
+    line_steps(axis, n, chunks, lag, x_ref, held, red, sems, finish, None, None)
 
 
 def chunk_count(rows, most, tile):
@@ -214,6 +214,135 @@
         compiler_params=line_params(cid),
         name="line_sum",
     )(x)
+
+
+def attend_kernel(
+    axis,
+    n,
+    chunks,
+    lag,
+    seq_len,
+    block,
+    raw_ref,
+    k_ref,
+    v_ref,
+    own_ref,
+    all_ref,
+    cos_ref,
+    sin_ref,
+    out_ref,
+    base_ref,
+    o_ref,
+    q_ref,
+    mixed_ref,
+    norm_ref,
+    part,
+    red,
+    *sems,
+):
+    rows, head_dim = k_ref.shape
+    heads = raw_ref.shape[1] // head_dim
+    half_dim = head_dim // 2
+    blocks = seq_len // block
+    scale = head_dim ** (-0.5)
+    pairs = rows // (2 * block)
+    turns = heads + 1
+    pair_jobs = 2 * turns
+
+    def job(j, carry):
+        pair = lax.div(j, pair_jobs)
+        side = lax.div(lax.rem(j, pair_jobs), turns)
+        head = lax.rem(j, turns)
+        row_block = side * pairs + pair
+        seq = lax.div(row_block, blocks)
+        block_at = lax.rem(row_block, blocks)
+        own = pl.ds(pl.multiple_of(row_block * block, block), block)
+        cols = pl.ds(pl.multiple_of(head * head_dim, head_dim), head_dim)
+        low_cols = pl.ds(pl.multiple_of(head * head_dim, half_dim), half_dim)
+        high_cols = pl.ds(pl.multiple_of(head * head_dim + half_dim, half_dim), half_dim)
+
+        def run(reach):
+            keys = pl.ds(pl.multiple_of(seq * seq_len, seq_len), reach)
+            first = raw_ref[own, low_cols]
+            second = raw_ref[own, high_cols]
+            cos_tab = cos_ref[own, :]
+            sin_tab = sin_ref[own, :]
+            q_ref[own, low_cols] = (first * cos_tab - second * sin_tab).astype(q_ref.dtype)
+            q_ref[own, high_cols] = (second * cos_tab + first * sin_tab).astype(q_ref.dtype)
+            scores = right_dot(q_ref[own, cols], k_ref[keys, :]) * scale
+            q_pos = block_at * block + lax.broadcasted_iota(jnp.int32, scores.shape, 0)
+            k_pos = lax.broadcasted_iota(jnp.int32, scores.shape, 1)
+            same = own_ref[own, :] == all_ref[:, keys]
+            scores = jnp.where((k_pos <= q_pos) | same, scores, masked_score)
+            row_max = jnp.max(scores, axis=1, keepdims=True)
+            exp_terms = jnp.exp(scores - row_max)
+            row_sum = jnp.sum(exp_terms, axis=1, keepdims=True)
+            probs = (exp_terms * (1.0 / row_sum)).astype(jnp.bfloat16)
+            mixed = jnp.dot(probs, v_ref[keys, :], preferred_element_type=jnp.float32)
+            mixed_ref[own, cols] = mixed.astype(mixed_ref.dtype)
+            norm_ref[head, own, :] = row_max + jnp.log(row_sum)
+
+        reaches = reach_list(seq_len, block)
+        for reach in sorted(set(reaches)):
+            first = reaches.index(reach)
+            last = first + reaches.count(reach) - 1
+
+            @pl.when((head < heads) & (block_at >= first) & (block_at <= last))
+            def _():
+                run(reach)
+
+        @pl.when(head == heads)
+        def _():
+            part[own, :] = jnp.dot(
+                mixed_ref[own, :], out_ref[...], preferred_element_type=jnp.float32
+            )
+
+        @pl.when((head == heads) & (lax.axis_index(axis) == 0))
+        def _():
+            part[own, :] += base_ref[own, :].astype(jnp.float32)
+
+        return carry
+
+    lax.fori_loop(0, pair_jobs, job, 0)
+    pair_steps = chunks // pairs
+
+    def job_range(s, steps):
+        return tuple(
+            jnp.minimum((pair_steps + at) * pair_jobs // pair_steps, pairs * pair_jobs)
+            for at in (s, s + 1)
+        )
+
+    line_steps(axis, n, chunks, lag, part, o_ref, red, sems, lambda at: None, job, job_range)
+
+
+def reach_list(seq_len, block):
+    step = max(256, block)
+    ends = [(b + 1) * block + PIECE for b in range(seq_len // block)]
+    return [min(seq_len, -(-end // step) * step) for end in ends]
+
+
+def attend(raw, k, v, own_ids, all_ids, cos_tab, sin_tab, out_proj, base, axis, n, seq_len, cid):
+    rows, width = base.shape
+    block = min(128, seq_len)
+    chunks = chunk_count(rows, 32, 8)
+    vmem = pl.BlockSpec(memory_space=pltpu.VMEM)
+    return pl.pallas_call(
+        functools.partial(attend_kernel, axis, n, chunks, 2, seq_len, block),
+        out_shape=(
+            jax.ShapeDtypeStruct((rows, width), jnp.float32),
+            jax.ShapeDtypeStruct(raw.shape, jnp.bfloat16),
+            jax.ShapeDtypeStruct(raw.shape, jnp.bfloat16),
+            jax.ShapeDtypeStruct((raw.shape[1] // k.shape[1], rows, 1), jnp.float32),
+        ),
+        in_specs=[vmem] * 9,
+        out_specs=(vmem,) * 4,
+        scratch_shapes=[pltpu.VMEM((rows, width), jnp.float32)] * 2
+        + [pltpu.SemaphoreType.DMA((2, chunks))] * 4,
+        compiler_params=pltpu.CompilerParams(
+            collective_id=cid, has_side_effects=True, vmem_limit_bytes=60 << 20
+        ),
+        name="attend",
+    )(raw, k, v, own_ids, all_ids, cos_tab, sin_tab, out_proj, base)
 
 
 def attend_back_kernel(
@@ -233,9 +362,10 @@
     all_ref,
     cos_ref,
     sin_ref,
+    up_ref,
     o_ref,
     dq_ref,
-    dkv_ref,
+    sums_ref,
     red,
     held,
     *sems,
@@ -245,7 +375,10 @@
     half_dim = head_dim // 2
     blocks = seq_len // block
     scale = head_dim ** (-0.5)
-    dkv_ref[...] = jnp.zeros_like(dkv_ref)
+    rank = up_ref.shape[0]
+    key_cols = slice(rank, rank + head_dim)
+    val_cols = slice(rank + head_dim, rank + 2 * head_dim)
+    sums_ref[:, rank:] = jnp.zeros((rows, 2 * head_dim), jnp.float32)
 
     def finish(at):
         o_ref[at] = held[at].astype(o_ref.dtype)
@@ -276,8 +409,8 @@
             d_probs = right_dot(dm, v)
             row_sum = jnp.sum(probs * d_probs, axis=1, keepdims=True)
             d_scores = (probs * (d_probs - row_sum)).astype(jnp.bfloat16)
-            dkv_ref[keys, 0:head_dim] += left_dot(d_scores, q) * scale
-            dkv_ref[keys, head_dim : 2 * head_dim] += left_dot(probs.astype(jnp.bfloat16), dm)
+            sums_ref[keys, key_cols] += left_dot(d_scores, q) * scale
+            sums_ref[keys, val_cols] += left_dot(probs.astype(jnp.bfloat16), dm)
             dq = jnp.dot(d_scores, k, preferred_element_type=jnp.float32) * scale
             first = dq[:, :half_dim]
             second = dq[:, half_dim:]
@@ -286,7 +419,7 @@
             dq_ref[own, low_cols] = (first * cos_tab + second * sin_tab).astype(dq_ref.dtype)
             dq_ref[own, high_cols] = (second * cos_tab - first * sin_tab).astype(dq_ref.dtype)
 
-        reaches = [min(seq_len, (b + 1) * block + PIECE) for b in range(blocks)]
+        reaches = reach_list(seq_len, block)
         for reach in sorted(set(reaches)):
             first = reaches.index(reach)
             last = first + reaches.count(reach) - 1
@@ -295,13 +428,23 @@
             def _():
                 run(reach)
 
+        @pl.when(head == heads - 1)
+        def _():
+            sums_ref[own, 0:rank] = right_dot(dq_ref[own, :], up_ref[...])
+
         return carry
 
     job_count = heads * (rows // block)
-    line_steps(axis, n, chunks, lag, x_ref, held, red, sems, finish, job, job_count)
-
-
-def attend_back(x, q, dm, k, v, norm, own_ids, all_ids, cos_tab, sin_tab, axis, n, seq_len, cid):
+
+    def job_range(s, steps):
+        return s * job_count // steps, (s + 1) * job_count // steps
+
+    line_steps(axis, n, chunks, lag, x_ref, held, red, sems, finish, job, job_range)
+
+
+def attend_back(
+    x, q, dm, k, v, norm, own_ids, all_ids, cos_tab, sin_tab, q_up, axis, n, seq_len, cid
+):
     chunks = chunk_count(x.shape[0], 32, 16)
     block = min(256, seq_len)
     vmem = pl.BlockSpec(memory_space=pltpu.VMEM)
@@ -310,15 +453,15 @@
         out_shape=(
             jax.ShapeDtypeStruct(x.shape, jnp.bfloat16),
             jax.ShapeDtypeStruct(q.shape, jnp.bfloat16),
-            jax.ShapeDtypeStruct((k.shape[0], 2 * k.shape[1]), jnp.float32),
+            jax.ShapeDtypeStruct((k.shape[0], q_up.shape[0] + 2 * k.shape[1]), jnp.float32),
         ),
-        in_specs=[vmem] * 10,
+        in_specs=[vmem] * 11,
         out_specs=(vmem, vmem, vmem),
         scratch_shapes=[pltpu.VMEM(x.shape, x.dtype)] * 2
         + [pltpu.SemaphoreType.DMA((2, chunks))] * 4,
         compiler_params=line_params(cid),
         name="attend_back",
-    )(x, q, dm, k, v, norm, own_ids, all_ids, cos_tab, sin_tab)
+    )(x, q, dm, k, v, norm, own_ids, all_ids, cos_tab, sin_tab, q_up)
 
 
 def shards(
@@ -351,10 +494,6 @@
     seq_count = image_starts.shape[0]
     seq_len = row_count // seq_count
     head_dim = k_proj.shape[1]
-    head_count = q_up.shape[1] // head_dim
-    block_rows = min(512, seq_len)
-    block_count = seq_len // block_rows
-    score_scale = head_dim ** (-0.5)
     positions = jnp.arange(seq_len, dtype=jnp.float32)
     inv_freq = 10000.0 ** (-(jnp.arange(head_dim // 2, dtype=jnp.float32) * 2.0) / head_dim)
     angles = positions[:, None] * inv_freq[None, :]
@@ -367,18 +506,8 @@
     labels = jnp.arange(1, image_starts.shape[1] + 1, dtype=jnp.int32)
     piece_ids = jnp.sum(jnp.where(inside, labels, 0), axis=2)
 
-    def block_scores(q_block, key_rows, seq_ids, row_start):
-        raw = (
-            jnp.einsum("qhd,kd->hqk", q_block, key_rows, preferred_element_type=jnp.float32)
-            * score_scale
-        )
-        query_pos = row_start + jnp.arange(block_rows, dtype=jnp.int32)
-        query_ids = lax.dynamic_slice_in_dim(seq_ids, row_start, block_rows)
-        visible = (pos_int[None, :] <= query_pos[:, None]) | (
-            query_ids[:, None] == seq_ids[None, :]
-        ) & (query_ids[:, None] > 0)
-        return jnp.where(visible[None], raw, masked_score)
-
+    own_ids = jnp.where(piece_ids > 0, piece_ids, -1).reshape(row_count, 1)
+    all_ids = piece_ids.reshape(1, row_count)
     input_f32 = block_input.astype(jnp.float32)
     gain_attn = norm_gain.astype(jnp.float32)
     gain_query = q_gain.astype(jnp.float32)
@@ -389,43 +518,27 @@
     q_latent = jnp.dot(normed_in, q_down, preferred_element_type=jnp.float32)
     q_unit, q_scale = normalize(q_latent)
     q_normed = (q_unit * gain_query).astype(jnp.bfloat16)
-    q_raw = jnp.dot(q_normed, q_up, preferred_element_type=jnp.float32).reshape(
-        row_count, head_count, head_dim
-    )
-    queries = rotate(q_raw, cos_all[:, None, :], sin_all[:, None, :]).astype(jnp.bfloat16)
+    q_raw = jnp.dot(q_normed, q_up, preferred_element_type=jnp.float32)
     key_rows = rotate(
         jnp.dot(normed_in, k_proj, preferred_element_type=jnp.float32), cos_all, sin_all
     ).astype(jnp.bfloat16)
     val_rows = jnp.dot(normed_in, v_proj, preferred_element_type=jnp.float32).astype(jnp.bfloat16)
-    query_seq = queries.reshape(seq_count, block_count, block_rows, head_count, head_dim)
-    key_seq = key_rows.reshape(seq_count, seq_len, head_dim)
-    val_seq = val_rows.reshape(seq_count, seq_len, head_dim)
-    block_ids = jnp.arange(block_count, dtype=jnp.int32)
-
-    def forward_seq(seq_item):
-        q_all, seq_keys, seq_vals, seq_ids = seq_item
-
-        def forward_block(block_item):
-            q_block, blk_index = block_item
-            scores = block_scores(q_block, seq_keys, seq_ids, blk_index * block_rows)
-            row_max = jnp.max(scores, axis=-1, keepdims=True)
-            exp_terms = jnp.exp(scores - row_max)
-            row_sum = jnp.sum(exp_terms, axis=-1, keepdims=True)
-            attn_probs = (exp_terms / row_sum).astype(jnp.bfloat16)
-            mixed_block = jnp.einsum(
-                "hqk,kd->qhd", attn_probs, seq_vals, preferred_element_type=jnp.float32
-            )
-            return (mixed_block.astype(jnp.bfloat16), (row_max + jnp.log(row_sum))[..., 0])
-
-        return lax.map(forward_block, (q_all, block_ids))
-
-    mixed_seq, log_norm = lax.map(forward_seq, (query_seq, key_seq, val_seq, piece_ids))
-    mixed_heads = mixed_seq.reshape(row_count, head_count * head_dim)
     first_here = (tp_index == 0).astype(jnp.float32)
-    hidden_part = (
-        jnp.dot(mixed_heads, out_proj, preferred_element_type=jnp.float32) + first_here * input_f32
-    )
-    hidden_in = line_sum(hidden_part, "tensor", tp_count, 1)
+    hidden_in, queries, mixed_heads, log_norm = attend(
+        q_raw,
+        key_rows,
+        val_rows,
+        own_ids,
+        all_ids,
+        cos_all,
+        sin_all,
+        out_proj,
+        block_input,
+        "tensor",
+        tp_count,
+        seq_len,
+        5,
+    )
     normed_two, scale_two = normalize(hidden_in)
     normed_mid = (normed_two * gain_mlp).astype(jnp.bfloat16)
     gate_pre = jnp.dot(normed_mid, w_gate, preferred_element_type=jnp.float32)
@@ -457,32 +570,29 @@
     d_hidden_low = d_hidden.astype(jnp.bfloat16)
     grad_out = left_dot(mixed_heads, d_hidden_low)
     d_mixed = right_dot(d_hidden_low, out_proj).astype(jnp.bfloat16)
-    log_cols = jnp.transpose(log_norm, (2, 0, 1, 3)).reshape(head_count, row_count, 1)
     out_part_one, grad_out = lax.optimization_barrier((out_part_one, grad_out))
     grad_out = lax.psum_scatter(grad_out, "dp", scatter_dimension=1, tiled=True)
-    output_one, d_q_raw, key_val_part = attend_back(
+    output_one, d_q_raw, query_key_val = attend_back(
         out_part_one,
-        queries.reshape(row_count, head_count * head_dim),
+        queries,
         d_mixed,
         key_rows,
         val_rows,
-        log_cols,
-        jnp.where(piece_ids > 0, piece_ids, -1).reshape(row_count, 1),
-        piece_ids.reshape(1, row_count),
+        log_norm,
+        own_ids,
+        all_ids,
         cos_all,
         sin_all,
+        q_up,
         "tensor",
         tp_count,
         seq_len,
         3,
     )
     grad_query_up = left_dot(q_normed, d_q_raw)
-    d_bq_part = right_dot(d_q_raw, q_up)
-    d_bq_part, grad_query_up = lax.optimization_barrier((d_bq_part, grad_query_up))
+    query_key_val, grad_query_up = lax.optimization_barrier((query_key_val, grad_query_up))
     grad_query_up = lax.psum_scatter(grad_query_up, "dp", scatter_dimension=0, tiled=True)
-    query_key_val = line_sum(
-        jnp.concatenate([d_bq_part, key_val_part], axis=1), "tensor", tp_count, 2
-    )
+    query_key_val = line_sum(query_key_val, "tensor", tp_count, 2)
     d_q_normed = query_key_val[:, : q_gain.shape[0]]
     key_val_full = query_key_val[:, q_gain.shape[0] :]
     d_key_low = unrotate(key_val_full[:, :head_dim], cos_all, sin_all).astype(jnp.bfloat16)

time: 1450 us -> 1400 us (0.966)
  matrix products: 201 us -> 177 us
  local copies, waits for them, and re-layouts: 53.3 us -> 29.5 us
  Pallas kernels: 786 us -> 802 us
    pallas_call x0 -> x1, Pallas kernels: none -> 221 us  [attend(): pl.pallas_call(functools.partial(attend_kernel, axis, n, chunks, 2, seq_l...]
    pallas_call x4 -> x3, Pallas kernels: 672 us -> 464 us  [line_sum(): pl.pallas_call(functools.partial(line_low_kernel if low else line_kernel,...]
    dot_general x6 -> x1, matrix products: 25.1 us -> 6.59 us  [shards(): q_raw = jnp.dot(q_normed, q_up, preferred_element_type=jnp.float32)]
    dot_general x8 -> x7, matrix products: 75.7 us -> 69.1 us  [right_dot(): lax.dot_general(left, right, (((1,), (1,)), ((), ())), preferred_element_...]
  transfers between devices with their start and end apart: 6 -> 6, of which waited for: 4 -> 4; matrix products, arithmetic and copies ran while one was open for 2% -> 2% of each run, Pallas kernels for 7% -> 8%
where the time goes in v3:
time: 1400 us
  Pallas kernels  802 us (57%)
  waiting for transfers between devices  315 us (22%)
  matrix products  177 us (13%)
  other arithmetic  60.2 us (4%)
  local copies, waits for them, and re-layouts  29.5 us (2%)
  between operations  14.8 us (1%)
    pallas_call x3, Pallas kernels, line_sum(): pl.pallas_call(functools.partial(line_low_kernel if low else line_kernel,...  464 us
    pallas_call x1, Pallas kernels, attend(): pl.pallas_call(functools.partial(attend_kernel, axis, n, chunks, 2, seq_l...  221 us
    pallas_call x1, Pallas kernels, attend_back(): pl.pallas_call(functools.partial(attend_back_kernel, axis, n, chunks, 2,...  117 us
    reduce_scatter x1, waiting for transfers between devices, shards(): lax.psum_scatter(grad_gate, 'dp', scatter_dimension=0, tiled=True)  91.1 us
    reduce_scatter x1, waiting for transfers between devices, shards(): grad_up = lax.psum_scatter(grad_up, 'dp', scatter_dimension=0, tiled=True)  91.1 us
    reduce_scatter x1, waiting for transfers between devices, shards(): lax.psum_scatter(grad_down, 'dp', scatter_dimension=1, tiled=True)  90.8 us
    dot_general x7, matrix products, right_dot(): lax.dot_general(left, right, (((1,), (1,)), ((), ())), preferred_element_...  69.1 us
    dot_general x6, matrix products, left_dot(): lax.dot_general(left, right, (((0,), (0,)), ((), ())), preferred_element_...  48 us
  transfers between devices with their start and end apart: 6, of which 4 were waited for; matrix products, arithmetic and copies ran while one was open for 2% of the time, Pallas kernels for 8%

profile of v3, /device:TPU:0, one launch (start us, length us, event | category | flops | bytes accessed | tf_op | source)
XLA Modules:
  0.0 1398.8 jit_solution(13964105660885824538)
XLA Ops:
  8.7 3.1 fusion.11
  13.1 5.2 fusion.4
  18.3 6.7 copy.51
  25.0 4.4 convolution_convert_fusion.v_ref
  29.4 2.2 fusion.42
  31.6 6.1 multiply_reduce_fusion.5
  37.8 5.5 copy.46
  43.3 4.3 subtract_convert_fusion.1
  48.4 6.6 fusion.39.raw_ref
  55.0 220.7 %attend.1 = (f32[1024,2048]{1,0:T(8,128)}, bf16[1024,1024]{1,0:T(8,128)(2,1)}, bf16[1024,1024]{1,0:T(8,128)(2,1)}, f32[4,1024,1]{2,1,0:T(8,128)}) custom-call(f32[1024,1024]{1,0:T(8,128)} %fusion.39.raw_ref, bf16[1024,256]{1,0:T(8,128)(2,1)} %pad_maximum_fusion.1.k_ref, bf16[1024,256]{1,0:T(8,128)(2,1)} %convolution_convert_fusion.v_ref, ...), custom_call_target="tpu_custom_call" | custom-call | tf_op jit(solution)/shard_map/attend/pallas_call | solution.py:329
  275.8 4.1 multiply_reduce_fusion.2
  279.9 1.6 copy-done.1
  282.3 11.8 fusion.44
  294.2 8.5 fusion.43
  302.6 15.4 %multiply_convert_fusion.1 = (bf16[1024,1408]{1,0:T(8,128)(2,1)}, bf16[1024,1408]{1,0:T(8,128)(2,1)}, bf16[1024,1408]{1,0:T(8,128)(2,1)}) fusion(f32[1024,1408]{1,0:T(8,128)} %fusion.43, f32[1024,1408]{1,0:T(8,128)} %fusion.44, bf16[1024,2048]{1,0:T(8,128)(2,1)S(1)} %copy-done.9, bf16[1408,2048]{1,0:T(8,128)(2,1)} %param.26), kind=kOutput, calls=%fused_computation.20 | convolution fusion | flops 5928648704 | bytes 30146560 | tf_op jit(solution)/shard_map/dot_general | solution.py:38
  318.1 11.8 fusion.45
  329.9 9.6 fusion.47
  339.5 11.5 fusion.46
  351.1 9.9 multiply_add_fusion.2.x_ref
  360.9 9.6 fusion.48
  370.5 12.9 convolution_add_fusion.x_ref
  383.4 204.6 %line_sum.3 = f32[1024,2048]{1,0:T(8,128)} custom-call(f32[1024,2048]{1,0:T(8,128)} %convolution_add_fusion.x_ref), custom_call_target="tpu_custom_call" | custom-call | tf_op jit(solution)/shard_map/line_sum/pallas_call | solution.py:206
  588.0 8.1 multiply_reduce_fusion
  598.7 4.3 multiply_add_fusion
  603.1 10.6 fusion.24.dm_ref
  613.6 6.8 fusion.22
  620.5 117.2 %attend_back.1 = (bf16[512,2048]{1,0:T(8,128)(2,1)}, bf16[1024,1024]{1,0:T(8,128)(2,1)}, f32[1024,1536]{1,0:T(8,128)}) custom-call(f32[512,2048]{1,0:T(8,128)} %multiply_add_fusion.2.x_ref, bf16[1024,1024]{1,0:T(8,128)(2,1)} %get-tuple-element.32.q_ref, bf16[1024,1024]{1,0:T(8,128)(2,1)} %fusion.24.dm_ref, bf16[1024,256]{1,0:T(8,128)(2,1)} %pad_maximum_fusion.1.k_ref, ...), custom_call_target="tpu_custom_call" | custom-call | tf_op jit(solution)/shard_map/attend_back/pallas_call | solution.py:451
  737.7 6.2 fusion.38
  743.9 153.7 %line_sum.5 = f32[1024,1536]{1,0:T(8,128)} custom-call(f32[1024,1536]{1,0:T(8,128)} %get-tuple-element.37.x_ref), custom_call_target="tpu_custom_call" | custom-call | tf_op jit(solution)/shard_map/line_sum/pallas_call | solution.py:206
  897.7 3.3 multiply_reduce_fusion.3
  900.9 4.1 add_convert_fusion
  905.1 2.1 slice.103
  907.2 2.3 constant_dynamic-slice_fusion
  909.6 4.0 multiply_convert_fusion.4
  913.7 9.0 fusion.49
  924.9 8.2 fusion.10
  934.2 4.2 fusion.12
  938.4 2.0 select_maximum_fusion
  943.6 10.1 multiply_add_fusion.1.x_ref
  953.7 105.7 %line_sum.4 = bf16[512,2048]{1,0:T(8,128)(2,1)} custom-call(f32[512,2048]{1,0:T(8,128)} %multiply_add_fusion.1.x_ref), custom_call_target="tpu_custom_call" | custom-call | tf_op jit(solution)/shard_map/line_sum/pallas_call | solution.py:206
  1059.5 4.8 pad_maximum_fusion
  1064.2 9.0 fusion.9
  1073.2 1.7 slice.77
  1076.3 1.5 slice_reduce_fusion
  1079.4 39.4 %reduce-scatter.11.cloned.1.call-done = f32[1024,256]{1,0:T(8,128)} async-done(((f32[1024,2048]{1,0:T(8,128)}), f32[1024,256]{1,0:T(8,128)}) %reduce-scatter.11.cloned.1.call-update) | async-done | bytes 1048592 | tf_op jit(solution)/shard_map/reduce_scatter | solution.py:574
  1118.8 91.1 %reduce-scatter.13.cloned.1.call-done = f32[256,1408]{1,0:T(8,128)} async-done(((f32[2048,1408]{1,0:T(8,128)}), f32[256,1408]{1,0:T(8,128)}) %reduce-scatter.13.cloned.1.call-update) | async-done | bytes 1441808 | tf_op jit(solution)/shard_map/reduce_scatter | solution.py:564
  1209.9 91.1 %reduce-scatter.15.cloned.1.call-done = f32[256,1408]{1,0:T(8,128)} async-done(((f32[2048,1408]{1,0:T(8,128)}), f32[256,1408]{1,0:T(8,128)}) %reduce-scatter.15.cloned.1.call-update) | async-done | bytes 1441808 | tf_op jit(solution)/shard_map/reduce_scatter | solution.py:565
  1300.9 90.8 %reduce-scatter.17.cloned.1.call-done = f32[1408,256]{1,0:T(8,128)} async-done(((f32[1408,2048]{1,0:T(8,128)}), f32[1408,256]{1,0:T(8,128)}) %reduce-scatter.17.cloned.1.call-update) | async-done | bytes 1441808 | tf_op jit(solution)/shard_map/reduce_scatter | solution.py:566
  (128 shorter events, 16.7 us)
Async XLA Ops:
  7.2 17.8 %copy-start = (bf16[2048,256]{1,0:T(8,128)(2,1)S(1)}, bf16[2048,256]{1,0:T(8,128)(2,1)}, u32[]{:S(2)}) copy-start(bf16[2048,256]{1,0:T(8,128)(2,1)} %param.21) | copy-start | bytes 3145732
  7.2 4.7 copy-start.32
  7.2 4.6 copy-start.28
  7.2 4.6 copy-start.29
  7.2 1066.0 %reduce-scatter.7.cloned.1.call-start = ((), (), s32[]{:S(2)}) async-start(), calls=%async_computation.6 | async-start | bytes 3833856 | tf_op jit(solution)/shard_map/reduce_scatter | solution.py:619
  7.3 36.0 %copy-start.30 = (f32[128]{0:T(128)}, f32[128]{0:T(128)S(1)}, u32[]{:S(2)}) copy-start(f32[128]{0:T(128)S(1)} %multiply_power_fusion) | copy-start | bytes 1540
  8.7 39.7 %copy-start.24 = (f32[1024]{0:T(1024)}, f32[1024]{0:T(1024)S(1)}, u32[]{:S(2)}) copy-start(f32[1024]{0:T(1024)S(1)} %convert_element_type.61) | copy-start | bytes 12292
  11.8 6.5 copy-start.22
  11.9 6.4 copy-start.19
  12.0 6.3 copy-start.21
  25.0 4.4 copy-start.8
  25.0 4.4 copy-start.15
  29.4 2.2 copy-start.33
  37.8 10.7 copy-start.26
  37.8 10.7 copy-start.13
  275.8 5.8 copy-start.1
  281.5 12.6 slice-start.2
  282.3 47.6 %copy-start.11 = (bf16[1024,2048]{1,0:T(8,128)(2,1)}, bf16[1024,2048]{1,0:T(8,128)(2,1)S(1)}, u32[]{:S(2)}) copy-start(bf16[1024,2048]{1,0:T(8,128)(2,1)S(1)} %multiply_convert_fusion) | copy-start | bytes 12582916
  282.3 11.9 slice-start.3
  294.2 8.5 copy-start.9
  318.0 11.8 copy-start.36
  351.0 9.9 copy-start.12
  351.0 9.9 copy-start.35
  383.4 212.7 %slice-start = ((s8[8388608]{0:T(1024)(128)(4,1)}), s8[4194304]{0:T(1024)(128)(4,1)S(1)}, s32[]{:S(2)}) async-start(s8[8388608]{0:T(1024)(128)(4,1)} %bitcast.40), calls=%async_computation.12 | async-start | bytes 8388608
  588.0 8.1 slice-start.1
  588.0 9.5 copy-start.4
  588.0 10.7 copy-start.10
  603.1 10.6 copy-start.7
  603.1 10.6 copy-start.34
  620.5 117.2 %copy-start.5 = (f32[1024,1024]{1,0:T(8,128)S(1)}, f32[1024,1024]{1,0:T(8,128)}, u32[]{:S(2)}) copy-start(f32[1024,1024]{1,0:T(8,128)} %copy.46) | copy-start | bytes 12582916
  620.5 117.2 %copy-start.25 = (f32[1024]{0:T(1024)S(1)}, f32[1024]{0:T(1024)}, u32[]{:S(2)}) copy-start(f32[1024]{0:T(1024)} %copy-done.24) | copy-start | bytes 12292
  620.5 117.2 %copy-start.27 = (f32[1024]{0:T(1024)S(1)}, f32[1024]{0:T(1024)}, u32[]{:S(2)}) copy-start(f32[1024]{0:T(1024)} %copy-done.26) | copy-start | bytes 12292
  743.9 153.7 %copy-start.6 = (f32[1024,1024]{1,0:T(8,128)S(1)}, f32[1024,1024]{1,0:T(8,128)}, u32[]{:S(2)}) copy-start(f32[1024,1024]{1,0:T(8,128)} %copy.46) | copy-start | bytes 12582916
  897.6 3.3 copy-start.31
  913.7 9.0 copy-start.16
  913.7 9.0 copy-start.17
  922.8 2.2 copy-start.2
  922.8 2.2 copy-start.20
  922.8 2.2 copy-start.23
  934.2 4.2 copy-start.18
  940.4 139.0 %reduce-scatter.9.cloned.1.call-start = ((), (), s32[]{:S(2)}) async-start(), calls=%async_computation.7 | async-start | bytes 4718592 | tf_op jit(solution)/shard_map/reduce_scatter | solution.py:594
  941.1 177.7 %reduce-scatter.11.cloned.1.call-start = ((), (), s32[]{:S(2)}) async-start(), calls=%async_computation.8 | async-start | bytes 9437184 | tf_op jit(solution)/shard_map/reduce_scatter | solution.py:574
  941.9 268.0 %reduce-scatter.13.cloned.1.call-start = ((), (), s32[]{:S(2)}) async-start(), calls=%async_computation.9 | async-start | bytes 12976128 | tf_op jit(solution)/shard_map/reduce_scatter | solution.py:564
  942.5 358.5 %reduce-scatter.15.cloned.1.call-start = ((), (), s32[]{:S(2)}) async-start(), calls=%async_computation.10 | async-start | bytes 12976128 | tf_op jit(solution)/shard_map/reduce_scatter | solution.py:565
  943.0 448.7 %reduce-scatter.17.cloned.1.call-start = ((), (), s32[]{:S(2)}) async-start(), calls=%async_computation.11 | async-start | bytes 12976128 | tf_op jit(solution)/shard_map/reduce_scatter | solution.py:566
  953.7 105.7 %copy-start.14 = (bf16[512,2048]{1,0:T(8,128)(2,1)S(1)}, bf16[512,2048]{1,0:T(8,128)(2,1)}, u32[]{:S(2)}) copy-start(bf16[512,2048]{1,0:T(8,128)(2,1)} %get-tuple-element.34) | copy-start | bytes 6291460
  1059.4 4.8 copy-start.3
Sparse Core Ops, SparseCore 0:
  940.5 47.7 reduce-scatter.6
  992.2 51.1 reduce-scatter.8
  1047.5 71.2 reduce-scatter.10
  1122.7 87.0 reduce-scatter.12
  1213.8 87.0 reduce-scatter.14
  1304.8 86.8 reduce-scatter.16

commit v4 on v3

--- a/solution.py
+++ b/solution.py
@@ -180,9 +180,9 @@
     line_steps(axis, n, chunks, lag, x_ref, o_ref, red, sems, lambda at: None, None, None)
 
 
-def line_low_kernel(axis, n, chunks, lag, x_ref, o_ref, red, held, *sems):
+def line_low_kernel(axis, n, chunks, lag, x_ref, base_ref, o_ref, red, held, *sems):
     def finish(at):
-        o_ref[at] = held[at].astype(o_ref.dtype)
+        o_ref[at] = (base_ref[at] + held[at]).astype(o_ref.dtype)
 
     line_steps(axis, n, chunks, lag, x_ref, held, red, sems, finish, None, None)
 
@@ -200,20 +200,214 @@
     )
 
 
-def line_sum(x, axis, n, cid, low=False):
+def line_sum(x, axis, n, cid, base=None):
+    low = base is not None
     chunks = chunk_count(x.shape[0], 32, 16 if low else 8)
     held = [pltpu.VMEM(x.shape, x.dtype)] if low else []
+    operands = (x, base) if low else (x,)
     return pl.pallas_call(
         functools.partial(line_low_kernel if low else line_kernel, axis, n, chunks, 2),
         out_shape=jax.ShapeDtypeStruct(x.shape, jnp.bfloat16 if low else x.dtype),
-        in_specs=[pl.BlockSpec(memory_space=pltpu.VMEM)],
+        in_specs=[pl.BlockSpec(memory_space=pltpu.VMEM)] * len(operands),
         out_specs=pl.BlockSpec(memory_space=pltpu.VMEM),
         scratch_shapes=[pltpu.VMEM(x.shape, x.dtype)]
         + held
         + [pltpu.SemaphoreType.DMA((2, chunks))] * 4,
         compiler_params=line_params(cid),
         name="line_sum",
-    )(x)
+    )(*operands)
+
+
+def mid_kernel(
+    axis,
+    n,
+    chunks,
+    lag,
+    x_ref,
+    mid_hbm,
+    act_hbm,
+    gate_hbm,
+    up_hbm,
+    cot_hbm,
+    down_hbm,
+    o_ref,
+    grad_gate_ref,
+    grad_up_ref,
+    grad_down_ref,
+    one_ref,
+    two_ref,
+    red,
+    mid_ref,
+    act_ref,
+    gate_ref,
+    up_ref,
+    cot_ref,
+    down_ref,
+    wide_tile,
+    row_tile,
+    load_sem,
+    wide_sem,
+    row_sem,
+    *sems,
+):
+    rows, width = cot_ref.shape
+    units = act_ref.shape[1]
+    tile = wide_tile.shape[0]
+    wide_count = width // tile
+    by_units = units % 128 == 0 and units >= tile
+    tall_count = -(-units // tile) if by_units else wide_count
+    row_blocks = rows // tile
+    loads = [
+        pltpu.make_async_copy(src, dst, load_sem.at[i])
+        for i, (src, dst) in enumerate(
+            (
+                (mid_hbm, mid_ref),
+                (gate_hbm, gate_ref),
+                (up_hbm, up_ref),
+                (act_hbm, act_ref),
+                (cot_hbm, cot_ref),
+                (down_hbm, down_ref),
+            )
+        )
+    ]
+    for load in loads:
+        load.start()
+
+    def block(t):
+        return pl.ds(pl.multiple_of(t * tile, tile), tile)
+
+    def wide_copy(dst, t):
+        return pltpu.make_async_copy(wide_tile, dst.at[block(t)], wide_sem.at[0])
+
+    def tall_at(t):
+        return pl.ds(pl.multiple_of(jnp.minimum(t * tile, units - tile), 128), tile)
+
+    def tall_copy(t):
+        if by_units:
+            return pltpu.make_async_copy(
+                row_tile.at[0:tile], grad_down_ref.at[tall_at(t)], row_sem.at[0]
+            )
+        return pltpu.make_async_copy(
+            row_tile.at[0:units, 0:tile], grad_down_ref.at[:, block(t)], row_sem.at[0]
+        )
+
+    def out_copy(dst, t):
+        return pltpu.make_async_copy(row_tile.at[0:tile], dst.at[block(t)], row_sem.at[0])
+
+    half_blocks = row_blocks // 2
+    tall_from = 2 * wide_count
+    out_from = tall_from + tall_count
+    job_count = out_from + row_blocks
+
+    def job(j, carry):
+        @pl.when(j == 0)
+        def _():
+            for load in loads:
+                load.wait()
+
+        for src, dst, start, before in (
+            (gate_ref, grad_gate_ref, 0, None),
+            (up_ref, grad_up_ref, wide_count, grad_gate_ref),
+        ):
+            t = j - start
+
+            @pl.when((t >= 0) & (t < wide_count))
+            def _():
+                value = left_dot(mid_ref[:, block(t)], src[...])
+
+                @pl.when(t > 0)
+                def _():
+                    wide_copy(dst, t - 1).wait()
+
+                if before is not None:
+
+                    @pl.when(t == 0)
+                    def _():
+                        wide_copy(before, wide_count - 1).wait()
+
+                wide_tile[...] = value
+                wide_copy(dst, t).start()
+
+        @pl.when((j >= tall_from) & (j < out_from))
+        def _():
+            t = j - tall_from
+
+            @pl.when(t > 0)
+            def _():
+                tall_copy(t - 1).wait()
+
+            if by_units:
+                row_tile[...] = left_dot(act_ref[:, tall_at(t)], cot_ref[...])
+            else:
+                row_tile[0:units, 0:tile] = left_dot(act_ref[...], cot_ref[:, block(t)])
+            tall_copy(t).start()
+
+        for side, dst in enumerate((one_ref, two_ref)):
+            t = j - out_from - side * half_blocks
+
+            @pl.when((t >= 0) & (t < half_blocks))
+            def _():
+                @pl.when(t > 0)
+                def _():
+                    out_copy(dst, t - 1).wait()
+
+                @pl.when(t == 0)
+                def _():
+                    if side == 0:
+                        tall_copy(tall_count - 1).wait()
+                    else:
+                        out_copy(one_ref, half_blocks - 1).wait()
+
+                row_tile[0:tile, :] = jnp.dot(
+                    act_ref[block(t + side * half_blocks), :],
+                    down_ref[...],
+                    preferred_element_type=jnp.float32,
+                )
+                out_copy(dst, t).start()
+
+        return carry
+
+    def bounds(s, steps):
+        late = steps - 4
+        return tuple(jnp.clip(at - 2, 0, late) * job_count // late for at in (s, s + 1))
+
+    line_steps(axis, n, chunks, lag, x_ref, o_ref, red, sems, lambda at: None, job, bounds)
+    wide_copy(grad_up_ref, wide_count - 1).wait()
+    out_copy(two_ref, half_blocks - 1).wait()
+
+
+def mid_sum(x, mid, act, d_gate, d_up, cot, w_down, axis, n, cid):
+    rows, width = x.shape
+    units = act.shape[1]
+    tile = min(256, rows // 2)
+    chunks = chunk_count(rows, 32, 8)
+    vmem = pl.BlockSpec(memory_space=pltpu.VMEM)
+    anywhere = pl.BlockSpec(memory_space=pl.ANY)
+    loaded = (mid, act, d_gate, d_up, cot, w_down)
+    tall = tile if units % 128 == 0 and units >= tile else max(tile, units)
+    return pl.pallas_call(
+        functools.partial(mid_kernel, axis, n, chunks, 2),
+        out_shape=(
+            jax.ShapeDtypeStruct(x.shape, jnp.float32),
+            jax.ShapeDtypeStruct((width, units), jnp.float32),
+            jax.ShapeDtypeStruct((width, units), jnp.float32),
+            jax.ShapeDtypeStruct((units, width), jnp.float32),
+            jax.ShapeDtypeStruct((rows // 2, width), jnp.float32),
+            jax.ShapeDtypeStruct((rows // 2, width), jnp.float32),
+        ),
+        in_specs=[vmem] + [anywhere] * 6,
+        out_specs=(vmem,) + (anywhere,) * 5,
+        scratch_shapes=[pltpu.VMEM(x.shape, jnp.float32)]
+        + [pltpu.VMEM(item.shape, item.dtype) for item in loaded]
+        + [pltpu.VMEM((tile, units), jnp.float32), pltpu.VMEM((tall, width), jnp.float32)]
+        + [pltpu.SemaphoreType.DMA((len(loaded),))]
+        + [pltpu.SemaphoreType.DMA((1,))] * 2
+        + [pltpu.SemaphoreType.DMA((2, chunks))] * 4,
+        compiler_params=pltpu.CompilerParams(
+            collective_id=cid, has_side_effects=True, vmem_limit_bytes=62 << 20
+        ),
+        name="mid_sum",
+    )(x, *loaded)
 
 
 def attend_kernel(
@@ -353,6 +547,7 @@
     seq_len,
     block,
     x_ref,
+    base_ref,
     q_ref,
     dm_ref,
     k_ref,
@@ -381,7 +576,7 @@
     sums_ref[:, rank:] = jnp.zeros((rows, 2 * head_dim), jnp.float32)
 
     def finish(at):
-        o_ref[at] = held[at].astype(o_ref.dtype)
+        o_ref[at] = (base_ref[at] + held[at]).astype(o_ref.dtype)
 
     def job(j, carry):
         head = lax.rem(j, heads)
@@ -443,7 +638,7 @@
 
 
 def attend_back(
-    x, q, dm, k, v, norm, own_ids, all_ids, cos_tab, sin_tab, q_up, axis, n, seq_len, cid
+    x, base, q, dm, k, v, norm, own_ids, all_ids, cos_tab, sin_tab, q_up, axis, n, seq_len, cid
 ):
     chunks = chunk_count(x.shape[0], 32, 16)
     block = min(256, seq_len)
@@ -455,13 +650,13 @@
             jax.ShapeDtypeStruct(q.shape, jnp.bfloat16),
             jax.ShapeDtypeStruct((k.shape[0], q_up.shape[0] + 2 * k.shape[1]), jnp.float32),
         ),
-        in_specs=[vmem] * 11,
+        in_specs=[vmem] * 12,
         out_specs=(vmem, vmem, vmem),
         scratch_shapes=[pltpu.VMEM(x.shape, x.dtype)] * 2
         + [pltpu.SemaphoreType.DMA((2, chunks))] * 4,
         compiler_params=line_params(cid),
         name="attend_back",
-    )(x, q, dm, k, v, norm, own_ids, all_ids, cos_tab, sin_tab, q_up)
+    )(x, base, q, dm, k, v, norm, own_ids, all_ids, cos_tab, sin_tab, q_up)
 
 
 def shards(
@@ -480,7 +675,7 @@
     w_down,
     d_output,
 ):
-    row_count, _ = block_input.shape
+    row_count, model_width = block_input.shape
     dp_count = lax.axis_size("dp")
     tp_count = lax.axis_size("tensor")
     tp_index = lax.axis_index("tensor")
@@ -516,6 +711,7 @@
     normed_one, scale_one = normalize(input_f32)
     normed_in = (normed_one * gain_attn).astype(jnp.bfloat16)
     q_latent = jnp.dot(normed_in, q_down, preferred_element_type=jnp.float32)
+    q_latent = lax.optimization_barrier(q_latent)
     q_unit, q_scale = normalize(q_latent)
     q_normed = (q_unit * gain_query).astype(jnp.bfloat16)
     q_raw = jnp.dot(q_normed, q_up, preferred_element_type=jnp.float32)
@@ -523,7 +719,6 @@
         jnp.dot(normed_in, k_proj, preferred_element_type=jnp.float32), cos_all, sin_all
     ).astype(jnp.bfloat16)
     val_rows = jnp.dot(normed_in, v_proj, preferred_element_type=jnp.float32).astype(jnp.bfloat16)
-    first_here = (tp_index == 0).astype(jnp.float32)
     hidden_in, queries, mixed_heads, log_norm = attend(
         q_raw,
         key_rows,
@@ -545,35 +740,36 @@
     up_pre = jnp.dot(normed_mid, w_up, preferred_element_type=jnp.float32)
     gate_sig = jax.nn.sigmoid(gate_pre)
     hidden_act = (gate_pre * gate_sig * up_pre).astype(jnp.bfloat16)
-    half_rows = row_count // 2
-    out_part_one, out_part_two = (
-        jnp.dot(hidden_act[at], w_down, preferred_element_type=jnp.float32)
-        + first_here * hidden_in[at]
-        for at in (slice(0, half_rows), slice(half_rows, row_count))
-    )
-    grad_down = left_dot(hidden_act, d_output)
     d_act = right_dot(d_output, w_down)
     d_gate = (d_act * up_pre * gate_sig * (1.0 + gate_pre * (1.0 - gate_sig))).astype(jnp.bfloat16)
     d_up = (d_act * gate_pre * gate_sig).astype(jnp.bfloat16)
-    grad_gate = left_dot(normed_mid, d_gate)
-    grad_up = left_dot(normed_mid, d_up)
     d_mid_part = right_dot(d_gate, w_gate) + right_dot(d_up, w_up)
-    d_mid_part, grad_down, grad_gate, grad_up = lax.optimization_barrier(
-        (d_mid_part, grad_down, grad_gate, grad_up)
+    d_mid, grad_gate, grad_up, grad_down, out_part_one, out_part_two = mid_sum(
+        d_mid_part,
+        normed_mid,
+        hidden_act,
+        d_gate,
+        d_up,
+        d_output,
+        w_down,
+        "tensor",
+        tp_count,
+        1,
     )
     grad_gate = lax.psum_scatter(grad_gate, "dp", scatter_dimension=0, tiled=True)
     grad_up = lax.psum_scatter(grad_up, "dp", scatter_dimension=0, tiled=True)
     grad_down = lax.psum_scatter(grad_down, "dp", scatter_dimension=1, tiled=True)
-    d_mid = line_sum(d_mid_part, "tensor", tp_count, 1)
     grad_gain_mlp = jnp.sum(d_mid * normed_two, axis=0)
     d_hidden = cotan_f32 + norm_back(d_mid * gain_mlp, normed_two, scale_two)
     d_hidden_low = d_hidden.astype(jnp.bfloat16)
     grad_out = left_dot(mixed_heads, d_hidden_low)
     d_mixed = right_dot(d_hidden_low, out_proj).astype(jnp.bfloat16)
+    half_rows = row_count // 2
     out_part_one, grad_out = lax.optimization_barrier((out_part_one, grad_out))
     grad_out = lax.psum_scatter(grad_out, "dp", scatter_dimension=1, tiled=True)
     output_one, d_q_raw, query_key_val = attend_back(
         out_part_one,
+        hidden_in[:half_rows],
         queries,
         d_mixed,
         key_rows,
@@ -606,7 +802,11 @@
     grad_input = (d_hidden + norm_back(d_normed_in * gain_attn, normed_one, scale_one)).astype(
         jnp.bfloat16
     )
-    own_in = own_part(normed_in, 1).reshape(row_count, -1)
+    own_width = model_width // (dp_count * tp_count)
+    own_at = jnp.arange(model_width // tp_count)
+    own_at = (own_at // own_width * tp_count + tp_index) * own_width + own_at % own_width
+    pick = (jnp.arange(model_width)[:, None] == own_at[None, :]).astype(jnp.bfloat16)
+    own_in = jnp.dot(normed_in, pick, preferred_element_type=jnp.float32).astype(jnp.bfloat16)
     own_grads = left_dot(own_in, jnp.concatenate([d_latent, d_key_low, d_val_low], axis=1))
     own_rows = own_grads.shape[0]
     gain_one = own_part(grad_gain_attn, 0).reshape(own_rows, 1)
@@ -617,7 +817,7 @@
     gain_cols = jnp.concatenate([gain_one, gain_two, gain_mid], axis=1)
     own_grads = jnp.concatenate([own_grads, jnp.pad(gain_cols, ((0, 0), (0, 125)))], axis=1)
     own_sum = lax.psum_scatter(own_grads, "dp", scatter_dimension=0, tiled=True)
-    output_two = line_sum(out_part_two, "tensor", tp_count, 4, low=True)
+    output_two = line_sum(out_part_two, "tensor", tp_count, 4, base=hidden_in[half_rows:])
     block_output = jnp.concatenate([output_one, output_two], axis=0)
     rank = q_down.shape[1]
     grad_qd = own_sum[:, :rank]

time: 1400 us -> 1350 us (0.964)
  matrix products: 177 us -> 123 us
    pallas_call x0 -> x1, Pallas kernels: none -> 206 us  [mid_sum(): pl.pallas_call(functools.partial(mid_kernel, axis, n, chunks, 2), out_sha...]
    pallas_call x3 -> x2, Pallas kernels: 464 us -> 261 us  [line_sum(): pl.pallas_call(functools.partial(line_low_kernel if low else line_kernel,...]
    dot_general x6 -> x3, matrix products: 48 us -> 21.2 us  [left_dot(): lax.dot_general(left, right, (((0,), (0,)), ((), ())), preferred_element_...]
    dot_general x2 -> x0, matrix products: 20 us -> none  [shards(): jnp.dot(hidden_act[at], w_down, preferred_element_type=jnp.float32)]
where the time goes in v4:
time: 1350 us; the launch traced here: 1340 us
  Pallas kernels  805 us (60%)
  waiting for transfers between devices  321 us (24%)
  matrix products  123 us (9%)
  other arithmetic  53.4 us (4%)
  local copies, waits for them, and re-layouts  20.4 us (2%)
  between operations  15.1 us (1%)
    pallas_call x2, Pallas kernels, line_sum(): pl.pallas_call(functools.partial(line_low_kernel if low else line_kernel,...  261 us
    pallas_call x1, Pallas kernels, attend(): pl.pallas_call(functools.partial(attend_kernel, axis, n, chunks, 2, seq_l...  220 us
    pallas_call x1, Pallas kernels, mid_sum(): pl.pallas_call(functools.partial(mid_kernel, axis, n, chunks, 2), out_sha...  206 us
    pallas_call x1, Pallas kernels, attend_back(): pl.pallas_call(functools.partial(attend_back_kernel, axis, n, chunks, 2,...  118 us
    reduce_scatter x1, waiting for transfers between devices, shards(): lax.psum_scatter(grad_gate, 'dp', scatter_dimension=0, tiled=True)  91.1 us
    reduce_scatter x1, waiting for transfers between devices, shards(): grad_up = lax.psum_scatter(grad_up, 'dp', scatter_dimension=0, tiled=True)  91.1 us
    reduce_scatter x1, waiting for transfers between devices, shards(): lax.psum_scatter(grad_down, 'dp', scatter_dimension=1, tiled=True)  90.8 us
    dot_general x7, matrix products, right_dot(): lax.dot_general(left, right, (((1,), (1,)), ((), ())), preferred_element_...  59.2 us
  transfers between devices with their start and end apart: 6, of which 4 were waited for; matrix products, arithmetic and copies ran while one was open for 2% of the time, Pallas kernels for 8%

profile of v4, /device:TPU:0, one launch (start us, length us, event | category | flops | bytes accessed | tf_op | source)
XLA Modules:
  0.0 1339.3 jit_solution(8110570770588323421)
XLA Ops:
  8.1 3.4 fusion.11
  11.5 6.4 fusion.56
  18.3 1.6 copy-done.17
  19.9 1.3 fusion.54
  21.3 2.1 convolution_convert_fusion.v_ref
  24.6 3.0 subtract_convert_fusion.1
  27.6 0.8 pad_maximum_fusion.1.k_ref
  28.4 6.0 fusion.51.raw_ref
  34.5 220.4 %attend.1 = (f32[1024,2048]{1,0:T(8,128)}, bf16[1024,1024]{1,0:T(8,128)(2,1)}, bf16[1024,1024]{1,0:T(8,128)(2,1)}, f32[4,1024,1]{2,1,0:T(8,128)}) custom-call(f32[1024,1024]{1,0:T(8,128)} %fusion.51.raw_ref, bf16[1024,256]{1,0:T(8,128)(2,1)} %pad_maximum_fusion.1.k_ref, bf16[1024,256]{1,0:T(8,128)(2,1)} %convolution_convert_fusion.v_ref, ...), custom_call_target="tpu_custom_call" | custom-call | tf_op jit(solution)/shard_map/attend/pallas_call | solution.py:523
  254.9 4.1 multiply_reduce_fusion.2
  259.0 1.6 copy-done.1
  260.6 3.8 fusion.60
  265.3 12.3 fusion.64
  277.6 8.6 fusion.63
  286.2 14.7 %multiply_convert_fusion.1 = (bf16[1024,1408]{1,0:T(8,128)(2,1)}, bf16[1024,1408]{1,0:T(8,128)(2,1)S(1)}, bf16[1024,1408]{1,0:T(8,128)(2,1)S(1)}) fusion(f32[1024,1408]{1,0:T(8,128)} %fusion.64, f32[1024,1408]{1,0:T(8,128)} %fusion.63, bf16[1024,2048]{1,0:T(8,128)(2,1)S(1)} %multiply_convert_fusion.mid_hbm, bf16[2048,1408]{1,0:T(8,128)(2,1)} %param.25), kind=kOutput, calls=%fused_computation.20 | convolution fusion | flops 5928648704 | bytes 30146560 | tf_op jit(solution)/shard_map/dot_general | solution.py:740
  300.9 9.0 fusion.65
  310.0 12.6 convolution_add_fusion.x_ref
  322.6 205.6 %mid_sum.1 = (f32[1024,2048]{1,0:T(8,128)}, f32[2048,1408]{1,0:T(8,128)}, f32[2048,1408]{1,0:T(8,128)}, f32[1408,2048]{1,0:T(8,128)}, f32[512,2048]{1,0:T(8,128)}, /*index=5*/f32[512,2048]{1,0:T(8,128)}) custom-call(f32[1024,2048]{1,0:T(8,128)} %convolution_add_fusion.x_ref, bf16[1024,2048]{1,0:T(8,128)(2,1)} %copy-done.13, ...), custom_call_target="tpu_custom_call" | custom-call | tf_op jit(solution)/shard_map/mid_sum/pallas_call | solution.py:388
  528.3 7.6 multiply_reduce_fusion
  536.5 2.4 copy-done.10
  538.9 3.8 multiply_add_fusion
  542.8 11.0 fusion.26.dm_ref
  553.8 7.1 fusion.24
  560.9 118.4 %attend_back.1 = (bf16[512,2048]{1,0:T(8,128)(2,1)}, bf16[1024,1024]{1,0:T(8,128)(2,1)}, f32[1024,1536]{1,0:T(8,128)}) custom-call(f32[512,2048]{1,0:T(8,128)} %get-tuple-element.34.x_ref, f32[512,2048]{1,0:T(8,128)} %get-tuple-element.58.base_ref, bf16[1024,1024]{1,0:T(8,128)(2,1)} %get-tuple-element.35.q_ref, bf16[1024,1024]{1,0:T(8,128)(2,1)} %fusion.26.dm_ref, ...), custom_call_target="tpu_custom_call" | custom-call | tf_op jit(solution)/shard_map/attend_back/pallas_call | solution.py:646
  679.3 6.1 fusion.50
  685.3 153.8 %line_sum.3 = f32[1024,1536]{1,0:T(8,128)} custom-call(f32[1024,1536]{1,0:T(8,128)} %get-tuple-element.41.x_ref), custom_call_target="tpu_custom_call" | custom-call | tf_op jit(solution)/shard_map/line_sum/pallas_call | solution.py:208
  839.1 3.4 multiply_reduce_fusion.3
  843.2 2.9 add_convert_fusion
  846.0 0.9 slice.87
  846.9 1.2 multiply_convert_fusion.4
  848.1 0.9 copy-done.26
  849.1 7.0 fusion.66
  856.4 2.7 fusion.30
  859.2 8.2 fusion.10
  867.6 0.9 copy.45
  868.5 8.1 fusion.13
  876.5 3.9 select_maximum_fusion
  883.7 107.1 %line_sum.2 = bf16[512,2048]{1,0:T(8,128)(2,1)} custom-call(f32[512,2048]{1,0:T(8,128)} %get-tuple-element.38.x_ref, f32[512,2048]{1,0:T(8,128)} %get-tuple-element.59.base_ref), custom_call_target="tpu_custom_call" | custom-call | tf_op jit(solution)/shard_map/line_sum/pallas_call | solution.py:208
  990.9 4.3 pad_maximum_fusion
  995.2 11.8 fusion.9
  1007.0 1.7 slice.67
  1008.7 1.4 slice_reduce_fusion.2
  1010.1 1.5 slice_reduce_fusion
  1011.7 1.5 fusion.61
  1013.2 45.8 %reduce-scatter.11.cloned.1.call-done = f32[1024,256]{1,0:T(8,128)} async-done(((f32[1024,2048]{1,0:T(8,128)}), f32[1024,256]{1,0:T(8,128)}) %reduce-scatter.11.cloned.1.call-update) | async-done | bytes 1048592 | tf_op jit(solution)/shard_map/reduce_scatter | solution.py:769
  1059.0 91.1 %reduce-scatter.13.cloned.1.call-done = f32[256,1408]{1,0:T(8,128)} async-done(((f32[2048,1408]{1,0:T(8,128)}), f32[256,1408]{1,0:T(8,128)}) %reduce-scatter.13.cloned.1.call-update) | async-done | bytes 1441808 | tf_op jit(solution)/shard_map/reduce_scatter | solution.py:759
  1150.1 91.1 %reduce-scatter.15.cloned.1.call-done = f32[256,1408]{1,0:T(8,128)} async-done(((f32[2048,1408]{1,0:T(8,128)}), f32[256,1408]{1,0:T(8,128)}) %reduce-scatter.15.cloned.1.call-update) | async-done | bytes 1441808 | tf_op jit(solution)/shard_map/reduce_scatter | solution.py:760
  1241.2 90.8 %reduce-scatter.17.cloned.1.call-done = f32[1408,256]{1,0:T(8,128)} async-done(((f32[1408,2048]{1,0:T(8,128)}), f32[1408,256]{1,0:T(8,128)}) %reduce-scatter.17.cloned.1.call-update) | async-done | bytes 1441808 | tf_op jit(solution)/shard_map/reduce_scatter | solution.py:761
  (109 shorter events, 8.3 us)
Async XLA Ops:
  7.2 14.1 %copy-start = (bf16[2048,256]{1,0:T(8,128)(2,1)S(1)}, bf16[2048,256]{1,0:T(8,128)(2,1)}, u32[]{:S(2)}) copy-start(bf16[2048,256]{1,0:T(8,128)(2,1)} %param.21) | copy-start | bytes 3145732
  7.2 999.8 %reduce-scatter.7.cloned.1.call-start = ((), (), s32[]{:S(2)}) async-start(), calls=%async_computation.6 | async-start | bytes 3833856 | tf_op jit(solution)/shard_map/reduce_scatter | solution.py:819
  7.2 4.2 copy-start.2
  8.1 13.1 copy-start.18
  11.5 9.8 copy-start.21
  11.5 6.4 copy-start.24
  17.9 3.4 copy-start.6
  17.9 2.0 copy-start.17
  21.3 2.1 copy-start.25
  23.5 11.0 copy-start.20
  23.7 4.7 copy-start.7
  254.9 5.8 copy-start.1
  260.6 3.8 copy-start.23
  264.5 13.1 slice-start.2
  265.3 20.9 %copy-start.13 = (bf16[1024,2048]{1,0:T(8,128)(2,1)}, bf16[1024,2048]{1,0:T(8,128)(2,1)S(1)}, u32[]{:S(2)}) copy-start(bf16[1024,2048]{1,0:T(8,128)(2,1)S(1)} %multiply_convert_fusion.mid_hbm) | copy-start | bytes 12582916
  265.3 12.3 copy-start.12
  265.3 12.3 slice-start.3
  277.6 23.3 %slice-start.4 = ((s8[5767168]{0:T(1024)(128)(4,1)}), s8[1572864]{0:T(1024)(128)(4,1)S(1)}, s32[]{:S(2)}) async-start(s8[5767168]{0:T(1024)(128)(4,1)} %bitcast.35), calls=%async_computation.16 | async-start | bytes 3145728
  286.2 14.7 %slice-start.5 = ((s8[5767168]{0:T(1024)(128)(4,1)}), s8[4194304]{0:T(1024)(128)(4,1)S(1)}, s32[]{:S(2)}) async-start(s8[5767168]{0:T(1024)(128)(4,1)} %bitcast.35), calls=%async_computation.17 | async-start | bytes 8388608
  300.9 9.1 copy-start.14
  300.9 9.1 copy-start.15
  528.2 7.7 slice-start
  528.2 8.3 slice-start.1
  528.2 10.7 copy-start.10
  542.8 11.0 copy-start.11
  542.8 11.0 copy-start.27
  560.9 118.4 %copy-start.8 = (f32[1024,1024]{1,0:T(8,128)S(1)}, f32[1024,1024]{1,0:T(8,128)}, u32[]{:S(2)}) copy-start(f32[1024,1024]{1,0:T(8,128)} %copy-done.6) | copy-start | bytes 12582916
  685.3 153.8 %copy-start.9 = (f32[1024,1024]{1,0:T(8,128)S(1)}, f32[1024,1024]{1,0:T(8,128)}, u32[]{:S(2)}) copy-start(f32[1024,1024]{1,0:T(8,128)} %copy-done.6) | copy-start | bytes 12582916
  839.1 4.0 copy-start.5
  846.9 2.2 copy-start.26
  856.4 2.8 copy-start.3
  856.4 2.8 copy-start.19
  856.4 2.8 copy-start.22
  880.5 132.7 %reduce-scatter.9.cloned.1.call-start = ((), (), s32[]{:S(2)}) async-start(), calls=%async_computation.7 | async-start | bytes 4718592 | tf_op jit(solution)/shard_map/reduce_scatter | solution.py:790
  881.2 177.7 %reduce-scatter.11.cloned.1.call-start = ((), (), s32[]{:S(2)}) async-start(), calls=%async_computation.8 | async-start | bytes 9437184 | tf_op jit(solution)/shard_map/reduce_scatter | solution.py:769
  882.0 268.1 %reduce-scatter.13.cloned.1.call-start = ((), (), s32[]{:S(2)}) async-start(), calls=%async_computation.9 | async-start | bytes 12976128 | tf_op jit(solution)/shard_map/reduce_scatter | solution.py:759
  882.6 358.6 %reduce-scatter.15.cloned.1.call-start = ((), (), s32[]{:S(2)}) async-start(), calls=%async_computation.10 | async-start | bytes 12976128 | tf_op jit(solution)/shard_map/reduce_scatter | solution.py:760
  883.1 448.8 %reduce-scatter.17.cloned.1.call-start = ((), (), s32[]{:S(2)}) async-start(), calls=%async_computation.11 | async-start | bytes 12976128 | tf_op jit(solution)/shard_map/reduce_scatter | solution.py:761
  883.7 107.1 %copy-start.16 = (bf16[512,2048]{1,0:T(8,128)(2,1)S(1)}, bf16[512,2048]{1,0:T(8,128)(2,1)}, u32[]{:S(2)}) copy-start(bf16[512,2048]{1,0:T(8,128)(2,1)} %get-tuple-element.37) | copy-start | bytes 6291460
  990.9 4.4 copy-start.4
Sparse Core Ops, SparseCore 0:
  880.6 47.8 reduce-scatter.6
  932.4 51.1 reduce-scatter.8
  987.6 71.2 reduce-scatter.10
  1062.9 87.1 reduce-scatter.12
  1154.0 87.1 reduce-scatter.14
  1245.1 86.8 reduce-scatter.16

commit v5 on v4

--- a/solution.py
+++ b/solution.py
@@ -53,20 +53,7 @@
     )
 
 
-def unrotate(grads, cos_tab, sin_tab):
-    half = grads.shape[-1] // 2
-    first_half = grads[..., :half]
-    second_half = grads[..., half:]
-    return jnp.concatenate(
-        [
-            first_half * cos_tab + second_half * sin_tab,
-            second_half * cos_tab - first_half * sin_tab,
-        ],
-        axis=-1,
-    )
-
-
-def line_steps(axis, n, chunks, lag, x_ref, held, red, sems, finish, job, job_range):
+def line_steps(axis, n, chunks, lag, x_ref, held, red, sems, finish, after_step):
     me = lax.axis_index(axis)
     rows = x_ref.shape[0] // (2 * chunks)
     s_red, r_red, s_fin, r_fin = sems
@@ -153,8 +140,8 @@
             def _():
                 finish(at(half, c))
 
-        if job is not None:
-            lax.fori_loop(*job_range(s, steps), job, 0)
+        if after_step is not None:
+            after_step(s, steps)
         return carry
 
     lax.fori_loop(0, steps, step, 0)
@@ -177,14 +164,14 @@
 
 
 def line_kernel(axis, n, chunks, lag, x_ref, o_ref, red, *sems):
-    line_steps(axis, n, chunks, lag, x_ref, o_ref, red, sems, lambda at: None, None, None)
+    line_steps(axis, n, chunks, lag, x_ref, o_ref, red, sems, lambda at: None, None)
 
 
 def line_low_kernel(axis, n, chunks, lag, x_ref, base_ref, o_ref, red, held, *sems):
     def finish(at):
         o_ref[at] = (base_ref[at] + held[at]).astype(o_ref.dtype)
 
-    line_steps(axis, n, chunks, lag, x_ref, held, red, sems, finish, None, None)
+    line_steps(axis, n, chunks, lag, x_ref, held, red, sems, finish, None)
 
 
 def chunk_count(rows, most, tile):
@@ -231,8 +218,7 @@
     cot_hbm,
     down_hbm,
     o_ref,
-    grad_gate_ref,
-    grad_up_ref,
+    grad_wide_ref,
     grad_down_ref,
     one_ref,
     two_ref,
@@ -252,10 +238,11 @@
 ):
     rows, width = cot_ref.shape
     units = act_ref.shape[1]
-    tile = wide_tile.shape[0]
-    wide_count = width // tile
+    wide = wide_tile.shape[0]
+    wide_count = width // wide
+    tile = min(256, rows // 2)
     by_units = units % 128 == 0 and units >= tile
-    tall_count = -(-units // tile) if by_units else wide_count
+    tall_count = -(-units // tile) if by_units else width // tile
     row_blocks = rows // tile
     loads = [
         pltpu.make_async_copy(src, dst, load_sem.at[i])
@@ -276,8 +263,9 @@
     def block(t):
         return pl.ds(pl.multiple_of(t * tile, tile), tile)
 
-    def wide_copy(dst, t):
-        return pltpu.make_async_copy(wide_tile, dst.at[block(t)], wide_sem.at[0])
+    def wide_copy(which, t):
+        to = pl.ds(pl.multiple_of((2 * t + which) * wide, wide), wide)
+        return pltpu.make_async_copy(wide_tile, grad_wide_ref.at[to], wide_sem.at[0])
 
     def tall_at(t):
         return pl.ds(pl.multiple_of(jnp.minimum(t * tile, units - tile), 128), tile)
@@ -305,28 +293,23 @@
             for load in loads:
                 load.wait()
 
-        for src, dst, start, before in (
-            (gate_ref, grad_gate_ref, 0, None),
-            (up_ref, grad_up_ref, wide_count, grad_gate_ref),
-        ):
-            t = j - start
-
-            @pl.when((t >= 0) & (t < wide_count))
-            def _():
-                value = left_dot(mid_ref[:, block(t)], src[...])
-
-                @pl.when(t > 0)
-                def _():
-                    wide_copy(dst, t - 1).wait()
-
-                if before is not None:
-
-                    @pl.when(t == 0)
+        for which, src in enumerate((gate_ref, up_ref)):
+            t = lax.div(j, 2)
+
+            @pl.when((j < tall_from) & (lax.rem(j, 2) == which))
+            def _():
+                cols = pl.ds(pl.multiple_of(t * wide, wide), wide)
+                value = left_dot(mid_ref[:, cols], src[...])
+                if which:
+                    wide_copy(0, t).wait()
+                else:
+
+                    @pl.when(t > 0)
                     def _():
-                        wide_copy(before, wide_count - 1).wait()
+                        wide_copy(1, t - 1).wait()
 
                 wide_tile[...] = value
-                wide_copy(dst, t).start()
+                wide_copy(which, t).start()
 
         @pl.when((j >= tall_from) & (j < out_from))
         def _():
@@ -367,16 +350,17 @@
 
         return carry
 
-    def bounds(s, steps):
+    def after_step(s, steps):
         late = steps - 4
-        return tuple(jnp.clip(at - 2, 0, late) * job_count // late for at in (s, s + 1))
-
-    line_steps(axis, n, chunks, lag, x_ref, o_ref, red, sems, lambda at: None, job, bounds)
-    wide_copy(grad_up_ref, wide_count - 1).wait()
+        bounds = tuple(jnp.clip(at - 2, 0, late) * job_count // late for at in (s, s + 1))
+        lax.fori_loop(*bounds, job, 0)
+
+    line_steps(axis, n, chunks, lag, x_ref, o_ref, red, sems, lambda at: None, after_step)
+    wide_copy(1, wide_count - 1).wait()
     out_copy(two_ref, half_blocks - 1).wait()
 
 
-def mid_sum(x, mid, act, d_gate, d_up, cot, w_down, axis, n, cid):
+def mid_sum(x, mid, act, d_gate, d_up, cot, w_down, axis, n, parts, cid):
     rows, width = x.shape
     units = act.shape[1]
     tile = min(256, rows // 2)
@@ -389,17 +373,16 @@
         functools.partial(mid_kernel, axis, n, chunks, 2),
         out_shape=(
             jax.ShapeDtypeStruct(x.shape, jnp.float32),
-            jax.ShapeDtypeStruct((width, units), jnp.float32),
-            jax.ShapeDtypeStruct((width, units), jnp.float32),
+            jax.ShapeDtypeStruct((2 * width, units), jnp.float32),
             jax.ShapeDtypeStruct((units, width), jnp.float32),
             jax.ShapeDtypeStruct((rows // 2, width), jnp.float32),
             jax.ShapeDtypeStruct((rows // 2, width), jnp.float32),
         ),
         in_specs=[vmem] + [anywhere] * 6,
-        out_specs=(vmem,) + (anywhere,) * 5,
+        out_specs=(vmem,) + (anywhere,) * 4,
         scratch_shapes=[pltpu.VMEM(x.shape, jnp.float32)]
         + [pltpu.VMEM(item.shape, item.dtype) for item in loaded]
-        + [pltpu.VMEM((tile, units), jnp.float32), pltpu.VMEM((tall, width), jnp.float32)]
+        + [pltpu.VMEM((width // parts, units), jnp.float32), pltpu.VMEM((tall, width), jnp.float32)]
         + [pltpu.SemaphoreType.DMA((len(loaded),))]
         + [pltpu.SemaphoreType.DMA((1,))] * 2
         + [pltpu.SemaphoreType.DMA((2, chunks))] * 4,
@@ -408,6 +391,197 @@
         ),
         name="mid_sum",
     )(x, *loaded)
+
+
+def tail_kernel(
+    axis,
+    n,
+    chunks,
+    lag,
+    block,
+    x_ref,
+    scale_one_ref,
+    scale_mid_ref,
+    cos_ref,
+    sin_ref,
+    gain_one_ref,
+    gain_mid_ref,
+    unit_hbm,
+    down_hbm,
+    key_hbm,
+    val_hbm,
+    own_hbm,
+    input_hbm,
+    hidden_hbm,
+    grad_hbm,
+    own_ref,
+    acc_one_ref,
+    acc_mid_ref,
+    held,
+    red,
+    unit_ref,
+    down_ref,
+    key_ref,
+    val_ref,
+    own_in_ref,
+    input_ref,
+    hidden_ref,
+    grad_ref,
+    low_ref,
+    load_sem,
+    block_sem,
+    store_sem,
+    *sems,
+):
+    me = lax.axis_index(axis)
+    rows = x_ref.shape[0]
+    rank = unit_ref.shape[1]
+    head_dim = key_ref.shape[1]
+    half_dim = head_dim // 2
+    pairs = rows // (2 * block)
+    per = chunks // pairs
+    loads = [
+        pltpu.make_async_copy(src, dst, load_sem.at[i])
+        for i, (src, dst) in enumerate(
+            (
+                (unit_hbm, unit_ref),
+                (down_hbm, down_ref),
+                (key_hbm, key_ref),
+                (val_hbm, val_ref),
+                (own_hbm, own_in_ref),
+            )
+        )
+    ]
+    for load in loads:
+        load.start()
+    acc_one_ref[...] = jnp.zeros_like(acc_one_ref)
+    acc_mid_ref[...] = jnp.zeros_like(acc_mid_ref)
+    own_ref[...] = jnp.zeros_like(own_ref)
+
+    def fold(values):
+        return jnp.sum(values.reshape(values.shape[0] // 8, 8, values.shape[1]), axis=0)
+
+    def store(own):
+        return pltpu.make_async_copy(grad_ref, grad_hbm.at[own], store_sem.at[0])
+
+    def consume(row_block):
+        own = pl.ds(pl.multiple_of(row_block * block, block), block)
+        take_input = pltpu.make_async_copy(input_hbm.at[own], input_ref, block_sem.at[0])
+        take_hidden = pltpu.make_async_copy(hidden_hbm.at[own], hidden_ref, block_sem.at[1])
+        take_input.start()
+        take_hidden.start()
+        d_bq = held[own, 0:rank]
+        unit = unit_ref[own, :]
+        acc_mid_ref[...] += fold(d_bq * unit)
+        eq = d_bq * gain_mid_ref[...]
+        mean_mid = jnp.mean(eq * unit, axis=1, keepdims=True)
+        d_latent = (scale_mid_ref[own, :] * (eq - unit * mean_mid)).astype(jnp.bfloat16)
+        first = held[own, rank : rank + half_dim]
+        second = held[own, rank + half_dim : rank + head_dim]
+        cos_tab = cos_ref[own, :]
+        sin_tab = sin_ref[own, :]
+        low_ref[own, 0:rank] = d_latent
+        low_ref[own, rank : rank + half_dim] = (first * cos_tab + second * sin_tab).astype(
+            jnp.bfloat16
+        )
+        low_ref[own, rank + half_dim : rank + head_dim] = (
+            second * cos_tab - first * sin_tab
+        ).astype(jnp.bfloat16)
+        low_ref[own, rank + head_dim :] = held[own, rank + head_dim :].astype(jnp.bfloat16)
+        d_in = (
+            right_dot(d_latent, down_ref[...])
+            + right_dot(low_ref[own, rank : rank + head_dim], key_ref[...])
+            + right_dot(low_ref[own, rank + head_dim :], val_ref[...])
+        )
+        take_input.wait()
+        take_hidden.wait()
+        scale_one = scale_one_ref[own, :]
+        normed = input_ref[...].astype(jnp.float32) * scale_one
+        acc_one_ref[...] += fold(d_in * normed)
+        e_in = d_in * gain_one_ref[...]
+        mean_one = jnp.mean(e_in * normed, axis=1, keepdims=True)
+        grad_ref[...] = (hidden_ref[...] + scale_one * (e_in - normed * mean_one)).astype(
+            grad_ref.dtype
+        )
+        store(own).start()
+        store(own).wait()
+
+    def after_step(s, steps):
+        @pl.when(s == lag)
+        def _():
+            for load in loads:
+                load.wait()
+
+        for half in (0, 1):
+            back = me if half == 0 else (n - 1 - me)
+            c = s - lag * (n - 1) - lag * back
+
+            @pl.when((c >= 0) & (c < chunks) & (lax.rem(c + 1, per) == 0))
+            def _():
+                consume(half * pairs + lax.div(c, per))
+
+    line_steps(axis, n, chunks, lag, x_ref, held, red, sems, lambda at: None, after_step)
+    grads = left_dot(own_in_ref[...], low_ref[...])
+    parts, _, _ = own_ref.shape
+    kept = grads.shape[0] // parts
+    for part in range(parts):
+        own_ref[part, 0:kept, :] = grads[part * kept : (part + 1) * kept]
+
+
+def tail_sum(
+    x,
+    scale_one,
+    scale_mid,
+    cos_tab,
+    sin_tab,
+    gain_one,
+    gain_mid,
+    unit,
+    q_down,
+    k_proj,
+    v_proj,
+    own_in,
+    block_input,
+    d_hidden,
+    axis,
+    n,
+    parts,
+    cid,
+):
+    rows, width = block_input.shape
+    block = min(128, rows // 2)
+    chunks = chunk_count(rows, 32, 8)
+    kept = -(-(own_in.shape[1] // parts) // 8) * 8 + 8
+    vmem = pl.BlockSpec(memory_space=pltpu.VMEM)
+    anywhere = pl.BlockSpec(memory_space=pl.ANY)
+    loaded = (unit, q_down, k_proj, v_proj, own_in)
+    return pl.pallas_call(
+        functools.partial(tail_kernel, axis, n, chunks, 2, block),
+        out_shape=(
+            jax.ShapeDtypeStruct((rows, width), jnp.bfloat16),
+            jax.ShapeDtypeStruct((parts, kept, x.shape[1]), jnp.float32),
+            jax.ShapeDtypeStruct((8, width), jnp.float32),
+            jax.ShapeDtypeStruct((8, unit.shape[1]), jnp.float32),
+        ),
+        in_specs=[vmem] * 7 + [anywhere] * 7,
+        out_specs=(anywhere, vmem, vmem, vmem),
+        scratch_shapes=[pltpu.VMEM(x.shape, jnp.float32)] * 2
+        + [pltpu.VMEM(item.shape, item.dtype) for item in loaded]
+        + [
+            pltpu.VMEM((block, width), jnp.bfloat16),
+            pltpu.VMEM((block, width), jnp.float32),
+            pltpu.VMEM((block, width), jnp.bfloat16),
+            pltpu.VMEM(x.shape, jnp.bfloat16),
+            pltpu.SemaphoreType.DMA((len(loaded),)),
+            pltpu.SemaphoreType.DMA((2,)),
+            pltpu.SemaphoreType.DMA((1,)),
+        ]
+        + [pltpu.SemaphoreType.DMA((2, chunks))] * 4,
+        compiler_params=pltpu.CompilerParams(
+            collective_id=cid, has_side_effects=True, vmem_limit_bytes=60 << 20
+        ),
+        name="tail_sum",
+    )(x, scale_one, scale_mid, cos_tab, sin_tab, gain_one, gain_mid, *loaded, block_input, d_hidden)
 
 
 def attend_kernel(
@@ -500,13 +674,14 @@
     lax.fori_loop(0, pair_jobs, job, 0)
     pair_steps = chunks // pairs
 
-    def job_range(s, steps):
-        return tuple(
+    def after_step(s, steps):
+        bounds = tuple(
             jnp.minimum((pair_steps + at) * pair_jobs // pair_steps, pairs * pair_jobs)
             for at in (s, s + 1)
         )
-
-    line_steps(axis, n, chunks, lag, part, o_ref, red, sems, lambda at: None, job, job_range)
+        lax.fori_loop(*bounds, job, 0)
+
+    line_steps(axis, n, chunks, lag, part, o_ref, red, sems, lambda at: None, after_step)
 
 
 def reach_list(seq_len, block):
@@ -631,10 +806,10 @@
 
     job_count = heads * (rows // block)
 
-    def job_range(s, steps):
-        return s * job_count // steps, (s + 1) * job_count // steps
-
-    line_steps(axis, n, chunks, lag, x_ref, held, red, sems, finish, job, job_range)
+    def after_step(s, steps):
+        lax.fori_loop(s * job_count // steps, (s + 1) * job_count // steps, job, 0)
+
+    line_steps(axis, n, chunks, lag, x_ref, held, red, sems, finish, after_step)
 
 
 def attend_back(
@@ -744,7 +919,7 @@
     d_gate = (d_act * up_pre * gate_sig * (1.0 + gate_pre * (1.0 - gate_sig))).astype(jnp.bfloat16)
     d_up = (d_act * gate_pre * gate_sig).astype(jnp.bfloat16)
     d_mid_part = right_dot(d_gate, w_gate) + right_dot(d_up, w_up)
-    d_mid, grad_gate, grad_up, grad_down, out_part_one, out_part_two = mid_sum(
+    d_mid, grad_wide, grad_down, out_part_one, out_part_two = mid_sum(
         d_mid_part,
         normed_mid,
         hidden_act,
@@ -754,10 +929,12 @@
         w_down,
         "tensor",
         tp_count,
+        dp_count,
         1,
     )
-    grad_gate = lax.psum_scatter(grad_gate, "dp", scatter_dimension=0, tiled=True)
-    grad_up = lax.psum_scatter(grad_up, "dp", scatter_dimension=0, tiled=True)
+    grad_wide = lax.psum_scatter(grad_wide, "dp", scatter_dimension=0, tiled=True)
+    grad_gate = grad_wide[: grad_wide.shape[0] // 2]
+    grad_up = grad_wide[grad_wide.shape[0] // 2 :]
     grad_down = lax.psum_scatter(grad_down, "dp", scatter_dimension=1, tiled=True)
     grad_gain_mlp = jnp.sum(d_mid * normed_two, axis=0)
     d_hidden = cotan_f32 + norm_back(d_mid * gain_mlp, normed_two, scale_two)
@@ -788,45 +965,54 @@
     grad_query_up = left_dot(q_normed, d_q_raw)
     query_key_val, grad_query_up = lax.optimization_barrier((query_key_val, grad_query_up))
     grad_query_up = lax.psum_scatter(grad_query_up, "dp", scatter_dimension=0, tiled=True)
-    query_key_val = line_sum(query_key_val, "tensor", tp_count, 2)
-    d_q_normed = query_key_val[:, : q_gain.shape[0]]
-    key_val_full = query_key_val[:, q_gain.shape[0] :]
-    d_key_low = unrotate(key_val_full[:, :head_dim], cos_all, sin_all).astype(jnp.bfloat16)
-    d_val_low = key_val_full[:, head_dim:].astype(jnp.bfloat16)
-    grad_gain_query = jnp.sum(d_q_normed * q_unit, axis=0)
-    d_latent = norm_back(d_q_normed * gain_query, q_unit, q_scale).astype(jnp.bfloat16)
-    d_normed_in = (
-        right_dot(d_latent, q_down) + right_dot(d_key_low, k_proj) + right_dot(d_val_low, v_proj)
-    )
-    grad_gain_attn = jnp.sum(d_normed_in * normed_one, axis=0)
-    grad_input = (d_hidden + norm_back(d_normed_in * gain_attn, normed_one, scale_one)).astype(
-        jnp.bfloat16
-    )
     own_width = model_width // (dp_count * tp_count)
     own_at = jnp.arange(model_width // tp_count)
     own_at = (own_at // own_width * tp_count + tp_index) * own_width + own_at % own_width
     pick = (jnp.arange(model_width)[:, None] == own_at[None, :]).astype(jnp.bfloat16)
     own_in = jnp.dot(normed_in, pick, preferred_element_type=jnp.float32).astype(jnp.bfloat16)
-    own_grads = left_dot(own_in, jnp.concatenate([d_latent, d_key_low, d_val_low], axis=1))
-    own_rows = own_grads.shape[0]
-    gain_one = own_part(grad_gain_attn, 0).reshape(own_rows, 1)
-    gain_two = own_part(grad_gain_mlp, 0).reshape(own_rows, 1)
-    gain_mid = own_part(grad_gain_query, 0)
-    own_mid = gain_mid.shape[1]
-    gain_mid = jnp.pad(gain_mid, ((0, 0), (0, own_rows // dp_count - own_mid))).reshape(own_rows, 1)
-    gain_cols = jnp.concatenate([gain_one, gain_two, gain_mid], axis=1)
-    own_grads = jnp.concatenate([own_grads, jnp.pad(gain_cols, ((0, 0), (0, 125)))], axis=1)
+    grad_input, own_grads, acc_one, acc_mid = tail_sum(
+        query_key_val,
+        scale_one,
+        q_scale,
+        cos_all,
+        sin_all,
+        gain_attn.reshape(1, -1),
+        gain_query.reshape(1, -1),
+        q_unit,
+        q_down,
+        k_proj,
+        v_proj,
+        own_in,
+        block_input,
+        d_hidden,
+        "tensor",
+        tp_count,
+        dp_count,
+        2,
+    )
+    gains = jnp.concatenate(
+        [
+            own_part(jnp.sum(acc_one, axis=0), 0),
+            own_part(grad_gain_mlp, 0),
+            own_part(jnp.sum(acc_mid, axis=0), 0),
+        ],
+        axis=1,
+    )
+    kept = own_width
+    gain_row = own_grads.shape[1] - 8
+    own_grads = lax.dynamic_update_slice(own_grads, gains[:, None, :], (0, gain_row, 0))
+    own_grads = own_grads.reshape(-1, own_grads.shape[2])
     own_sum = lax.psum_scatter(own_grads, "dp", scatter_dimension=0, tiled=True)
+    rank = q_down.shape[1]
+    own_mid = rank // (dp_count * tp_count)
+    grad_qd = own_sum[:kept, :rank]
+    grad_key = own_sum[:kept, rank : rank + head_dim]
+    grad_val = own_sum[:kept, rank + head_dim :]
+    grad_g1 = own_sum[gain_row, :kept]
+    grad_g2 = own_sum[gain_row, kept : 2 * kept]
+    grad_gq = own_sum[gain_row, 2 * kept : 2 * kept + own_mid]
     output_two = line_sum(out_part_two, "tensor", tp_count, 4, base=hidden_in[half_rows:])
     block_output = jnp.concatenate([output_one, output_two], axis=0)
-    rank = q_down.shape[1]
-    grad_qd = own_sum[:, :rank]
-    grad_key = own_sum[:, rank : rank + head_dim]
-    grad_val = own_sum[:, rank + head_dim : rank + 2 * head_dim]
-    gain_at = rank + 2 * head_dim
-    grad_g1 = own_sum[:, gain_at]
-    grad_g2 = own_sum[:, gain_at + 1]
-    grad_gq = own_sum[:own_mid, gain_at + 2]
     return (
         block_output,
         grad_input,

time: 1350 us -> 1300 us (0.963)
  waiting for transfers between devices: 321 us -> 299 us
  matrix products: 123 us -> 102 us
  other arithmetic: 53.4 us -> 35 us
    pallas_call x0 -> x1, Pallas kernels: none -> 163 us  [tail_sum(): pl.pallas_call(functools.partial(tail_kernel, axis, n, chunks, 2, block),...]
    pallas_call x2 -> x1, Pallas kernels: 261 us -> 106 us  [line_sum(): pl.pallas_call(functools.partial(line_low_kernel if low else line_kernel,...]
    reduce_scatter x2 -> x1, waiting for transfers between devices: 182 us -> 78.9 us  [shards(): lax.psum_scatter(grad_wide, 'dp', scatter_dimension=0, tiled=True)]
    reduce_scatter x1, waiting for transfers between devices: 0.01 us -> 51.6 us  [shards(): lax.psum_scatter(grad_query_up, 'dp', scatter_dimension=0, tiled=True)]
    reduce_scatter x1, waiting for transfers between devices: 45.8 us -> 75.2 us  [shards(): grad_out = lax.psum_scatter(grad_out, 'dp', scatter_dimension=1, tiled=True)]
    dot_general x7 -> x4, matrix products: 59.2 us -> 41.2 us  [right_dot(): lax.dot_general(left, right, (((1,), (1,)), ((), ())), preferred_element_...]
  transfers between devices with their start and end apart: 6 -> 5, of which waited for: 4 -> 4; matrix products, arithmetic and copies ran while one was open for 2% -> 1% of each run, Pallas kernels for 8% -> 8%
where the time goes in v5:
time: 1300 us; the launch traced here: 1290 us
  Pallas kernels  813 us (63%)
  waiting for transfers between devices  299 us (23%)
  matrix products  102 us (8%)
  other arithmetic  35 us (3%)
  local copies, waits for them, and re-layouts  27 us (2%)
  between operations  14.6 us (1%)
    pallas_call x1, Pallas kernels, attend(): pl.pallas_call(functools.partial(attend_kernel, axis, n, chunks, 2, seq_l...  220 us
    pallas_call x1, Pallas kernels, mid_sum(): pl.pallas_call(functools.partial(mid_kernel, axis, n, chunks, 2), out_sha...  206 us
    pallas_call x1, Pallas kernels, tail_sum(): pl.pallas_call(functools.partial(tail_kernel, axis, n, chunks, 2, block),...  163 us
    pallas_call x1, Pallas kernels, attend_back(): pl.pallas_call(functools.partial(attend_back_kernel, axis, n, chunks, 2,...  118 us
    pallas_call x1, Pallas kernels, line_sum(): pl.pallas_call(functools.partial(line_low_kernel if low else line_kernel,...  106 us
    reduce_scatter x1, waiting for transfers between devices, shards(): lax.psum_scatter(grad_down, 'dp', scatter_dimension=1, tiled=True)  90.8 us
    reduce_scatter x1, waiting for transfers between devices, shards(): lax.psum_scatter(grad_wide, 'dp', scatter_dimension=0, tiled=True)  78.9 us
    reduce_scatter x1, waiting for transfers between devices, shards(): grad_out = lax.psum_scatter(grad_out, 'dp', scatter_dimension=1, tiled=True)  75.2 us
  transfers between devices with their start and end apart: 5, of which 4 were waited for; matrix products, arithmetic and copies ran while one was open for 1% of the time, Pallas kernels for 8%

profile of v5, /device:TPU:0, one launch (start us, length us, event | category | flops | bytes accessed | tf_op | source)
XLA Modules:
  0.0 1290.4 jit_solution(7052189210631485312)
XLA Ops:
  7.3 3.2 fusion
  10.7 6.4 fusion.33
  17.5 2.4 broadcast_multiply_fusion.unit_hbm
  19.9 2.3 fusion.31
  22.2 2.1 convolution_convert_fusion.v_ref
  24.6 0.8 compare_select_fusion.own_ref
  25.5 4.9 subtract_convert_fusion
  30.4 0.8 pad_maximum_fusion.1.k_ref
  31.2 4.4 fusion.14.raw_ref
  35.6 220.4 %attend.1 = (f32[1024,2048]{1,0:T(8,128)}, bf16[1024,1024]{1,0:T(8,128)(2,1)}, bf16[1024,1024]{1,0:T(8,128)(2,1)}, f32[4,1024,1]{2,1,0:T(8,128)}) custom-call(f32[1024,1024]{1,0:T(8,128)} %fusion.14.raw_ref, bf16[1024,256]{1,0:T(8,128)(2,1)} %pad_maximum_fusion.1.k_ref, bf16[1024,256]{1,0:T(8,128)(2,1)} %convolution_convert_fusion.v_ref, ...), custom_call_target="tpu_custom_call" | custom-call | tf_op jit(solution)/shard_map/attend/pallas_call | solution.py:698
  256.0 4.1 multiply_reduce_fusion.2
  260.1 1.6 copy-done
  261.7 3.9 fusion.35
  265.7 0.8 multiply_convert_fusion.mid_hbm
  266.5 12.2 fusion.39
  278.7 8.5 fusion.38
  287.3 14.8 %multiply_convert_fusion.1 = (bf16[1024,1408]{1,0:T(8,128)(2,1)}, bf16[1024,1408]{1,0:T(8,128)(2,1)S(1)}, bf16[1024,1408]{1,0:T(8,128)(2,1)S(1)}) fusion(f32[1024,1408]{1,0:T(8,128)} %fusion.39, f32[1024,1408]{1,0:T(8,128)} %fusion.38, bf16[1024,2048]{1,0:T(8,128)(2,1)S(1)} %multiply_convert_fusion.mid_hbm, bf16[2048,1408]{1,0:T(8,128)(2,1)} %param.25), kind=kOutput, calls=%fused_computation.10 | convolution fusion | flops 5928648704 | bytes 30146560 | tf_op jit(solution)/shard_map/dot_general | solution.py:915
  302.1 9.1 fusion.40
  311.1 12.6 convolution_add_fusion.x_ref
  323.8 205.6 %mid_sum.1 = (f32[1024,2048]{1,0:T(8,128)}, f32[4096,1408]{1,0:T(8,128)}, f32[1408,2048]{1,0:T(8,128)}, f32[512,2048]{1,0:T(8,128)}, f32[512,2048]{1,0:T(8,128)}) custom-call(f32[1024,2048]{1,0:T(8,128)} %convolution_add_fusion.x_ref, bf16[1024,2048]{1,0:T(8,128)(2,1)} %copy-done.7, bf16[1024,1408]{1,0:T(8,128)(2,1)} %get-tuple-element.55.act_hbm, ...), custom_call_target="tpu_custom_call" | custom-call | tf_op jit(solution)/shard_map/mid_sum/pallas_call | solution.py:372
  529.4 7.8 multiply_reduce_fusion
  537.7 2.4 copy-done.3
  540.1 3.8 multiply_add_fusion.hidden_hbm
  544.0 11.0 fusion.9.dm_ref
  555.0 7.1 fusion.7
  562.1 118.3 %attend_back.1 = (bf16[512,2048]{1,0:T(8,128)(2,1)}, bf16[1024,1024]{1,0:T(8,128)(2,1)}, f32[1024,1536]{1,0:T(8,128)}) custom-call(f32[512,2048]{1,0:T(8,128)} %get-tuple-element.37.x_ref, f32[512,2048]{1,0:T(8,128)} %get-tuple-element.58.base_ref, bf16[1024,1024]{1,0:T(8,128)(2,1)} %get-tuple-element.38.q_ref, bf16[1024,1024]{1,0:T(8,128)(2,1)} %fusion.9.dm_ref, ...), custom_call_target="tpu_custom_call" | custom-call | tf_op jit(solution)/shard_map/attend_back/pallas_call | solution.py:821
  680.4 6.0 fusion.13
  686.4 5.6 fusion.12.own_hbm
  692.0 1.0 copy.40.scale_mid_ref
  693.0 1.0 copy.39.scale_one_ref
  694.0 162.7 %tail_sum.1 = (bf16[1024,2048]{1,0:T(8,128)(2,1)}, f32[8,72,1536]{2,1,0:T(8,128)}, f32[8,2048]{1,0:T(8,128)}, f32[8,1024]{1,0:T(8,128)}) custom-call(f32[1024,1536]{1,0:T(8,128)} %get-tuple-element.44.x_ref, f32[1024,1]{1,0:T(8,128)} %copy.39.scale_one_ref, f32[1024,1]{1,0:T(8,128)} %copy.40.scale_mid_ref, f32[1024,128]{1,0:T(8,128)} %get-tuple-element.69.cos_ref, ...), custom_call_target="tpu_custom_call" | custom-call | tf_op jit(solution)/shard_map/tail_sum/pallas_call | solution.py:558
  856.7 0.9 reduce_sum.83
  857.7 0.8 reduce_sum.85
  858.7 1.6 dynamic_update_slice.3
  860.4 0.7 reduce-scatter.12.cloned.1.call-update
  861.2 0.7 reduce-scatter.8.cloned.1.call-update
  863.1 105.7 %line_sum.1 = bf16[512,2048]{1,0:T(8,128)(2,1)} custom-call(f32[512,2048]{1,0:T(8,128)} %get-tuple-element.41.x_ref, f32[512,2048]{1,0:T(8,128)} %get-tuple-element.59.base_ref), custom_call_target="tpu_custom_call" | custom-call | tf_op jit(solution)/shard_map/line_sum/pallas_call | solution.py:195
  968.7 4.2 pad_maximum_fusion
  972.9 1.7 slice.51
  974.6 1.2 slice_bitcast_fusion.1
  975.8 1.3 slice_bitcast_fusion
  977.1 1.5 fusion.37
  978.6 78.9 %reduce-scatter.12.cloned.1.call-done = f32[512,1408]{1,0:T(8,128)} async-done(((f32[4096,1408]{1,0:T(8,128)}), f32[512,1408]{1,0:T(8,128)}) %reduce-scatter.12.cloned.1.call-update) | async-done | bytes 2883600 | tf_op jit(solution)/shard_map/reduce_scatter | solution.py:935
  1057.5 3.6 fusion.36
  1061.1 51.6 %reduce-scatter.8.cloned.1.call-done = f32[128,1024]{1,0:T(8,128)} async-done(((f32[1024,1024]{1,0:T(8,128)}), f32[128,1024]{1,0:T(8,128)}) %reduce-scatter.8.cloned.1.call-update) | async-done | bytes 524304 | tf_op jit(solution)/shard_map/reduce_scatter | solution.py:967
  1112.6 75.2 %reduce-scatter.10.cloned.1.call-done = f32[1024,256]{1,0:T(8,128)} async-done(((f32[1024,2048]{1,0:T(8,128)}), f32[1024,256]{1,0:T(8,128)}) %reduce-scatter.10.cloned.1.call-update) | async-done | bytes 1048592 | tf_op jit(solution)/shard_map/reduce_scatter | solution.py:946
  1187.9 90.8 %reduce-scatter.14.cloned.1.call-done = f32[1408,256]{1,0:T(8,128)} async-done(((f32[1408,2048]{1,0:T(8,128)}), f32[1408,256]{1,0:T(8,128)}) %reduce-scatter.14.cloned.1.call-update) | async-done | bytes 1441808 | tf_op jit(solution)/shard_map/reduce_scatter | solution.py:938
  1278.7 4.8 copy.44
  (91 shorter events, 3.1 us)
Async XLA Ops:
  7.2 3.3 copy-start.19
  7.2 965.7 %reduce-scatter.6.cloned.1.call-start = ((), (), s32[]{:S(2)}) async-start(), calls=%async_computation.5 | async-start | bytes 3981312 | tf_op jit(solution)/shard_map/reduce_scatter | solution.py:1005
  7.2 3.5 copy-start.1
  10.7 675.7 %copy-start.17 = (f32[2048]{0:T(1024)}, f32[2048]{0:T(1024)S(1)}, u32[]{:S(2)}) copy-start(f32[2048]{0:T(1024)S(1)} %convert_element_type.48) | copy-start | bytes 24580
  17.4 2.4 copy-start.15
  17.5 2.4 copy-start.21
  17.5 2.4 copy-start.12
  19.8 660.5 %copy-start.18 = (f32[1024]{0:T(1024)}, f32[1024]{0:T(1024)S(1)}, u32[]{:S(2)}) copy-start(f32[1024]{0:T(1024)S(1)} %convert_element_type.50) | copy-start | bytes 12292
  19.9 2.3 copy-start.13
  22.1 2.1 copy-start.22
  22.2 9.1 copy-start.11
  24.4 11.2 copy-start.14
  24.6 6.6 copy-start.4
  256.0 5.8 copy-start
  261.7 3.9 copy-start.20
  265.7 13.0 %slice-start.2 = ((s8[5767168]{0:T(1024)(128)(4,1)}), s8[4194304]{0:T(1024)(128)(4,1)S(1)}, s32[]{:S(2)}) async-start(s8[5767168]{0:T(1024)(128)(4,1)} %bitcast.37), calls=%async_computation.12 | async-start | bytes 8388608
  266.4 20.8 %copy-start.7 = (bf16[1024,2048]{1,0:T(8,128)(2,1)}, bf16[1024,2048]{1,0:T(8,128)(2,1)S(1)}, u32[]{:S(2)}) copy-start(bf16[1024,2048]{1,0:T(8,128)(2,1)S(1)} %multiply_convert_fusion.mid_hbm) | copy-start | bytes 12582916
  266.5 12.2 copy-start.6
  266.5 12.2 slice-start.3
  278.7 23.3 %slice-start.4 = ((s8[5767168]{0:T(1024)(128)(4,1)}), s8[1572864]{0:T(1024)(128)(4,1)S(1)}, s32[]{:S(2)}) async-start(s8[5767168]{0:T(1024)(128)(4,1)} %bitcast.51), calls=%async_computation.14 | async-start | bytes 3145728
  287.3 14.8 %slice-start.5 = ((s8[5767168]{0:T(1024)(128)(4,1)}), s8[4194304]{0:T(1024)(128)(4,1)S(1)}, s32[]{:S(2)}) async-start(s8[5767168]{0:T(1024)(128)(4,1)} %bitcast.51), calls=%async_computation.15 | async-start | bytes 8388608
  302.0 9.1 copy-start.8
  302.0 9.1 copy-start.9
  529.4 7.8 slice-start
  529.4 8.3 slice-start.1
  529.4 10.7 copy-start.3
  544.0 11.0 copy-start.2
  544.0 11.0 copy-start.23
  562.1 118.3 %copy-start.5 = (f32[1024,1024]{1,0:T(8,128)S(1)}, f32[1024,1024]{1,0:T(8,128)}, u32[]{:S(2)}) copy-start(f32[1024,1024]{1,0:T(8,128)} %broadcast_multiply_fusion.unit_hbm) | copy-start | bytes 12582916
  686.4 5.6 copy-start.16
  860.4 197.1 %reduce-scatter.12.cloned.1.call-start = ((), (), s32[]{:S(2)}) async-start(), calls=%async_computation.8 | async-start | bytes 25952256 | tf_op jit(solution)/shard_map/reduce_scatter | solution.py:935
  861.1 251.5 %reduce-scatter.8.cloned.1.call-start = ((), (), s32[]{:S(2)}) async-start(), calls=%async_computation.6 | async-start | bytes 4718592 | tf_op jit(solution)/shard_map/reduce_scatter | solution.py:967
  861.9 326.0 %reduce-scatter.10.cloned.1.call-start = ((), (), s32[]{:S(2)}) async-start(), calls=%async_computation.7 | async-start | bytes 9437184 | tf_op jit(solution)/shard_map/reduce_scatter | solution.py:946
  862.5 416.2 %reduce-scatter.14.cloned.1.call-start = ((), (), s32[]{:S(2)}) async-start(), calls=%async_computation.9 | async-start | bytes 12976128 | tf_op jit(solution)/shard_map/reduce_scatter | solution.py:938
  863.0 105.7 %copy-start.10 = (bf16[512,2048]{1,0:T(8,128)(2,1)S(1)}, bf16[512,2048]{1,0:T(8,128)(2,1)}, u32[]{:S(2)}) copy-start(bf16[512,2048]{1,0:T(8,128)(2,1)} %get-tuple-element.40) | copy-start | bytes 6291460
Sparse Core Ops, SparseCore 0:
  860.5 46.9 reduce-scatter.5
  911.1 146.3 reduce-scatter.11
  1061.4 51.1 reduce-scatter.7
  1116.5 71.3 reduce-scatter.9
  1191.8 86.8 reduce-scatter.13

commit v6 on v5

--- a/solution.py
+++ b/solution.py
@@ -20,12 +20,6 @@
 def normalize(values):
     scale_rows = lax.rsqrt(jnp.mean(values * values, axis=-1, keepdims=True) + epsilon)
     return (values * scale_rows, scale_rows)
-
-
-def norm_back(grad_normed, normed, scale_rows):
-    return scale_rows * (
-        grad_normed - normed * jnp.mean(grad_normed * normed, axis=-1, keepdims=True)
-    )
 
 
 def left_dot(left, right):
@@ -163,13 +157,9 @@
     lax.fori_loop(0, chunks, drain, 0)
 
 
-def line_kernel(axis, n, chunks, lag, x_ref, o_ref, red, *sems):
-    line_steps(axis, n, chunks, lag, x_ref, o_ref, red, sems, lambda at: None, None)
-
-
-def line_low_kernel(axis, n, chunks, lag, x_ref, base_ref, o_ref, red, held, *sems):
+def line_low_kernel(axis, n, chunks, lag, x_ref, o_ref, red, held, *sems):
     def finish(at):
-        o_ref[at] = (base_ref[at] + held[at]).astype(o_ref.dtype)
+        o_ref[at] = held[at].astype(o_ref.dtype)
 
     line_steps(axis, n, chunks, lag, x_ref, held, red, sems, finish, None)
 
@@ -187,22 +177,22 @@
     )
 
 
-def line_sum(x, axis, n, cid, base=None):
-    low = base is not None
-    chunks = chunk_count(x.shape[0], 32, 16 if low else 8)
-    held = [pltpu.VMEM(x.shape, x.dtype)] if low else []
-    operands = (x, base) if low else (x,)
+def line_sum(x, axis, n, cid):
+    chunks = chunk_count(x.shape[0], 32, 16)
     return pl.pallas_call(
-        functools.partial(line_low_kernel if low else line_kernel, axis, n, chunks, 2),
-        out_shape=jax.ShapeDtypeStruct(x.shape, jnp.bfloat16 if low else x.dtype),
-        in_specs=[pl.BlockSpec(memory_space=pltpu.VMEM)] * len(operands),
+        functools.partial(line_low_kernel, axis, n, chunks, 2),
+        out_shape=jax.ShapeDtypeStruct(x.shape, jnp.bfloat16),
+        in_specs=[pl.BlockSpec(memory_space=pltpu.VMEM)],
         out_specs=pl.BlockSpec(memory_space=pltpu.VMEM),
-        scratch_shapes=[pltpu.VMEM(x.shape, x.dtype)]
-        + held
+        scratch_shapes=[pltpu.VMEM(x.shape, x.dtype)] * 2
         + [pltpu.SemaphoreType.DMA((2, chunks))] * 4,
         compiler_params=line_params(cid),
         name="line_sum",
-    )(*operands)
+    )(x)
+
+
+def fold_rows(values):
+    return jnp.sum(values.reshape(values.shape[0] // 8, 8, values.shape[1]), axis=0)
 
 
 def mid_kernel(
@@ -211,17 +201,23 @@
     chunks,
     lag,
     x_ref,
+    scale_ref,
+    gain_ref,
     mid_hbm,
     act_hbm,
     gate_hbm,
     up_hbm,
     cot_hbm,
     down_hbm,
-    o_ref,
+    hidden_hbm,
+    d_hidden_ref,
+    d_low_ref,
+    acc_ref,
     grad_wide_ref,
     grad_down_ref,
     one_ref,
     two_ref,
+    held,
     red,
     mid_ref,
     act_ref,
@@ -231,12 +227,23 @@
     down_ref,
     wide_tile,
     row_tile,
+    base_tile,
+    hidden_tile,
+    d_tile,
+    low_tile,
     load_sem,
     wide_sem,
     row_sem,
+    base_sem,
+    hidden_sem,
+    d_sem,
+    low_sem,
     *sems,
 ):
+    me = lax.axis_index(axis)
     rows, width = cot_ref.shape
+    part_rows = rows // (2 * chunks)
+    acc_ref[...] = jnp.zeros_like(acc_ref)
     units = act_ref.shape[1]
     wide = wide_tile.shape[0]
     wide_count = width // wide
@@ -341,11 +348,21 @@
                     else:
                         out_copy(one_ref, half_blocks - 1).wait()
 
+                base = pltpu.make_async_copy(
+                    hidden_hbm.at[block(t + side * half_blocks)], base_tile, base_sem.at[0]
+                )
+                base.start()
                 row_tile[0:tile, :] = jnp.dot(
                     act_ref[block(t + side * half_blocks), :],
                     down_ref[...],
                     preferred_element_type=jnp.float32,
                 )
+                base.wait()
+
+                @pl.when(me == 0)
+                def _():
+                    row_tile[0:tile, :] += base_tile[...]
+
                 out_copy(dst, t).start()
 
         return carry
@@ -354,17 +371,75 @@
         late = steps - 4
         bounds = tuple(jnp.clip(at - 2, 0, late) * job_count // late for at in (s, s + 1))
         lax.fori_loop(*bounds, job, 0)
-
-    line_steps(axis, n, chunks, lag, x_ref, o_ref, red, sems, lambda at: None, after_step)
+        for half in (0, 1):
+            back = me if half == 0 else (n - 1 - me)
+            c = s - lag * (n - 1) - lag * back
+
+            @pl.when((c + 1 >= 0) & (c + 1 < chunks))
+            def _():
+                take_hidden(half, c + 1).start()
+
+            @pl.when((c >= 0) & (c < chunks))
+            def _():
+                close(half, c)
+
+    def at_chunk(half, c):
+        return pl.ds(pl.multiple_of((half * chunks + c) * part_rows, part_rows), part_rows)
+
+    def take_hidden(half, c):
+        slot = lax.rem(c, 2)
+        return pltpu.make_async_copy(
+            hidden_hbm.at[at_chunk(half, c)], hidden_tile.at[half, slot], hidden_sem.at[half, slot]
+        )
+
+    def put(tile_ref, dst, sem, half, c):
+        slot = lax.rem(c, 2)
+        return pltpu.make_async_copy(
+            tile_ref.at[half, slot], dst.at[at_chunk(half, c)], sem.at[half, slot]
+        )
+
+    def puts(half, c):
+        return (
+            put(d_tile, d_hidden_ref, d_sem, half, c),
+            put(low_tile, d_low_ref, low_sem, half, c),
+        )
+
+    def close(half, c):
+        at = at_chunk(half, c)
+        slot = lax.rem(c, 2)
+        take_hidden(half, c).wait()
+
+        @pl.when(c >= 2)
+        def _():
+            for item in puts(half, c - 2):
+                item.wait()
+
+        d_mid = held[at]
+        scale = scale_ref[at, :]
+        normed = hidden_tile[half, slot] * scale
+        acc_ref[...] += fold_rows(d_mid * normed)
+        grad_normed = d_mid * gain_ref[...]
+        mean = jnp.mean(grad_normed * normed, axis=1, keepdims=True)
+        d_hidden = cot_ref[at].astype(jnp.float32) + scale * (grad_normed - normed * mean)
+        d_tile[half, slot] = d_hidden
+        low_tile[half, slot] = d_hidden.astype(low_tile.dtype)
+        for item in puts(half, c):
+            item.start()
+
+    line_steps(axis, n, chunks, lag, x_ref, held, red, sems, lambda at: None, after_step)
+    for half in (0, 1):
+        for c in range(max(chunks - 2, 0), chunks):
+            for item in puts(half, c):
+                item.wait()
     wide_copy(1, wide_count - 1).wait()
     out_copy(two_ref, half_blocks - 1).wait()
 
 
-def mid_sum(x, mid, act, d_gate, d_up, cot, w_down, axis, n, parts, cid):
+def mid_sum(x, scale, gain, mid, act, d_gate, d_up, cot, w_down, hidden, axis, n, parts, cid):
     rows, width = x.shape
     units = act.shape[1]
     tile = min(256, rows // 2)
-    chunks = chunk_count(rows, 32, 8)
+    chunks = chunk_count(rows, 32, 16)
     vmem = pl.BlockSpec(memory_space=pltpu.VMEM)
     anywhere = pl.BlockSpec(memory_space=pl.ANY)
     loaded = (mid, act, d_gate, d_up, cot, w_down)
@@ -373,24 +448,34 @@
         functools.partial(mid_kernel, axis, n, chunks, 2),
         out_shape=(
             jax.ShapeDtypeStruct(x.shape, jnp.float32),
+            jax.ShapeDtypeStruct(x.shape, jnp.bfloat16),
+            jax.ShapeDtypeStruct((8, width), jnp.float32),
             jax.ShapeDtypeStruct((2 * width, units), jnp.float32),
             jax.ShapeDtypeStruct((units, width), jnp.float32),
             jax.ShapeDtypeStruct((rows // 2, width), jnp.float32),
             jax.ShapeDtypeStruct((rows // 2, width), jnp.float32),
         ),
-        in_specs=[vmem] + [anywhere] * 6,
-        out_specs=(vmem,) + (anywhere,) * 4,
-        scratch_shapes=[pltpu.VMEM(x.shape, jnp.float32)]
+        in_specs=[vmem] * 3 + [anywhere] * 7,
+        out_specs=(anywhere, anywhere, vmem) + (anywhere,) * 4,
+        scratch_shapes=[pltpu.VMEM(x.shape, jnp.float32)] * 2
         + [pltpu.VMEM(item.shape, item.dtype) for item in loaded]
-        + [pltpu.VMEM((width // parts, units), jnp.float32), pltpu.VMEM((tall, width), jnp.float32)]
-        + [pltpu.SemaphoreType.DMA((len(loaded),))]
-        + [pltpu.SemaphoreType.DMA((1,))] * 2
+        + [
+            pltpu.VMEM((width // parts, units), jnp.float32),
+            pltpu.VMEM((tall, width), jnp.float32),
+            pltpu.VMEM((tile, width), jnp.float32),
+            pltpu.VMEM((2, 2, rows // (2 * chunks), width), jnp.float32),
+            pltpu.VMEM((2, 2, rows // (2 * chunks), width), jnp.float32),
+            pltpu.VMEM((2, 2, rows // (2 * chunks), width), jnp.bfloat16),
+            pltpu.SemaphoreType.DMA((len(loaded),)),
+        ]
+        + [pltpu.SemaphoreType.DMA((1,))] * 3
+        + [pltpu.SemaphoreType.DMA((2, 2))] * 3
         + [pltpu.SemaphoreType.DMA((2, chunks))] * 4,
         compiler_params=pltpu.CompilerParams(
             collective_id=cid, has_side_effects=True, vmem_limit_bytes=62 << 20
         ),
         name="mid_sum",
-    )(x, *loaded)
+    )(x, scale, gain, *loaded, hidden)
 
 
 def tail_kernel(
@@ -458,9 +543,6 @@
     acc_mid_ref[...] = jnp.zeros_like(acc_mid_ref)
     own_ref[...] = jnp.zeros_like(own_ref)
 
-    def fold(values):
-        return jnp.sum(values.reshape(values.shape[0] // 8, 8, values.shape[1]), axis=0)
-
     def store(own):
         return pltpu.make_async_copy(grad_ref, grad_hbm.at[own], store_sem.at[0])
 
@@ -472,7 +554,7 @@
         take_hidden.start()
         d_bq = held[own, 0:rank]
         unit = unit_ref[own, :]
-        acc_mid_ref[...] += fold(d_bq * unit)
+        acc_mid_ref[...] += fold_rows(d_bq * unit)
         eq = d_bq * gain_mid_ref[...]
         mean_mid = jnp.mean(eq * unit, axis=1, keepdims=True)
         d_latent = (scale_mid_ref[own, :] * (eq - unit * mean_mid)).astype(jnp.bfloat16)
@@ -497,7 +579,7 @@
         take_hidden.wait()
         scale_one = scale_one_ref[own, :]
         normed = input_ref[...].astype(jnp.float32) * scale_one
-        acc_one_ref[...] += fold(d_in * normed)
+        acc_one_ref[...] += fold_rows(d_in * normed)
         e_in = d_in * gain_one_ref[...]
         mean_one = jnp.mean(e_in * normed, axis=1, keepdims=True)
         grad_ref[...] = (hidden_ref[...] + scale_one * (e_in - normed * mean_one)).astype(
@@ -600,10 +682,13 @@
     sin_ref,
     out_ref,
     base_ref,
+    gain_ref,
     o_ref,
     q_ref,
     mixed_ref,
     norm_ref,
+    normed_ref,
+    scale_ref,
     part,
     red,
     *sems,
@@ -681,7 +766,13 @@
         )
         lax.fori_loop(*bounds, job, 0)
 
-    line_steps(axis, n, chunks, lag, part, o_ref, red, sems, lambda at: None, after_step)
+    def finish(at):
+        hidden = o_ref[at]
+        scale_rows = lax.rsqrt(jnp.mean(hidden * hidden, axis=1, keepdims=True) + epsilon)
+        scale_ref[at, :] = scale_rows
+        normed_ref[at] = (hidden * scale_rows * gain_ref[...]).astype(normed_ref.dtype)
+
+    line_steps(axis, n, chunks, lag, part, o_ref, red, sems, finish, after_step)
 
 
 def reach_list(seq_len, block):
@@ -690,10 +781,12 @@
     return [min(seq_len, -(-end // step) * step) for end in ends]
 
 
-def attend(raw, k, v, own_ids, all_ids, cos_tab, sin_tab, out_proj, base, axis, n, seq_len, cid):
+def attend(
+    raw, k, v, own_ids, all_ids, cos_tab, sin_tab, out_proj, base, gain, axis, n, seq_len, cid
+):
     rows, width = base.shape
-    block = min(128, seq_len)
-    chunks = chunk_count(rows, 32, 8)
+    block = min(64, seq_len)
+    chunks = chunk_count(rows, 32, 16)
     vmem = pl.BlockSpec(memory_space=pltpu.VMEM)
     return pl.pallas_call(
         functools.partial(attend_kernel, axis, n, chunks, 2, seq_len, block),
@@ -702,16 +795,18 @@
             jax.ShapeDtypeStruct(raw.shape, jnp.bfloat16),
             jax.ShapeDtypeStruct(raw.shape, jnp.bfloat16),
             jax.ShapeDtypeStruct((raw.shape[1] // k.shape[1], rows, 1), jnp.float32),
+            jax.ShapeDtypeStruct((rows, width), jnp.bfloat16),
+            jax.ShapeDtypeStruct((rows, 1), jnp.float32),
         ),
-        in_specs=[vmem] * 9,
-        out_specs=(vmem,) * 4,
+        in_specs=[vmem] * 10,
+        out_specs=(vmem,) * 6,
         scratch_shapes=[pltpu.VMEM((rows, width), jnp.float32)] * 2
         + [pltpu.SemaphoreType.DMA((2, chunks))] * 4,
         compiler_params=pltpu.CompilerParams(
             collective_id=cid, has_side_effects=True, vmem_limit_bytes=60 << 20
         ),
         name="attend",
-    )(raw, k, v, own_ids, all_ids, cos_tab, sin_tab, out_proj, base)
+    )(raw, k, v, own_ids, all_ids, cos_tab, sin_tab, out_proj, base, gain)
 
 
 def attend_back_kernel(
@@ -722,7 +817,6 @@
     seq_len,
     block,
     x_ref,
-    base_ref,
     q_ref,
     dm_ref,
     k_ref,
@@ -751,7 +845,7 @@
     sums_ref[:, rank:] = jnp.zeros((rows, 2 * head_dim), jnp.float32)
 
     def finish(at):
-        o_ref[at] = (base_ref[at] + held[at]).astype(o_ref.dtype)
+        o_ref[at] = held[at].astype(o_ref.dtype)
 
     def job(j, carry):
         head = lax.rem(j, heads)
@@ -813,7 +907,7 @@
 
 
 def attend_back(
-    x, base, q, dm, k, v, norm, own_ids, all_ids, cos_tab, sin_tab, q_up, axis, n, seq_len, cid
+    x, q, dm, k, v, norm, own_ids, all_ids, cos_tab, sin_tab, q_up, axis, n, seq_len, cid
 ):
     chunks = chunk_count(x.shape[0], 32, 16)
     block = min(256, seq_len)
@@ -825,13 +919,13 @@
             jax.ShapeDtypeStruct(q.shape, jnp.bfloat16),
             jax.ShapeDtypeStruct((k.shape[0], q_up.shape[0] + 2 * k.shape[1]), jnp.float32),
         ),
-        in_specs=[vmem] * 12,
+        in_specs=[vmem] * 11,
         out_specs=(vmem, vmem, vmem),
         scratch_shapes=[pltpu.VMEM(x.shape, x.dtype)] * 2
         + [pltpu.SemaphoreType.DMA((2, chunks))] * 4,
         compiler_params=line_params(cid),
         name="attend_back",
-    )(x, base, q, dm, k, v, norm, own_ids, all_ids, cos_tab, sin_tab, q_up)
+    )(x, q, dm, k, v, norm, own_ids, all_ids, cos_tab, sin_tab, q_up)
 
 
 def shards(
@@ -894,7 +988,7 @@
         jnp.dot(normed_in, k_proj, preferred_element_type=jnp.float32), cos_all, sin_all
     ).astype(jnp.bfloat16)
     val_rows = jnp.dot(normed_in, v_proj, preferred_element_type=jnp.float32).astype(jnp.bfloat16)
-    hidden_in, queries, mixed_heads, log_norm = attend(
+    hidden_in, queries, mixed_heads, log_norm, normed_mid, scale_two = attend(
         q_raw,
         key_rows,
         val_rows,
@@ -904,13 +998,12 @@
         sin_all,
         out_proj,
         block_input,
+        gain_mlp.reshape(1, -1),
         "tensor",
         tp_count,
         seq_len,
         5,
     )
-    normed_two, scale_two = normalize(hidden_in)
-    normed_mid = (normed_two * gain_mlp).astype(jnp.bfloat16)
     gate_pre = jnp.dot(normed_mid, w_gate, preferred_element_type=jnp.float32)
     up_pre = jnp.dot(normed_mid, w_up, preferred_element_type=jnp.float32)
     gate_sig = jax.nn.sigmoid(gate_pre)
@@ -919,14 +1012,17 @@
     d_gate = (d_act * up_pre * gate_sig * (1.0 + gate_pre * (1.0 - gate_sig))).astype(jnp.bfloat16)
     d_up = (d_act * gate_pre * gate_sig).astype(jnp.bfloat16)
     d_mid_part = right_dot(d_gate, w_gate) + right_dot(d_up, w_up)
-    d_mid, grad_wide, grad_down, out_part_one, out_part_two = mid_sum(
+    d_hidden, d_hidden_low, acc_two, grad_wide, grad_down, out_part_one, out_part_two = mid_sum(
         d_mid_part,
+        scale_two,
+        gain_mlp.reshape(1, -1),
         normed_mid,
         hidden_act,
         d_gate,
         d_up,
         d_output,
         w_down,
+        hidden_in,
         "tensor",
         tp_count,
         dp_count,
@@ -936,17 +1032,12 @@
     grad_gate = grad_wide[: grad_wide.shape[0] // 2]
     grad_up = grad_wide[grad_wide.shape[0] // 2 :]
     grad_down = lax.psum_scatter(grad_down, "dp", scatter_dimension=1, tiled=True)
-    grad_gain_mlp = jnp.sum(d_mid * normed_two, axis=0)
-    d_hidden = cotan_f32 + norm_back(d_mid * gain_mlp, normed_two, scale_two)
-    d_hidden_low = d_hidden.astype(jnp.bfloat16)
     grad_out = left_dot(mixed_heads, d_hidden_low)
     d_mixed = right_dot(d_hidden_low, out_proj).astype(jnp.bfloat16)
-    half_rows = row_count // 2
     out_part_one, grad_out = lax.optimization_barrier((out_part_one, grad_out))
     grad_out = lax.psum_scatter(grad_out, "dp", scatter_dimension=1, tiled=True)
     output_one, d_q_raw, query_key_val = attend_back(
         out_part_one,
-        hidden_in[:half_rows],
         queries,
         d_mixed,
         key_rows,
@@ -993,7 +1084,7 @@
     gains = jnp.concatenate(
         [
             own_part(jnp.sum(acc_one, axis=0), 0),
-            own_part(grad_gain_mlp, 0),
+            own_part(jnp.sum(acc_two, axis=0), 0),
             own_part(jnp.sum(acc_mid, axis=0), 0),
         ],
         axis=1,
@@ -1011,7 +1102,7 @@
     grad_g1 = own_sum[gain_row, :kept]
     grad_g2 = own_sum[gain_row, kept : 2 * kept]
     grad_gq = own_sum[gain_row, 2 * kept : 2 * kept + own_mid]
-    output_two = line_sum(out_part_two, "tensor", tp_count, 4, base=hidden_in[half_rows:])
+    output_two = line_sum(out_part_two, "tensor", tp_count, 4)
     block_output = jnp.concatenate([output_one, output_two], axis=0)
     return (
         block_output,

time: 1300 us -> 1280 us (0.985)
  other arithmetic: 35 us -> 18.7 us
where the time goes in v6:
time: 1280 us; the launch traced here: 1270 us
  Pallas kernels  820 us (64%)
  waiting for transfers between devices  300 us (23%)
  matrix products  99.2 us (8%)
  other arithmetic  18.7 us (1%)
  local copies, waits for them, and re-layouts  18.5 us (1%)
  between operations  14.6 us (1%)
    pallas_call x1, Pallas kernels, attend(): pl.pallas_call(functools.partial(attend_kernel, axis, n, chunks, 2, seq_l...  223 us
    pallas_call x1, Pallas kernels, mid_sum(): pl.pallas_call(functools.partial(mid_kernel, axis, n, chunks, 2), out_sha...  213 us
    pallas_call x1, Pallas kernels, tail_sum(): pl.pallas_call(functools.partial(tail_kernel, axis, n, chunks, 2, block),...  163 us
    pallas_call x1, Pallas kernels, attend_back(): pl.pallas_call(functools.partial(attend_back_kernel, axis, n, chunks, 2,...  117 us
    pallas_call x1, Pallas kernels, line_sum(): pl.pallas_call(functools.partial(line_low_kernel, axis, n, chunks, 2), ou...  104 us
    reduce_scatter x1, waiting for transfers between devices, shards(): lax.psum_scatter(grad_down, 'dp', scatter_dimension=1, tiled=True)  90.8 us
    reduce_scatter x1, waiting for transfers between devices, shards(): lax.psum_scatter(grad_wide, 'dp', scatter_dimension=0, tiled=True)  80.1 us
    reduce_scatter x1, waiting for transfers between devices, shards(): grad_out = lax.psum_scatter(grad_out, 'dp', scatter_dimension=1, tiled=True)  75.2 us
  transfers between devices with their start and end apart: 5, of which 4 were waited for; matrix products, arithmetic and copies ran while one was open for 1% of the time, Pallas kernels for 8%

profile of v6, /device:TPU:0, one launch (start us, length us, event | category | flops | bytes accessed | tf_op | source)
XLA Modules:
  0.0 1270.8 jit_solution(8530158067342663478)
XLA Ops:
  7.3 3.2 fusion
  10.5 0.2 copy-done
  10.7 6.4 fusion.26
  17.1 0.3 multiply_reduce_fusion
  17.5 2.4 broadcast_multiply_fusion.unit_hbm
  19.8 2.3 fusion.24
  22.1 2.1 convolution_convert_fusion.1.v_ref
  24.3 0.1 fusion.10
  24.4 0.2 copy.37
  24.6 0.8 compare_select_fusion.own_ref
  25.5 0.6 reshape.251
  26.1 4.3 subtract_convert_fusion
  30.4 0.8 pad_maximum_fusion.1.k_ref
  31.2 4.4 fusion.7.raw_ref
  35.6 222.7 %attend.1 = (f32[1024,2048]{1,0:T(8,128)}, bf16[1024,1024]{1,0:T(8,128)(2,1)}, bf16[1024,1024]{1,0:T(8,128)(2,1)}, f32[4,1024,1]{2,1,0:T(8,128)}, bf16[1024,2048]{1,0:T(8,128)(2,1)}, /*index=5*/f32[1024,1]{1,0:T(8,128)}) custom-call(f32[1024,1024]{1,0:T(8,128)} %fusion.7.raw_ref, bf16[1024,256]{1,0:T(8,128)(2,1)} %pad_maximum_fusion.1.k_ref, ...), custom_call_target="tpu_custom_call" | custom-call | tf_op jit(solution)/shard_map/attend/pallas_call | solution.py:791
  258.3 11.9 fusion.31
  270.2 8.7 fusion.30
  278.9 14.2 %multiply_convert_fusion = (bf16[1024,1408]{1,0:T(8,128)(2,1)}, bf16[1024,1408]{1,0:T(8,128)(2,1)S(1)}, bf16[1024,1408]{1,0:T(8,128)(2,1)S(1)}) fusion(f32[1024,1408]{1,0:T(8,128)} %fusion.31, f32[1024,1408]{1,0:T(8,128)} %fusion.30, bf16[1024,2048]{1,0:T(8,128)(2,1)S(1)} %copy-done.4, bf16[2048,1408]{1,0:T(8,128)(2,1)} %param.25), kind=kOutput, calls=%fused_computation.5 | convolution fusion | flops 5928648704 | bytes 30146560 | tf_op jit(solution)/shard_map/dot_general | solution.py:1008
  293.2 8.8 fusion.32
  302.0 12.6 convolution_add_fusion.x_ref
  314.7 213.3 %mid_sum.1 = (f32[1024,2048]{1,0:T(8,128)}, bf16[1024,2048]{1,0:T(8,128)(2,1)}, f32[8,2048]{1,0:T(8,128)}, f32[4096,1408]{1,0:T(8,128)}, f32[1408,2048]{1,0:T(8,...) custom-call(f32[1024,2048]{1,0:T(8,128)} %convolution_add_fusion.x_ref, f32[1024,1]{1,0:T(8,128)} %get-tuple-element.38.scale_ref, ...), custom_call_target="tpu_custom_call" | custom-call | tf_op jit(solution)/shard_map/mid_sum/pallas_call | solution.py:447
  528.1 9.4 convolution_convert_fusion.dm_ref
  537.5 6.8 fusion.33
  544.3 116.9 %attend_back.1 = (bf16[512,2048]{1,0:T(8,128)(2,1)}, bf16[1024,1024]{1,0:T(8,128)(2,1)}, f32[1024,1536]{1,0:T(8,128)}) custom-call(f32[512,2048]{1,0:T(8,128)} %get-tuple-element.43.x_ref, bf16[1024,1024]{1,0:T(8,128)(2,1)} %get-tuple-element.44.q_ref, bf16[1024,1024]{1,0:T(8,128)(2,1)} %convolution_convert_fusion.dm_ref, ...), custom_call_target="tpu_custom_call" | custom-call | tf_op jit(solution)/shard_map/attend_back/pallas_call | solution.py:915
  661.2 6.0 fusion.6
  667.2 5.6 fusion.5.own_hbm
  672.8 1.0 copy.40.scale_mid_ref
  673.8 1.0 copy.39.scale_one_ref
  674.8 162.6 %tail_sum.1 = (bf16[1024,2048]{1,0:T(8,128)(2,1)}, f32[8,72,1536]{2,1,0:T(8,128)}, f32[8,2048]{1,0:T(8,128)}, f32[8,1024]{1,0:T(8,128)}) custom-call(f32[1024,1536]{1,0:T(8,128)} %get-tuple-element.50.x_ref, f32[1024,1]{1,0:T(8,128)} %copy.39.scale_one_ref, f32[1024,1]{1,0:T(8,128)} %copy.40.scale_mid_ref, f32[1024,128]{1,0:T(8,128)} %get-tuple-element.73.cos_ref, ...), custom_call_target="tpu_custom_call" | custom-call | tf_op jit(solution)/shard_map/tail_sum/pallas_call | solution.py:640
  837.4 0.9 reduce_sum.63
  838.4 0.8 reduce_sum.65
  839.5 1.6 dynamic_update_slice.3
  841.2 0.7 reduce-scatter.12.cloned.1.call-update
  841.9 0.7 reduce-scatter.8.cloned.1.call-update
  842.7 0.5 reduce-scatter.10.cloned.1.call-update
  843.2 0.5 reduce-scatter.14.cloned.1.call-update
  843.8 104.0 %line_sum.1 = bf16[512,2048]{1,0:T(8,128)(2,1)} custom-call(f32[512,2048]{1,0:T(8,128)} %get-tuple-element.47.x_ref), custom_call_target="tpu_custom_call" | custom-call | tf_op jit(solution)/shard_map/line_sum/pallas_call | solution.py:182
  947.8 4.3 pad_maximum_fusion
  952.1 1.7 slice.43
  953.7 1.2 slice_bitcast_fusion.1
  954.9 1.3 slice_bitcast_fusion
  956.3 1.5 fusion.29
  957.8 80.1 %reduce-scatter.12.cloned.1.call-done = f32[512,1408]{1,0:T(8,128)} async-done(((f32[4096,1408]{1,0:T(8,128)}), f32[512,1408]{1,0:T(8,128)}) %reduce-scatter.12.cloned.1.call-update) | async-done | bytes 2883600 | tf_op jit(solution)/shard_map/reduce_scatter | solution.py:1031
  1037.9 3.6 fusion.28
  1041.4 51.6 %reduce-scatter.8.cloned.1.call-done = f32[128,1024]{1,0:T(8,128)} async-done(((f32[1024,1024]{1,0:T(8,128)}), f32[128,1024]{1,0:T(8,128)}) %reduce-scatter.8.cloned.1.call-update) | async-done | bytes 524304 | tf_op jit(solution)/shard_map/reduce_scatter | solution.py:1058
  1093.0 75.2 %reduce-scatter.10.cloned.1.call-done = f32[1024,256]{1,0:T(8,128)} async-done(((f32[1024,2048]{1,0:T(8,128)}), f32[1024,256]{1,0:T(8,128)}) %reduce-scatter.10.cloned.1.call-update) | async-done | bytes 1048592 | tf_op jit(solution)/shard_map/reduce_scatter | solution.py:1038
  1168.3 90.8 %reduce-scatter.14.cloned.1.call-done = f32[1408,256]{1,0:T(8,128)} async-done(((f32[1408,2048]{1,0:T(8,128)}), f32[1408,256]{1,0:T(8,128)}) %reduce-scatter.14.cloned.1.call-update) | async-done | bytes 1441808 | tf_op jit(solution)/shard_map/reduce_scatter | solution.py:1034
  1259.0 4.8 copy.44
  (74 shorter events, 0.7 us)
Async XLA Ops:
  7.2 3.3 copy-start.15
  7.2 944.9 %reduce-scatter.6.cloned.1.call-start = ((), (), s32[]{:S(2)}) async-start(), calls=%async_computation.5 | async-start | bytes 3981312 | tf_op jit(solution)/shard_map/reduce_scatter | solution.py:1096
  7.2 3.5 copy-start
  10.7 656.5 %copy-start.13 = (f32[2048]{0:T(1024)}, f32[2048]{0:T(1024)S(1)}, u32[]{:S(2)}) copy-start(f32[2048]{0:T(1024)S(1)} %convert_element_type.37) | copy-start | bytes 24580
  17.4 2.4 copy-start.17
  17.4 2.4 copy-start.9
  19.8 641.4 %copy-start.14 = (f32[1024]{0:T(1024)}, f32[1024]{0:T(1024)S(1)}, u32[]{:S(2)}) copy-start(f32[1024]{0:T(1024)S(1)} %convert_element_type.39) | copy-start | bytes 12292
  19.8 2.3 copy-start.10
  22.1 2.1 copy-start.18
  22.1 3.3 copy-start.16
  22.1 9.1 copy-start.7
  24.4 11.2 copy-start.12
  24.6 6.6 copy-start.1
  35.6 234.6 %slice-start = ((s8[5767168]{0:T(1024)(128)(4,1)}), s8[1572864]{0:T(1024)(128)(4,1)S(1)}, s32[]{:S(2)}) async-start(s8[5767168]{0:T(1024)(128)(4,1)} %bitcast.38), calls=%async_computation.10 | async-start | bytes 3145728
  258.3 11.9 slice-start.1
  258.3 11.9 copy-start.3
  270.2 8.7 copy-start.4
  270.2 23.0 %slice-start.2 = ((s8[5767168]{0:T(1024)(128)(4,1)}), s8[1572864]{0:T(1024)(128)(4,1)S(1)}, s32[]{:S(2)}) async-start(s8[5767168]{0:T(1024)(128)(4,1)} %bitcast.54), calls=%async_computation.12 | async-start | bytes 3145728
  278.9 14.2 %slice-start.3 = ((s8[5767168]{0:T(1024)(128)(4,1)}), s8[4194304]{0:T(1024)(128)(4,1)S(1)}, s32[]{:S(2)}) async-start(s8[5767168]{0:T(1024)(128)(4,1)} %bitcast.54), calls=%async_computation.13 | async-start | bytes 8388608
  293.2 8.9 copy-start.5
  293.2 8.9 copy-start.6
  528.0 9.5 copy-start.19
  528.0 9.5 copy-start.20
  544.3 116.9 %copy-start.2 = (f32[1024,1024]{1,0:T(8,128)S(1)}, f32[1024,1024]{1,0:T(8,128)}, u32[]{:S(2)}) copy-start(f32[1024,1024]{1,0:T(8,128)} %broadcast_multiply_fusion.unit_hbm) | copy-start | bytes 12582916
  674.8 164.4 %copy-start.11 = (f32[8,2048]{1,0:T(8,128)S(1)}, f32[8,2048]{1,0:T(8,128)}, u32[]{:S(2)}) copy-start(f32[8,2048]{1,0:T(8,128)} %get-tuple-element.55) | copy-start | bytes 196612
  841.1 196.8 %reduce-scatter.12.cloned.1.call-start = ((), (), s32[]{:S(2)}) async-start(), calls=%async_computation.8 | async-start | bytes 25952256 | tf_op jit(solution)/shard_map/reduce_scatter | solution.py:1031
  841.9 251.1 %reduce-scatter.8.cloned.1.call-start = ((), (), s32[]{:S(2)}) async-start(), calls=%async_computation.6 | async-start | bytes 4718592 | tf_op jit(solution)/shard_map/reduce_scatter | solution.py:1058
  842.6 325.6 %reduce-scatter.10.cloned.1.call-start = ((), (), s32[]{:S(2)}) async-start(), calls=%async_computation.7 | async-start | bytes 9437184 | tf_op jit(solution)/shard_map/reduce_scatter | solution.py:1038
  843.2 415.8 %reduce-scatter.14.cloned.1.call-start = ((), (), s32[]{:S(2)}) async-start(), calls=%async_computation.9 | async-start | bytes 12976128 | tf_op jit(solution)/shard_map/reduce_scatter | solution.py:1034
  843.8 104.0 %copy-start.8 = (bf16[512,2048]{1,0:T(8,128)(2,1)S(1)}, bf16[512,2048]{1,0:T(8,128)(2,1)}, u32[]{:S(2)}) copy-start(bf16[512,2048]{1,0:T(8,128)(2,1)} %get-tuple-element.46) | copy-start | bytes 6291460
Sparse Core Ops, SparseCore 0:
  841.3 46.5 reduce-scatter.5
  891.5 146.3 reduce-scatter.11
  1041.8 51.1 reduce-scatter.7
  1096.9 71.2 reduce-scatter.9
  1172.2 86.8 reduce-scatter.13

commit v7 on v6

--- a/solution.py
+++ b/solution.py
@@ -1,4 +1,5 @@
 import functools
+import math
 
 import jax
 import jax.numpy as jnp
@@ -250,7 +251,6 @@
     tile = min(256, rows // 2)
     by_units = units % 128 == 0 and units >= tile
     tall_count = -(-units // tile) if by_units else width // tile
-    row_blocks = rows // tile
     loads = [
         pltpu.make_async_copy(src, dst, load_sem.at[i])
         for i, (src, dst) in enumerate(
@@ -283,16 +283,20 @@
                 row_tile.at[0:tile], grad_down_ref.at[tall_at(t)], row_sem.at[0]
             )
         return pltpu.make_async_copy(
-            row_tile.at[0:units, 0:tile], grad_down_ref.at[:, block(t)], row_sem.at[0]
+            row_tile.at[0:units, 0:tile], grad_down_ref.at[0:units, block(t)], row_sem.at[0]
         )
 
+    def out_block(t):
+        return pl.ds(pl.multiple_of(t * out_tile, out_tile), out_tile)
+
     def out_copy(dst, t):
-        return pltpu.make_async_copy(row_tile.at[0:tile], dst.at[block(t)], row_sem.at[0])
-
-    half_blocks = row_blocks // 2
+        return pltpu.make_async_copy(row_tile.at[0:out_tile], dst.at[out_block(t)], row_sem.at[0])
+
+    out_tile = base_tile.shape[0]
+    out_counts = (one_ref.shape[0] // out_tile, two_ref.shape[0] // out_tile)
     tall_from = 2 * wide_count
     out_from = tall_from + tall_count
-    job_count = out_from + row_blocks
+    job_count = out_from + sum(out_counts)
 
     def job(j, carry):
         @pl.when(j == 0)
@@ -333,9 +337,10 @@
             tall_copy(t).start()
 
         for side, dst in enumerate((one_ref, two_ref)):
-            t = j - out_from - side * half_blocks
-
-            @pl.when((t >= 0) & (t < half_blocks))
+            begin = side * out_counts[0]
+            t = j - out_from - begin
+
+            @pl.when((t >= 0) & (t < out_counts[side]))
             def _():
                 @pl.when(t > 0)
                 def _():
@@ -346,14 +351,14 @@
                     if side == 0:
                         tall_copy(tall_count - 1).wait()
                     else:
-                        out_copy(one_ref, half_blocks - 1).wait()
+                        out_copy(one_ref, out_counts[0] - 1).wait()
 
                 base = pltpu.make_async_copy(
-                    hidden_hbm.at[block(t + side * half_blocks)], base_tile, base_sem.at[0]
+                    hidden_hbm.at[out_block(t + begin)], base_tile, base_sem.at[0]
                 )
                 base.start()
-                row_tile[0:tile, :] = jnp.dot(
-                    act_ref[block(t + side * half_blocks), :],
+                row_tile[0:out_tile, :] = jnp.dot(
+                    act_ref[out_block(t + begin), :],
                     down_ref[...],
                     preferred_element_type=jnp.float32,
                 )
@@ -361,7 +366,7 @@
 
                 @pl.when(me == 0)
                 def _():
-                    row_tile[0:tile, :] += base_tile[...]
+                    row_tile[0:out_tile, :] += base_tile[...]
 
                 out_copy(dst, t).start()
 
@@ -432,10 +437,10 @@
             for item in puts(half, c):
                 item.wait()
     wide_copy(1, wide_count - 1).wait()
-    out_copy(two_ref, half_blocks - 1).wait()
-
-
-def mid_sum(x, scale, gain, mid, act, d_gate, d_up, cot, w_down, hidden, axis, n, parts, cid):
+    out_copy(two_ref, out_counts[1] - 1).wait()
+
+
+def mid_sum(x, scale, gain, mid, act, d_gate, d_up, cot, w_down, hidden, more, axis, n, parts, cid):
     rows, width = x.shape
     units = act.shape[1]
     tile = min(256, rows // 2)
@@ -451,9 +456,9 @@
             jax.ShapeDtypeStruct(x.shape, jnp.bfloat16),
             jax.ShapeDtypeStruct((8, width), jnp.float32),
             jax.ShapeDtypeStruct((2 * width, units), jnp.float32),
-            jax.ShapeDtypeStruct((units, width), jnp.float32),
-            jax.ShapeDtypeStruct((rows // 2, width), jnp.float32),
-            jax.ShapeDtypeStruct((rows // 2, width), jnp.float32),
+            jax.ShapeDtypeStruct((units + more, width), jnp.float32),
+            jax.ShapeDtypeStruct((rows * 5 // 8, width), jnp.float32),
+            jax.ShapeDtypeStruct((rows - rows * 5 // 8, width), jnp.float32),
         ),
         in_specs=[vmem] * 3 + [anywhere] * 7,
         out_specs=(anywhere, anywhere, vmem) + (anywhere,) * 4,
@@ -462,7 +467,7 @@
         + [
             pltpu.VMEM((width // parts, units), jnp.float32),
             pltpu.VMEM((tall, width), jnp.float32),
-            pltpu.VMEM((tile, width), jnp.float32),
+            pltpu.VMEM((rows // 8, width), jnp.float32),
             pltpu.VMEM((2, 2, rows // (2 * chunks), width), jnp.float32),
             pltpu.VMEM((2, 2, rows // (2 * chunks), width), jnp.float32),
             pltpu.VMEM((2, 2, rows // (2 * chunks), width), jnp.bfloat16),
@@ -495,7 +500,9 @@
     down_hbm,
     key_hbm,
     val_hbm,
-    own_hbm,
+    pick_hbm,
+    q_hbm,
+    dq_hbm,
     input_hbm,
     hidden_hbm,
     grad_hbm,
@@ -508,6 +515,9 @@
     down_ref,
     key_ref,
     val_ref,
+    pick_ref,
+    q_ref,
+    dq_ref,
     own_in_ref,
     input_ref,
     hidden_ref,
@@ -533,7 +543,9 @@
                 (down_hbm, down_ref),
                 (key_hbm, key_ref),
                 (val_hbm, val_ref),
-                (own_hbm, own_in_ref),
+                (pick_hbm, pick_ref),
+                (q_hbm, q_ref),
+                (dq_hbm, dq_ref),
             )
         )
     ]
@@ -541,7 +553,29 @@
         load.start()
     acc_one_ref[...] = jnp.zeros_like(acc_one_ref)
     acc_mid_ref[...] = jnp.zeros_like(acc_mid_ref)
-    own_ref[...] = jnp.zeros_like(own_ref)
+    parts, all_rows, group = own_ref.shape
+    own_groups = x_ref.shape[1] // group
+    up_groups = dq_ref.shape[1] // group
+    up_rows = q_ref.shape[1] // parts
+    kept = (all_rows - up_groups * up_rows) // own_groups
+    used = own_in_ref.shape[1] // parts
+    for part in range(parts):
+        for g in range(own_groups):
+            own_ref[part, g * kept + used : (g + 1) * kept, :] = jnp.zeros(
+                (kept - used, group), jnp.float32
+            )
+    up_tile = max(128, up_rows)
+    up_count = q_ref.shape[1] // up_tile
+
+    def up_job(t):
+        cols = pl.ds(pl.multiple_of(t * up_tile, up_tile), up_tile)
+        value = left_dot(q_ref[:, cols], dq_ref[...])
+        for i in range(up_tile // up_rows):
+            for g in range(up_groups):
+                at = own_groups * kept + g * up_rows
+                own_ref[t * (up_tile // up_rows) + i, at : at + up_rows, :] = value[
+                    i * up_rows : (i + 1) * up_rows, g * group : (g + 1) * group
+                ]
 
     def store(own):
         return pltpu.make_async_copy(grad_ref, grad_hbm.at[own], store_sem.at[0])
@@ -579,6 +613,10 @@
         take_hidden.wait()
         scale_one = scale_one_ref[own, :]
         normed = input_ref[...].astype(jnp.float32) * scale_one
+        low_in = (normed * gain_one_ref[...]).astype(jnp.bfloat16)
+        own_in_ref[own, :] = jnp.dot(
+            low_in, pick_ref[...], preferred_element_type=jnp.float32
+        ).astype(jnp.bfloat16)
         acc_one_ref[...] += fold_rows(d_in * normed)
         e_in = d_in * gain_one_ref[...]
         mean_one = jnp.mean(e_in * normed, axis=1, keepdims=True)
@@ -594,6 +632,10 @@
             for load in loads:
                 load.wait()
 
+        @pl.when((s >= lag) & (s < lag + up_count))
+        def _():
+            up_job(s - lag)
+
         for half in (0, 1):
             back = me if half == 0 else (n - 1 - me)
             c = s - lag * (n - 1) - lag * back
@@ -604,10 +646,11 @@
 
     line_steps(axis, n, chunks, lag, x_ref, held, red, sems, lambda at: None, after_step)
     grads = left_dot(own_in_ref[...], low_ref[...])
-    parts, _, _ = own_ref.shape
-    kept = grads.shape[0] // parts
     for part in range(parts):
-        own_ref[part, 0:kept, :] = grads[part * kept : (part + 1) * kept]
+        for g in range(own_groups):
+            own_ref[part, g * kept : g * kept + used, :] = grads[
+                part * used : (part + 1) * used, g * group : (g + 1) * group
+            ]
 
 
 def tail_sum(
@@ -622,7 +665,9 @@
     q_down,
     k_proj,
     v_proj,
-    own_in,
+    pick,
+    q_normed,
+    d_q,
     block_input,
     d_hidden,
     axis,
@@ -633,23 +678,26 @@
     rows, width = block_input.shape
     block = min(128, rows // 2)
     chunks = chunk_count(rows, 32, 8)
-    kept = -(-(own_in.shape[1] // parts) // 8) * 8 + 8
+    kept = -(-(pick.shape[1] // parts) // 8) * 8 + 8
+    group = math.gcd(x.shape[1], d_q.shape[1])
+    all_rows = x.shape[1] // group * kept + d_q.shape[1] // group * (q_normed.shape[1] // parts)
     vmem = pl.BlockSpec(memory_space=pltpu.VMEM)
     anywhere = pl.BlockSpec(memory_space=pl.ANY)
-    loaded = (unit, q_down, k_proj, v_proj, own_in)
+    loaded = (unit, q_down, k_proj, v_proj, pick, q_normed, d_q)
     return pl.pallas_call(
         functools.partial(tail_kernel, axis, n, chunks, 2, block),
         out_shape=(
             jax.ShapeDtypeStruct((rows, width), jnp.bfloat16),
-            jax.ShapeDtypeStruct((parts, kept, x.shape[1]), jnp.float32),
+            jax.ShapeDtypeStruct((parts, all_rows, group), jnp.float32),
             jax.ShapeDtypeStruct((8, width), jnp.float32),
             jax.ShapeDtypeStruct((8, unit.shape[1]), jnp.float32),
         ),
-        in_specs=[vmem] * 7 + [anywhere] * 7,
+        in_specs=[vmem] * 7 + [anywhere] * 9,
         out_specs=(anywhere, vmem, vmem, vmem),
         scratch_shapes=[pltpu.VMEM(x.shape, jnp.float32)] * 2
         + [pltpu.VMEM(item.shape, item.dtype) for item in loaded]
         + [
+            pltpu.VMEM((rows, pick.shape[1]), jnp.bfloat16),
             pltpu.VMEM((block, width), jnp.bfloat16),
             pltpu.VMEM((block, width), jnp.float32),
             pltpu.VMEM((block, width), jnp.bfloat16),
@@ -817,8 +865,6 @@
     seq_len,
     block,
     x_ref,
-    q_ref,
-    dm_ref,
     k_ref,
     v_ref,
     norm_ref,
@@ -826,12 +872,27 @@
     all_ref,
     cos_ref,
     sin_ref,
-    up_ref,
+    q_hbm,
+    low_hbm,
+    proj_hbm,
+    up_hbm,
+    mixed_hbm,
+    grads_hbm,
     o_ref,
     dq_ref,
     sums_ref,
+    grads_ref,
     red,
     held,
+    q_ref,
+    low_ref,
+    proj_ref,
+    up_ref,
+    mixed_ref,
+    dm_ref,
+    row_tile,
+    load_sem,
+    row_sem,
     *sems,
 ):
     rows, head_dim = k_ref.shape
@@ -842,20 +903,56 @@
     rank = up_ref.shape[0]
     key_cols = slice(rank, rank + head_dim)
     val_cols = slice(rank + head_dim, rank + 2 * head_dim)
+    loads = [
+        pltpu.make_async_copy(src, dst, load_sem.at[i])
+        for i, (src, dst) in enumerate(
+            (
+                (low_hbm, low_ref),
+                (proj_hbm, proj_ref),
+                (q_hbm, q_ref),
+                (up_hbm, up_ref),
+                (mixed_hbm, mixed_ref),
+            )
+        )
+    ]
+    for load in loads:
+        load.start()
     sums_ref[:, rank:] = jnp.zeros((rows, 2 * head_dim), jnp.float32)
+    tile = row_tile.shape[0]
+    tile_count = mixed_ref.shape[1] // tile
+    grads_at = grads_ref.shape[0] - mixed_ref.shape[1]
 
     def finish(at):
         o_ref[at] = held[at].astype(o_ref.dtype)
 
+    def put(t):
+        to = pl.ds(pl.multiple_of(grads_at + t * tile, 8), tile)
+        return pltpu.make_async_copy(row_tile, grads_ref.at[to], row_sem.at[0])
+
+    turns = heads + 1
+    tiles_from = turns * (rows // block)
+    job_count = tiles_from + tile_count
+
     def job(j, carry):
-        head = lax.rem(j, heads)
-        row_block = lax.div(j, heads)
+        @pl.when(j == 0)
+        def _():
+            for load in loads:
+                load.wait()
+
+        turn = lax.rem(j, turns)
+        head = jnp.maximum(turn - 1, 0)
+        row_block = jnp.minimum(lax.div(j, turns), rows // block - 1)
+        in_blocks = j < tiles_from
         seq = lax.div(row_block, blocks)
         block_at = lax.rem(row_block, blocks)
         own = pl.ds(pl.multiple_of(row_block * block, block), block)
         cols = pl.ds(pl.multiple_of(head * head_dim, head_dim), head_dim)
         low_cols = pl.ds(pl.multiple_of(head * head_dim, half_dim), half_dim)
         high_cols = pl.ds(pl.multiple_of(head * head_dim + half_dim, half_dim), half_dim)
+
+        @pl.when(in_blocks & (turn == 0))
+        def _():
+            dm_ref[own, :] = right_dot(low_ref[own, :], proj_ref[...]).astype(dm_ref.dtype)
 
         def run(reach):
             keys = pl.ds(pl.multiple_of(seq * seq_len, seq_len), reach)
@@ -888,44 +985,87 @@
             first = reaches.index(reach)
             last = first + reaches.count(reach) - 1
 
-            @pl.when((block_at >= first) & (block_at <= last))
+            @pl.when(in_blocks & (turn > 0) & (block_at >= first) & (block_at <= last))
             def _():
                 run(reach)
 
-        @pl.when(head == heads - 1)
+        @pl.when(in_blocks & (turn == heads))
         def _():
             sums_ref[own, 0:rank] = right_dot(dq_ref[own, :], up_ref[...])
 
+        @pl.when(j >= tiles_from)
+        def _():
+            t = j - tiles_from
+
+            @pl.when(t > 0)
+            def _():
+                put(t - 1).wait()
+
+            part = pl.ds(pl.multiple_of(t * tile, tile), tile)
+            row_tile[...] = left_dot(mixed_ref[:, part], low_ref[...])
+            put(t).start()
+
         return carry
 
-    job_count = heads * (rows // block)
-
     def after_step(s, steps):
-        lax.fori_loop(s * job_count // steps, (s + 1) * job_count // steps, job, 0)
+        late = steps - 2
+        bounds = tuple(jnp.clip(at - 1, 0, late) * job_count // late for at in (s, s + 1))
+        lax.fori_loop(*bounds, job, 0)
 
     line_steps(axis, n, chunks, lag, x_ref, held, red, sems, finish, after_step)
+    put(tile_count - 1).wait()
 
 
 def attend_back(
-    x, q, dm, k, v, norm, own_ids, all_ids, cos_tab, sin_tab, q_up, axis, n, seq_len, cid
+    x,
+    k,
+    v,
+    norm,
+    own_ids,
+    all_ids,
+    cos_tab,
+    sin_tab,
+    q,
+    d_low,
+    out_proj,
+    q_up,
+    mixed,
+    grads,
+    axis,
+    n,
+    seq_len,
+    cid,
 ):
     chunks = chunk_count(x.shape[0], 32, 16)
-    block = min(256, seq_len)
+    block = min(128, seq_len)
     vmem = pl.BlockSpec(memory_space=pltpu.VMEM)
+    anywhere = pl.BlockSpec(memory_space=pl.ANY)
+    loaded = (q, d_low, out_proj, q_up, mixed)
     return pl.pallas_call(
         functools.partial(attend_back_kernel, axis, n, chunks, 2, seq_len, block),
         out_shape=(
             jax.ShapeDtypeStruct(x.shape, jnp.bfloat16),
             jax.ShapeDtypeStruct(q.shape, jnp.bfloat16),
             jax.ShapeDtypeStruct((k.shape[0], q_up.shape[0] + 2 * k.shape[1]), jnp.float32),
+            jax.ShapeDtypeStruct(grads.shape, grads.dtype),
         ),
-        in_specs=[vmem] * 11,
-        out_specs=(vmem, vmem, vmem),
+        in_specs=[vmem] * 8 + [anywhere] * 6,
+        out_specs=(vmem, vmem, vmem, anywhere),
+        input_output_aliases={13: 3},
         scratch_shapes=[pltpu.VMEM(x.shape, x.dtype)] * 2
+        + [pltpu.VMEM(item.shape, item.dtype) for item in loaded]
+        + [
+            pltpu.VMEM(q.shape, jnp.bfloat16),
+            pltpu.VMEM((min(256, q.shape[1]), d_low.shape[1]), jnp.float32),
+            pltpu.SemaphoreType.DMA((len(loaded),)),
+            pltpu.SemaphoreType.DMA((1,)),
+        ]
         + [pltpu.SemaphoreType.DMA((2, chunks))] * 4,
-        compiler_params=line_params(cid),
+        compiler_params=pltpu.CompilerParams(
+            collective_id=cid, has_side_effects=True, vmem_limit_bytes=61 << 20
+        ),
         name="attend_back",
-    )(x, q, dm, k, v, norm, own_ids, all_ids, cos_tab, sin_tab, q_up)
+    )(x, k, v, norm, own_ids, all_ids, cos_tab, sin_tab, *loaded, grads)
 
 
 def shards(
@@ -1012,7 +1152,7 @@
     d_gate = (d_act * up_pre * gate_sig * (1.0 + gate_pre * (1.0 - gate_sig))).astype(jnp.bfloat16)
     d_up = (d_act * gate_pre * gate_sig).astype(jnp.bfloat16)
     d_mid_part = right_dot(d_gate, w_gate) + right_dot(d_up, w_up)
-    d_hidden, d_hidden_low, acc_two, grad_wide, grad_down, out_part_one, out_part_two = mid_sum(
+    d_hidden, d_hidden_low, acc_two, grad_wide, grad_rows, out_part_one, out_part_two = mid_sum(
         d_mid_part,
         scale_two,
         gain_mlp.reshape(1, -1),
@@ -1023,6 +1163,7 @@
         d_output,
         w_down,
         hidden_in,
+        out_proj.shape[0],
         "tensor",
         tp_count,
         dp_count,
@@ -1031,15 +1172,8 @@
     grad_wide = lax.psum_scatter(grad_wide, "dp", scatter_dimension=0, tiled=True)
     grad_gate = grad_wide[: grad_wide.shape[0] // 2]
     grad_up = grad_wide[grad_wide.shape[0] // 2 :]
-    grad_down = lax.psum_scatter(grad_down, "dp", scatter_dimension=1, tiled=True)
-    grad_out = left_dot(mixed_heads, d_hidden_low)
-    d_mixed = right_dot(d_hidden_low, out_proj).astype(jnp.bfloat16)
-    out_part_one, grad_out = lax.optimization_barrier((out_part_one, grad_out))
-    grad_out = lax.psum_scatter(grad_out, "dp", scatter_dimension=1, tiled=True)
-    output_one, d_q_raw, query_key_val = attend_back(
+    output_one, d_q_raw, query_key_val, grad_rows = attend_back(
         out_part_one,
-        queries,
-        d_mixed,
         key_rows,
         val_rows,
         log_norm,
@@ -1047,20 +1181,24 @@
         all_ids,
         cos_all,
         sin_all,
+        queries,
+        d_hidden_low,
+        out_proj,
         q_up,
+        mixed_heads,
+        grad_rows,
         "tensor",
         tp_count,
         seq_len,
         3,
     )
-    grad_query_up = left_dot(q_normed, d_q_raw)
-    query_key_val, grad_query_up = lax.optimization_barrier((query_key_val, grad_query_up))
-    grad_query_up = lax.psum_scatter(grad_query_up, "dp", scatter_dimension=0, tiled=True)
+    grad_rows = lax.psum_scatter(grad_rows, "dp", scatter_dimension=1, tiled=True)
+    grad_down = grad_rows[: w_down.shape[0]]
+    grad_out = grad_rows[w_down.shape[0] :]
     own_width = model_width // (dp_count * tp_count)
     own_at = jnp.arange(model_width // tp_count)
     own_at = (own_at // own_width * tp_count + tp_index) * own_width + own_at % own_width
     pick = (jnp.arange(model_width)[:, None] == own_at[None, :]).astype(jnp.bfloat16)
-    own_in = jnp.dot(normed_in, pick, preferred_element_type=jnp.float32).astype(jnp.bfloat16)
     grad_input, own_grads, acc_one, acc_mid = tail_sum(
         query_key_val,
         scale_one,
@@ -1073,7 +1211,9 @@
         q_down,
         k_proj,
         v_proj,
-        own_in,
+        pick,
+        q_normed,
+        d_q_raw,
         block_input,
         d_hidden,
         "tensor",
@@ -1090,15 +1230,26 @@
         axis=1,
     )
     kept = own_width
-    gain_row = own_grads.shape[1] - 8
+    group_rows = -(-kept // 8) * 8 + 8
+    gain_row = group_rows - 8
     own_grads = lax.dynamic_update_slice(own_grads, gains[:, None, :], (0, gain_row, 0))
-    own_grads = own_grads.reshape(-1, own_grads.shape[2])
+    group = own_grads.shape[2]
+    own_grads = own_grads.reshape(-1, group)
     own_sum = lax.psum_scatter(own_grads, "dp", scatter_dimension=0, tiled=True)
     rank = q_down.shape[1]
     own_mid = rank // (dp_count * tp_count)
-    grad_qd = own_sum[:kept, :rank]
-    grad_key = own_sum[:kept, rank : rank + head_dim]
-    grad_val = own_sum[:kept, rank + head_dim :]
+    own_groups = (rank + 2 * head_dim) // group
+    own_rows = jnp.concatenate(
+        [own_sum[g * group_rows : g * group_rows + kept] for g in range(own_groups)], axis=1
+    )
+    up_rows = rank // dp_count
+    grad_query_up = jnp.concatenate(
+        [own_sum[at : at + up_rows] for at in range(own_groups * group_rows, own_sum.shape[0], up_rows)],
+        axis=1,
+    )
+    grad_qd = own_rows[:, :rank]
+    grad_key = own_rows[:, rank : rank + head_dim]
+    grad_val = own_rows[:, rank + head_dim :]
     grad_g1 = own_sum[gain_row, :kept]
     grad_g2 = own_sum[gain_row, kept : 2 * kept]
     grad_gq = own_sum[gain_row, 2 * kept : 2 * kept + own_mid]

time: 1280 us -> 1210 us (0.945)
  waiting for transfers between devices: 300 us -> 255 us
  matrix products: 99.2 us -> 70.6 us
    reduce_scatter x3 -> x1, waiting for transfers between devices: 218 us -> 109 us  [shards(): lax.psum_scatter(grad_rows, 'dp', scatter_dimension=1, tiled=True)]
    reduce_scatter x1, waiting for transfers between devices: 80.1 us -> 145 us  [shards(): lax.psum_scatter(grad_wide, 'dp', scatter_dimension=0, tiled=True)]
    pallas_call x1, Pallas kernels: 117 us -> 147 us  [attend_back(): pl.pallas_call(functools.partial(attend_back_kernel, axis, n, chunks, 2,...]
    pallas_call x1, Pallas kernels: 104 us -> 79.2 us  [line_sum(): pl.pallas_call(functools.partial(line_low_kernel, axis, n, chunks, 2), ou...]
    dot_general x3 -> x0, matrix products: 18.3 us -> none  [the longest x2 12.7 us: left_dot(): lax.dot_general(left, right, (((0,), (0,)), ((), ())), preferred_element_...]
    dot_general x4 -> x3, matrix products: 39.6 us -> 30.3 us  [right_dot(): lax.dot_general(left, right, (((1,), (1,)), ((), ())), preferred_element_...]
  transfers between devices with their start and end apart: 5 -> 3, of which waited for: 4 -> 2; matrix products, arithmetic and copies ran while one was open for 1% -> 1% of each run, Pallas kernels for 8% -> 7%
where the time goes in v7:
time: 1210 us
  Pallas kernels  817 us (68%)
  waiting for transfers between devices  255 us (21%)
  matrix products  70.6 us (6%)
  other arithmetic  25.7 us (2%)
  local copies, waits for them, and re-layouts  22.8 us (2%)
  between operations  14.3 us (1%)
    pallas_call x1, Pallas kernels, attend(): pl.pallas_call(functools.partial(attend_kernel, axis, n, chunks, 2, seq_l...  223 us
    pallas_call x1, Pallas kernels, mid_sum(): pl.pallas_call(functools.partial(mid_kernel, axis, n, chunks, 2), out_sha...  204 us
    pallas_call x1, Pallas kernels, tail_sum(): pl.pallas_call(functools.partial(tail_kernel, axis, n, chunks, 2, block),...  164 us
    pallas_call x1, Pallas kernels, attend_back(): pl.pallas_call(functools.partial(attend_back_kernel, axis, n, chunks, 2,...  147 us
    reduce_scatter x1, waiting for transfers between devices, shards(): lax.psum_scatter(grad_wide, 'dp', scatter_dimension=0, tiled=True)  145 us
    reduce_scatter x1, waiting for transfers between devices, shards(): lax.psum_scatter(grad_rows, 'dp', scatter_dimension=1, tiled=True)  109 us
    pallas_call x1, Pallas kernels, line_sum(): pl.pallas_call(functools.partial(line_low_kernel, axis, n, chunks, 2), ou...  79.2 us
    dot_general x3, matrix products, right_dot(): lax.dot_general(left, right, (((1,), (1,)), ((), ())), preferred_element_...  30.3 us
  transfers between devices with their start and end apart: 3, of which 2 were waited for; matrix products, arithmetic and copies ran while one was open for 1% of the time, Pallas kernels for 7%

profile of v7, /device:TPU:0, one launch (start us, length us, event | category | flops | bytes accessed | tf_op | source)
XLA Modules:
  0.0 1205.8 jit_solution(2002482790613905130)
XLA Ops:
  7.3 0.8 convert_element_type.35
  8.1 0.9 convert_element_type.33
  9.0 3.1 fusion
  12.1 6.4 fusion.21
  18.5 0.3 multiply_reduce_fusion
  18.9 1.6 copy-done.10
  20.5 1.3 fusion.19
  21.9 2.1 convolution_convert_fusion.v_ref
  24.0 0.1 fusion.6
  24.1 0.2 copy.38
  24.3 0.8 compare_select_fusion.own_ref
  25.2 0.6 reshape.251
  25.8 4.9 multiply_convert_fusion.3
  30.6 4.4 fusion.28.raw_ref
  35.0 3.0 subtract_convert_fusion
  38.0 0.8 pad_maximum_fusion.1.k_ref
  38.8 223.0 %attend.1 = (f32[1024,2048]{1,0:T(8,128)}, bf16[1024,1024]{1,0:T(8,128)(2,1)}, bf16[1024,1024]{1,0:T(8,128)(2,1)}, f32[4,1024,1]{2,1,0:T(8,128)}, bf16[1024,2048]{1,0:T(8,128)(2,1)}, /*index=5*/f32[1024,1]{1,0:T(8,128)}) custom-call(f32[1024,1024]{1,0:T(8,128)} %fusion.28.raw_ref, bf16[1024,256]{1,0:T(8,128)(2,1)} %pad_maximum_fusion.1.k_ref, ...), custom_call_target="tpu_custom_call" | custom-call | tf_op jit(solution)/shard_map/attend/pallas_call | solution.py:839
  261.9 11.9 fusion.29
  273.8 8.7 fusion.27
  282.5 14.2 %multiply_convert_fusion = (bf16[1024,1408]{1,0:T(8,128)(2,1)}, bf16[1024,1408]{1,0:T(8,128)(2,1)S(1)}, bf16[1024,1408]{1,0:T(8,128)(2,1)S(1)}) fusion(f32[1024,1408]{1,0:T(8,128)} %fusion.29, f32[1024,1408]{1,0:T(8,128)} %fusion.27, bf16[1024,2048]{1,0:T(8,128)(2,1)S(1)} %copy-done.5, bf16[2048,1408]{1,0:T(8,128)(2,1)} %param.25), kind=kOutput, calls=%fused_computation.5 | convolution fusion | flops 5928648704 | bytes 30146560 | tf_op jit(solution)/shard_map/dot_general | solution.py:1148
  296.7 9.0 fusion.30
  305.7 1.1 copy.40.scale_one_ref
  306.8 1.0 copy.41.scale_mid_ref
  307.8 2.3 fusion.3.pick_hbm
  310.1 12.6 %convolution_add_fusion.x_ref = f32[1024,2048]{1,0:T(8,128)} fusion(f32[1024,2048]{1,0:T(8,128)} %fusion.30, bf16[1024,1408]{1,0:T(8,128)(2,1)S(1)} %get-tuple-element.59.up_hbm, bf16[2048,1408]{1,0:T(8,128)(2,1)} %param.25), kind=kOutput, calls=%fused_computation.14 | convolution fusion | flops 5907677184 | bytes 25427968 | tf_op jit(solution)/shard_map/dot_general | solution.py:33
  322.7 203.7 %mid_sum.1 = (f32[1024,2048]{1,0:T(8,128)}, bf16[1024,2048]{1,0:T(8,128)(2,1)}, f32[8,2048]{1,0:T(8,128)}, f32[4096,1408]{1,0:T(8,128)}, f32[2432,2048]{1,0:T(8,...) custom-call(f32[1024,2048]{1,0:T(8,128)} %convolution_add_fusion.x_ref, f32[1024,1]{1,0:T(8,128)} %get-tuple-element.35.scale_ref, ...), custom_call_target="tpu_custom_call" | custom-call | tf_op jit(solution)/shard_map/mid_sum/pallas_call | solution.py:452
  526.4 147.3 %attend_back.1 = (bf16[640,2048]{1,0:T(8,128)(2,1)}, bf16[1024,1024]{1,0:T(8,128)(2,1)}, f32[1024,1536]{1,0:T(8,128)}, f32[2432,2048]{1,0:T(8,128)}) custom-call(f32[640,2048]{1,0:T(8,128)} %get-tuple-element.37.x_ref, bf16[1024,256]{1,0:T(8,128)(2,1)} %pad_maximum_fusion.1.k_ref, ...), custom_call_target="tpu_custom_call", output_to_operand_aliasing={{3}: (13, {})} | custom-call | tf_op jit(solution)/shard_map/attend_back/pallas_call | solution.py:1044
  673.8 163.7 %tail_sum.1 = (bf16[1024,2048]{1,0:T(8,128)(2,1)}, f32[8,472,512]{2,1,0:T(8,128)}, f32[8,2048]{1,0:T(8,128)}, f32[8,1024]{1,0:T(8,128)}) custom-call(f32[1024,1536]{1,0:T(8,128)} %get-tuple-element.45.x_ref, f32[1024,1]{1,0:T(8,128)} %copy.40.scale_one_ref, f32[1024,1]{1,0:T(8,128)} %copy.41.scale_mid_ref, f32[1024,128]{1,0:T(8,128)} %get-tuple-element.73.cos_ref, ...), custom_call_target="tpu_custom_call" | custom-call | tf_op jit(solution)/shard_map/tail_sum/pallas_call | solution.py:687
  837.5 0.8 reduce_sum.65
  838.5 0.9 reduce_sum.63
  839.5 1.6 dynamic_update_slice.3
  841.2 0.7 reduce-scatter.6.cloned.1.call-update
  842.0 0.7 reduce-scatter.8.cloned.1.call-update
  842.7 79.2 %line_sum.1 = bf16[384,2048]{1,0:T(8,128)(2,1)} custom-call(f32[384,2048]{1,0:T(8,128)} %get-tuple-element.44.x_ref), custom_call_target="tpu_custom_call" | custom-call | tf_op jit(solution)/shard_map/line_sum/pallas_call | solution.py:183
  921.8 4.7 pad_maximum_fusion
  926.5 1.1 fusion.26
  927.6 0.7 pad_maximum_fusion.3
  928.3 1.3 fusion.25
  929.5 0.8 pad_maximum_fusion.2
  930.4 1.2 slice_bitcast_fusion.1
  931.6 1.3 slice_bitcast_fusion
  932.9 1.5 fusion.24
  934.4 108.9 %reduce-scatter.6.cloned.1.call-done = f32[2432,256]{1,0:T(8,128)} async-done(((f32[2432,2048]{1,0:T(8,128)}), f32[2432,256]{1,0:T(8,128)}) %reduce-scatter.6.cloned.1.call-update) | async-done | bytes 2490384 | tf_op jit(solution)/shard_map/reduce_scatter | solution.py:1195
  1043.3 2.3 slice.73
  1045.6 2.6 slice.77
  1048.1 145.2 %reduce-scatter.8.cloned.1.call-done = f32[512,1408]{1,0:T(8,128)} async-done(((f32[4096,1408]{1,0:T(8,128)}), f32[512,1408]{1,0:T(8,128)}) %reduce-scatter.8.cloned.1.call-update) | async-done | bytes 2883600 | tf_op jit(solution)/shard_map/reduce_scatter | solution.py:1172
  1193.3 3.7 fusion.23
  1197.0 2.0 copy.46
  (64 shorter events, 0.6 us)
Async XLA Ops:
  7.2 919.3 %reduce-scatter.4.cloned.1.call-start = ((), (), s32[]{:S(2)}) async-start(), calls=%async_computation.3 | async-start | bytes 8699904 | tf_op jit(solution)/shard_map/reduce_scatter | solution.py:1238
  7.2 4.8 copy-start
  8.1 17.7 %copy-start.14 = (f32[1024]{0:T(1024)}, f32[1024]{0:T(1024)S(1)}, u32[]{:S(2)}) copy-start(f32[1024]{0:T(1024)S(1)} %convert_element_type.35) | copy-start | bytes 12292
  9.0 12.8 %copy-start.15 = (f32[2048]{0:T(1024)}, f32[2048]{0:T(1024)S(1)}, u32[]{:S(2)}) copy-start(f32[2048]{0:T(1024)S(1)} %convert_element_type.33) | copy-start | bytes 24580
  18.5 3.3 copy-start.1
  18.5 2.0 copy-start.10
  20.5 1.3 copy-start.11
  21.8 2.1 copy-start.17
  21.8 3.3 copy-start.16
  24.1 6.6 copy-start.13
  25.8 4.9 copy-start.9
  30.6 4.4 copy-start.2
  38.8 234.9 %slice-start = ((s8[5767168]{0:T(1024)(128)(4,1)}), s8[1572864]{0:T(1024)(128)(4,1)S(1)}, s32[]{:S(2)}) async-start(s8[5767168]{0:T(1024)(128)(4,1)} %bitcast.35), calls=%async_computation.6 | async-start | bytes 3145728
  261.8 11.9 slice-start.1
  261.9 11.9 copy-start.4
  273.7 8.7 copy-start.5
  273.7 22.9 %slice-start.2 = ((s8[5767168]{0:T(1024)(128)(4,1)}), s8[4194304]{0:T(1024)(128)(4,1)S(1)}, s32[]{:S(2)}) async-start(s8[5767168]{0:T(1024)(128)(4,1)} %bitcast.50), calls=%async_computation.8 | async-start | bytes 8388608
  282.5 14.2 %slice-start.3 = ((s8[5767168]{0:T(1024)(128)(4,1)}), s8[1572864]{0:T(1024)(128)(4,1)S(1)}, s32[]{:S(2)}) async-start(s8[5767168]{0:T(1024)(128)(4,1)} %bitcast.50), calls=%async_computation.9 | async-start | bytes 3145728
  296.7 9.1 copy-start.6
  296.7 13.4 %copy-start.7 = (bf16[1024,1408]{1,0:T(8,128)(2,1)}, bf16[1024,1408]{1,0:T(8,128)(2,1)S(1)}, u32[]{:S(2)}) copy-start(bf16[1024,1408]{1,0:T(8,128)(2,1)S(1)} %get-tuple-element.59.up_hbm) | copy-start | bytes 8650756
  673.8 164.5 %copy-start.12 = (f32[8,2048]{1,0:T(8,128)S(1)}, f32[8,2048]{1,0:T(8,128)}, u32[]{:S(2)}) copy-start(f32[8,2048]{1,0:T(8,128)} %get-tuple-element.51) | copy-start | bytes 196612
  841.2 202.1 %reduce-scatter.6.cloned.1.call-start = ((), (), s32[]{:S(2)}) async-start(), calls=%async_computation.4 | async-start | bytes 22413312 | tf_op jit(solution)/shard_map/reduce_scatter | solution.py:1195
  841.9 351.4 %reduce-scatter.8.cloned.1.call-start = ((), (), s32[]{:S(2)}) async-start(), calls=%async_computation.5 | async-start | bytes 25952256 | tf_op jit(solution)/shard_map/reduce_scatter | solution.py:1172
  842.6 79.2 %copy-start.8 = (bf16[640,2048]{1,0:T(8,128)(2,1)S(1)}, bf16[640,2048]{1,0:T(8,128)(2,1)}, u32[]{:S(2)}) copy-start(bf16[640,2048]{1,0:T(8,128)(2,1)} %get-tuple-element.43) | copy-start | bytes 7864324
  1193.3 3.7 copy-start.3
Sparse Core Ops, SparseCore 0:
  841.3 67.3 reduce-scatter.3
  912.4 130.8 reduce-scatter.5
  1046.9 146.3 reduce-scatter.7

commit v8 on v7

--- a/solution.py
+++ b/solution.py
@@ -440,7 +440,7 @@
     out_copy(two_ref, out_counts[1] - 1).wait()
 
 
-def mid_sum(x, scale, gain, mid, act, d_gate, d_up, cot, w_down, hidden, more, axis, n, parts, cid):
+def mid_sum(x, scale, gain, mid, act, d_gate, d_up, cot, w_down, hidden, axis, n, parts, cid):
     rows, width = x.shape
     units = act.shape[1]
     tile = min(256, rows // 2)
@@ -456,7 +456,7 @@
             jax.ShapeDtypeStruct(x.shape, jnp.bfloat16),
             jax.ShapeDtypeStruct((8, width), jnp.float32),
             jax.ShapeDtypeStruct((2 * width, units), jnp.float32),
-            jax.ShapeDtypeStruct((units + more, width), jnp.float32),
+            jax.ShapeDtypeStruct((units, width), jnp.float32),
             jax.ShapeDtypeStruct((rows * 5 // 8, width), jnp.float32),
             jax.ShapeDtypeStruct((rows - rows * 5 // 8, width), jnp.float32),
         ),
@@ -728,19 +728,30 @@
     all_ref,
     cos_ref,
     sin_ref,
-    out_ref,
-    base_ref,
     gain_ref,
+    out_hbm,
+    down_hbm,
+    base_hbm,
+    cot_hbm,
     o_ref,
     q_ref,
     mixed_ref,
     norm_ref,
     normed_ref,
     scale_ref,
+    d_act_ref,
     part,
     red,
+    out_ref,
+    down_ref,
+    base_tile,
+    cot_tile,
+    act_tile,
+    load_sem,
+    tile_sem,
     *sems,
 ):
+    me = lax.axis_index(axis)
     rows, head_dim = k_ref.shape
     heads = raw_ref.shape[1] // head_dim
     half_dim = head_dim // 2
@@ -749,10 +760,48 @@
     pairs = rows // (2 * block)
     turns = heads + 1
     pair_jobs = 2 * turns
+    act_rows = cot_tile.shape[0]
+    act_count = rows // act_rows
+    out_load = pltpu.make_async_copy(out_hbm, out_ref, load_sem.at[0])
+    down_load = pltpu.make_async_copy(down_hbm, down_ref, load_sem.at[1])
+    out_load.start()
+    down_load.start()
+
+    def act_block(t):
+        return pl.ds(pl.multiple_of(t * act_rows, act_rows), act_rows)
+
+    def take_cot(t):
+        return pltpu.make_async_copy(cot_hbm.at[act_block(t)], cot_tile, tile_sem.at[0])
+
+    def put_act(t):
+        return pltpu.make_async_copy(act_tile, d_act_ref.at[act_block(t)], tile_sem.at[1])
+
+    take_cot(0).start()
+
+    def act_job(t, carry):
+        @pl.when(t == 0)
+        def _():
+            down_load.wait()
+
+        take_cot(t).wait()
+        value = right_dot(cot_tile[...], down_ref[...])
+
+        @pl.when(t + 1 < act_count)
+        def _():
+            take_cot(t + 1).start()
+
+        @pl.when(t > 0)
+        def _():
+            put_act(t - 1).wait()
+
+        act_tile[...] = value
+        put_act(t).start()
+        return carry
 
     def job(j, carry):
         pair = lax.div(j, pair_jobs)
-        side = lax.div(lax.rem(j, pair_jobs), turns)
+        turn_side = lax.div(lax.rem(j, pair_jobs), turns)
+        side = jnp.where(2 * me >= n, turn_side, 1 - turn_side)
         head = lax.rem(j, turns)
         row_block = side * pairs + pair
         seq = lax.div(row_block, blocks)
@@ -792,27 +841,43 @@
             def _():
                 run(reach)
 
+        @pl.when(j == heads)
+        def _():
+            out_load.wait()
+
         @pl.when(head == heads)
         def _():
+            base = pltpu.make_async_copy(base_hbm.at[own], base_tile, tile_sem.at[2])
+
+            @pl.when(me == 0)
+            def _():
+                base.start()
+
             part[own, :] = jnp.dot(
                 mixed_ref[own, :], out_ref[...], preferred_element_type=jnp.float32
             )
 
-        @pl.when((head == heads) & (lax.axis_index(axis) == 0))
-        def _():
-            part[own, :] += base_ref[own, :].astype(jnp.float32)
+            @pl.when(me == 0)
+            def _():
+                base.wait()
+                part[own, :] += base_tile[...].astype(jnp.float32)
 
         return carry
 
-    lax.fori_loop(0, pair_jobs, job, 0)
+    lax.fori_loop(0, turns, job, 0)
     pair_steps = chunks // pairs
 
     def after_step(s, steps):
         bounds = tuple(
-            jnp.minimum((pair_steps + at) * pair_jobs // pair_steps, pairs * pair_jobs)
+            jnp.minimum(turns + at * pair_jobs // pair_steps, pairs * pair_jobs)
             for at in (s, s + 1)
         )
         lax.fori_loop(*bounds, job, 0)
+        late = steps - chunks - 1
+        bounds = tuple(
+            jnp.clip(at - chunks, 0, late) * act_count // late for at in (s, s + 1)
+        )
+        lax.fori_loop(*bounds, act_job, 0)
 
     def finish(at):
         hidden = o_ref[at]
@@ -821,6 +886,7 @@
         normed_ref[at] = (hidden * scale_rows * gain_ref[...]).astype(normed_ref.dtype)
 
     line_steps(axis, n, chunks, lag, part, o_ref, red, sems, finish, after_step)
+    put_act(act_count - 1).wait()
 
 
 def reach_list(seq_len, block):
@@ -830,12 +896,30 @@
 
 
 def attend(
-    raw, k, v, own_ids, all_ids, cos_tab, sin_tab, out_proj, base, gain, axis, n, seq_len, cid
+    raw,
+    k,
+    v,
+    own_ids,
+    all_ids,
+    cos_tab,
+    sin_tab,
+    gain,
+    out_proj,
+    w_down,
+    base,
+    cot,
+    axis,
+    n,
+    seq_len,
+    cid,
 ):
     rows, width = base.shape
+    units = w_down.shape[0]
     block = min(64, seq_len)
+    act_rows = min(128, rows)
     chunks = chunk_count(rows, 32, 16)
     vmem = pl.BlockSpec(memory_space=pltpu.VMEM)
+    anywhere = pl.BlockSpec(memory_space=pl.ANY)
     return pl.pallas_call(
         functools.partial(attend_kernel, axis, n, chunks, 2, seq_len, block),
         out_shape=(
@@ -845,16 +929,39 @@
             jax.ShapeDtypeStruct((raw.shape[1] // k.shape[1], rows, 1), jnp.float32),
             jax.ShapeDtypeStruct((rows, width), jnp.bfloat16),
             jax.ShapeDtypeStruct((rows, 1), jnp.float32),
+            jax.ShapeDtypeStruct((rows, units), jnp.float32),
         ),
-        in_specs=[vmem] * 10,
-        out_specs=(vmem,) * 6,
+        in_specs=[vmem] * 8 + [anywhere] * 4,
+        out_specs=(vmem,) * 6 + (anywhere,),
         scratch_shapes=[pltpu.VMEM((rows, width), jnp.float32)] * 2
+        + [
+            pltpu.VMEM(out_proj.shape, out_proj.dtype),
+            pltpu.VMEM(w_down.shape, w_down.dtype),
+            pltpu.VMEM((block, width), base.dtype),
+            pltpu.VMEM((act_rows, width), cot.dtype),
+            pltpu.VMEM((act_rows, units), jnp.float32),
+            pltpu.SemaphoreType.DMA((2,)),
+            pltpu.SemaphoreType.DMA((3,)),
+        ]
         + [pltpu.SemaphoreType.DMA((2, chunks))] * 4,
         compiler_params=pltpu.CompilerParams(
-            collective_id=cid, has_side_effects=True, vmem_limit_bytes=60 << 20
+            collective_id=cid, has_side_effects=True, vmem_limit_bytes=62 << 20
         ),
         name="attend",
-    )(raw, k, v, own_ids, all_ids, cos_tab, sin_tab, out_proj, base, gain)
+    )(
+        raw,
+        k,
+        v,
+        own_ids,
+        all_ids,
+        cos_tab,
+        sin_tab,
+        gain,
+        out_proj,
+        w_down,
+        base,
+        cot,
+    )
 
 
 def attend_back_kernel(
@@ -877,7 +984,6 @@
     proj_hbm,
     up_hbm,
     mixed_hbm,
-    grads_hbm,
     o_ref,
     dq_ref,
     sums_ref,
@@ -920,13 +1026,12 @@
     sums_ref[:, rank:] = jnp.zeros((rows, 2 * head_dim), jnp.float32)
     tile = row_tile.shape[0]
     tile_count = mixed_ref.shape[1] // tile
-    grads_at = grads_ref.shape[0] - mixed_ref.shape[1]
 
     def finish(at):
         o_ref[at] = held[at].astype(o_ref.dtype)
 
     def put(t):
-        to = pl.ds(pl.multiple_of(grads_at + t * tile, 8), tile)
+        to = pl.ds(pl.multiple_of(t * tile, tile), tile)
         return pltpu.make_async_copy(row_tile, grads_ref.at[to], row_sem.at[0])
 
     turns = heads + 1
@@ -1030,7 +1135,6 @@
     out_proj,
     q_up,
     mixed,
-    grads,
     axis,
     n,
     seq_len,
@@ -1047,11 +1151,10 @@
             jax.ShapeDtypeStruct(x.shape, jnp.bfloat16),
             jax.ShapeDtypeStruct(q.shape, jnp.bfloat16),
             jax.ShapeDtypeStruct((k.shape[0], q_up.shape[0] + 2 * k.shape[1]), jnp.float32),
-            jax.ShapeDtypeStruct(grads.shape, grads.dtype),
+            jax.ShapeDtypeStruct((mixed.shape[1], d_low.shape[1]), jnp.float32),
         ),
-        in_specs=[vmem] * 8 + [anywhere] * 6,
+        in_specs=[vmem] * 8 + [anywhere] * 5,
         out_specs=(vmem, vmem, vmem, anywhere),
-        input_output_aliases={13: 3},
         scratch_shapes=[pltpu.VMEM(x.shape, x.dtype)] * 2
         + [pltpu.VMEM(item.shape, item.dtype) for item in loaded]
         + [
@@ -1065,7 +1168,7 @@
             collective_id=cid, has_side_effects=True, vmem_limit_bytes=61 << 20
         ),
         name="attend_back",
-    )(x, k, v, norm, own_ids, all_ids, cos_tab, sin_tab, *loaded, grads)
+    )(x, k, v, norm, own_ids, all_ids, cos_tab, sin_tab, *loaded)
 
 
 def shards(
@@ -1128,7 +1231,7 @@
         jnp.dot(normed_in, k_proj, preferred_element_type=jnp.float32), cos_all, sin_all
     ).astype(jnp.bfloat16)
     val_rows = jnp.dot(normed_in, v_proj, preferred_element_type=jnp.float32).astype(jnp.bfloat16)
-    hidden_in, queries, mixed_heads, log_norm, normed_mid, scale_two = attend(
+    hidden_in, queries, mixed_heads, log_norm, normed_mid, scale_two, d_act = attend(
         q_raw,
         key_rows,
         val_rows,
@@ -1136,9 +1239,11 @@
         all_ids,
         cos_all,
         sin_all,
+        gain_mlp.reshape(1, -1),
         out_proj,
+        w_down,
         block_input,
-        gain_mlp.reshape(1, -1),
+        d_output,
         "tensor",
         tp_count,
         seq_len,
@@ -1148,11 +1253,10 @@
     up_pre = jnp.dot(normed_mid, w_up, preferred_element_type=jnp.float32)
     gate_sig = jax.nn.sigmoid(gate_pre)
     hidden_act = (gate_pre * gate_sig * up_pre).astype(jnp.bfloat16)
-    d_act = right_dot(d_output, w_down)
     d_gate = (d_act * up_pre * gate_sig * (1.0 + gate_pre * (1.0 - gate_sig))).astype(jnp.bfloat16)
     d_up = (d_act * gate_pre * gate_sig).astype(jnp.bfloat16)
     d_mid_part = right_dot(d_gate, w_gate) + right_dot(d_up, w_up)
-    d_hidden, d_hidden_low, acc_two, grad_wide, grad_rows, out_part_one, out_part_two = mid_sum(
+    d_hidden, d_hidden_low, acc_two, grad_wide, grad_down, out_part_one, out_part_two = mid_sum(
         d_mid_part,
         scale_two,
         gain_mlp.reshape(1, -1),
@@ -1163,16 +1267,16 @@
         d_output,
         w_down,
         hidden_in,
-        out_proj.shape[0],
         "tensor",
         tp_count,
         dp_count,
         1,
     )
     grad_wide = lax.psum_scatter(grad_wide, "dp", scatter_dimension=0, tiled=True)
+    grad_down = lax.psum_scatter(grad_down, "dp", scatter_dimension=1, tiled=True)
     grad_gate = grad_wide[: grad_wide.shape[0] // 2]
     grad_up = grad_wide[grad_wide.shape[0] // 2 :]
-    output_one, d_q_raw, query_key_val, grad_rows = attend_back(
+    output_one, d_q_raw, query_key_val, grad_out = attend_back(
         out_part_one,
         key_rows,
         val_rows,
@@ -1186,15 +1290,12 @@
         out_proj,
         q_up,
         mixed_heads,
-        grad_rows,
         "tensor",
         tp_count,
         seq_len,
         3,
     )
-    grad_rows = lax.psum_scatter(grad_rows, "dp", scatter_dimension=1, tiled=True)
-    grad_down = grad_rows[: w_down.shape[0]]
-    grad_out = grad_rows[w_down.shape[0] :]
+    grad_out = lax.psum_scatter(grad_out, "dp", scatter_dimension=1, tiled=True)
     own_width = model_width // (dp_count * tp_count)
     own_at = jnp.arange(model_width // tp_count)
     own_at = (own_at // own_width * tp_count + tp_index) * own_width + own_at % own_width

time: 1210 us -> 1230 us (1.017)
  waiting for transfers between devices: 255 us -> 288 us
    reduce_scatter x1 -> x2, waiting for transfers between devices: 109 us -> 163 us  [the longest x1 90.8 us: shards(): lax.psum_scatter(grad_down, 'dp', scatter_dimension=1, tiled=True)]
    reduce_scatter x1, waiting for transfers between devices: 145 us -> 123 us  [shards(): lax.psum_scatter(grad_wide, 'dp', scatter_dimension=0, tiled=True)]
    dot_general x3 -> x2, matrix products: 30.3 us -> 21.8 us  [right_dot(): lax.dot_general(left, right, (((1,), (1,)), ((), ())), preferred_element_...]
  transfers between devices with their start and end apart: 3 -> 4, of which waited for: 2 -> 3; matrix products, arithmetic and copies ran while one was open for 1% -> 1% of each run, Pallas kernels for 7% -> 6%
where the time goes in v8:
time: 1230 us; the launch traced here: 1220 us
  Pallas kernels  811 us (66%)
  waiting for transfers between devices  288 us (23%)
  matrix products  61.5 us (5%)
  other arithmetic  22 us (2%)
  local copies, waits for them, and re-layouts  20.8 us (2%)
  between operations  14.5 us (1%)
    pallas_call x1, Pallas kernels, attend(): pl.pallas_call(functools.partial(attend_kernel, axis, n, chunks, 2, seq_l...  218 us
    pallas_call x1, Pallas kernels, mid_sum(): pl.pallas_call(functools.partial(mid_kernel, axis, n, chunks, 2), out_sha...  203 us
    pallas_call x1, Pallas kernels, tail_sum(): pl.pallas_call(functools.partial(tail_kernel, axis, n, chunks, 2, block),...  164 us
    pallas_call x1, Pallas kernels, attend_back(): pl.pallas_call(functools.partial(attend_back_kernel, axis, n, chunks, 2,...  147 us
    reduce_scatter x1, waiting for transfers between devices, shards(): lax.psum_scatter(grad_wide, 'dp', scatter_dimension=0, tiled=True)  123 us
    reduce_scatter x1, waiting for transfers between devices, shards(): lax.psum_scatter(grad_down, 'dp', scatter_dimension=1, tiled=True)  90.8 us
    pallas_call x1, Pallas kernels, line_sum(): pl.pallas_call(functools.partial(line_low_kernel, axis, n, chunks, 2), ou...  79.2 us
    reduce_scatter x1, waiting for transfers between devices, shards(): grad_out = lax.psum_scatter(grad_out, 'dp', scatter_dimension=1, tiled=True)  71.8 us
  transfers between devices with their start and end apart: 4, of which 3 were waited for; matrix products, arithmetic and copies ran while one was open for 1% of the time, Pallas kernels for 6%

profile of v8, /device:TPU:0, one launch (start us, length us, event | category | flops | bytes accessed | tf_op | source)
XLA Modules:
  0.0 1218.2 jit_solution(3948371665639959398)
XLA Ops:
  7.3 3.2 fusion
  10.5 0.2 copy-done
  10.7 2.7 fusion.19
  13.4 4.5 fusion.21
  18.0 0.3 multiply_reduce_fusion
  18.3 0.3 copy-done.17
  18.7 1.3 copy-done.10
  20.0 2.1 convolution_convert_fusion.v_ref
  22.1 0.1 fusion.6
  22.2 0.2 copy.37
  22.5 0.8 compare_select_fusion.own_ref
  23.3 0.6 reshape.251
  23.9 3.0 subtract_convert_fusion
  26.9 0.8 pad_maximum_fusion.1.k_ref
  27.8 2.5 multiply_convert_fusion.3
  30.3 4.4 fusion.27.raw_ref
  34.7 218.2 %attend.1 = (f32[1024,2048]{1,0:T(8,128)}, bf16[1024,1024]{1,0:T(8,128)(2,1)}, bf16[1024,1024]{1,0:T(8,128)(2,1)}, f32[4,1024,1]{2,1,0:T(8,128)}, bf16[1024,2048...) custom-call(f32[1024,1024]{1,0:T(8,128)} %fusion.27.raw_ref, bf16[1024,256]{1,0:T(8,128)(2,1)} %pad_maximum_fusion.1.k_ref, ...), custom_call_target="tpu_custom_call" | custom-call | tf_op jit(solution)/shard_map/attend/pallas_call | solution.py:923
  252.9 11.8 fusion.28
  264.7 14.2 %multiply_convert_fusion = (bf16[1024,1408]{1,0:T(8,128)(2,1)}, bf16[1024,1408]{1,0:T(8,128)(2,1)S(1)}, bf16[1024,1408]{1,0:T(8,128)(2,1)S(1)}) fusion(f32[1024,1408]{1,0:T(8,128)} %fusion.28, f32[1024,1408]{1,0:T(8,128)} %get-tuple-element.35, bf16[1024,2048]{1,0:T(8,128)(2,1)S(1)} %copy-done.5, bf16[2048,1408]{1,0:T(8,128)(2,1)} %param.25), kind=kOutput, calls=%fused_computation.5 | convolution fusion | flops 5928648704 | bytes 30146560 | tf_op jit(solution)/shard_map/dot_general | solution.py:1253
  278.9 8.9 fusion.29
  287.9 1.1 copy.40.scale_mid_ref
  288.9 2.3 fusion.3.pick_hbm
  291.3 1.0 copy.39.scale_one_ref
  292.3 12.9 %convolution_add_fusion.x_ref = f32[1024,2048]{1,0:T(8,128)} fusion(f32[1024,2048]{1,0:T(8,128)} %fusion.29, bf16[1024,1408]{1,0:T(8,128)(2,1)S(1)} %get-tuple-element.61.up_hbm, bf16[2048,1408]{1,0:T(8,128)(2,1)} %param.25), kind=kOutput, calls=%fused_computation.14 | convolution fusion | flops 5907677184 | bytes 25427968 | tf_op jit(solution)/shard_map/dot_general | solution.py:33
  305.1 202.9 %mid_sum.1 = (f32[1024,2048]{1,0:T(8,128)}, bf16[1024,2048]{1,0:T(8,128)(2,1)}, f32[8,2048]{1,0:T(8,128)}, f32[4096,1408]{1,0:T(8,128)}, f32[1408,2048]{1,0:T(8,...) custom-call(f32[1024,2048]{1,0:T(8,128)} %convolution_add_fusion.x_ref, f32[1024,1]{1,0:T(8,128)} %get-tuple-element.37.scale_ref, ...), custom_call_target="tpu_custom_call" | custom-call | tf_op jit(solution)/shard_map/mid_sum/pallas_call | solution.py:452
  508.0 147.2 %attend_back.1 = (bf16[640,2048]{1,0:T(8,128)(2,1)}, bf16[1024,1024]{1,0:T(8,128)(2,1)}, f32[1024,1536]{1,0:T(8,128)}, f32[1024,2048]{1,0:T(8,128)}) custom-call(f32[640,2048]{1,0:T(8,128)} %get-tuple-element.39.x_ref, bf16[1024,256]{1,0:T(8,128)(2,1)} %pad_maximum_fusion.1.k_ref, bf16[1024,256]{1,0:T(8,128)(2,1)} %convolution_convert_fusion.v_ref, ...), custom_call_target="tpu_custom_call" | custom-call | tf_op jit(solution)/shard_map/attend_back/pallas_call | solution.py:1148
  655.3 163.8 %tail_sum.1 = (bf16[1024,2048]{1,0:T(8,128)(2,1)}, f32[8,472,512]{2,1,0:T(8,128)}, f32[8,2048]{1,0:T(8,128)}, f32[8,1024]{1,0:T(8,128)}) custom-call(f32[1024,1536]{1,0:T(8,128)} %get-tuple-element.46.x_ref, f32[1024,1]{1,0:T(8,128)} %copy.39.scale_one_ref, f32[1024,1]{1,0:T(8,128)} %copy.40.scale_mid_ref, f32[1024,128]{1,0:T(8,128)} %get-tuple-element.75.cos_ref, ...), custom_call_target="tpu_custom_call" | custom-call | tf_op jit(solution)/shard_map/tail_sum/pallas_call | solution.py:687
  819.1 0.9 reduce_sum.63
  820.0 0.1 reshape.247
  820.1 0.8 reduce_sum.65
  821.2 1.6 dynamic_update_slice.3
  822.9 0.7 reduce-scatter.9.cloned.1.call-update
  823.6 0.7 reduce-scatter.7.cloned.1.call-update
  824.4 0.5 reduce-scatter.11.cloned.1.call-update
  824.9 79.2 %line_sum.1 = bf16[384,2048]{1,0:T(8,128)(2,1)} custom-call(f32[384,2048]{1,0:T(8,128)} %get-tuple-element.45.x_ref), custom_call_target="tpu_custom_call" | custom-call | tf_op jit(solution)/shard_map/line_sum/pallas_call | solution.py:183
  904.1 4.9 pad_maximum_fusion
  909.0 1.1 fusion.26
  910.1 0.7 pad_maximum_fusion.3
  910.8 1.1 fusion.25
  911.9 0.8 pad_maximum_fusion.2
  912.8 1.2 slice_bitcast_fusion.1
  914.0 1.3 slice_bitcast_fusion
  915.3 1.6 fusion.24
  916.9 123.4 %reduce-scatter.9.cloned.1.call-done = f32[512,1408]{1,0:T(8,128)} async-done(((f32[4096,1408]{1,0:T(8,128)}), f32[512,1408]{1,0:T(8,128)}) %reduce-scatter.9.cloned.1.call-update) | async-done | bytes 2883600 | tf_op jit(solution)/shard_map/reduce_scatter | solution.py:1275
  1040.3 3.6 fusion.23
  1043.9 71.8 %reduce-scatter.7.cloned.1.call-done = f32[1024,256]{1,0:T(8,128)} async-done(((f32[1024,2048]{1,0:T(8,128)}), f32[1024,256]{1,0:T(8,128)}) %reduce-scatter.7.cloned.1.call-update) | async-done | bytes 1048592 | tf_op jit(solution)/shard_map/reduce_scatter | solution.py:1298
  1115.7 90.8 %reduce-scatter.11.cloned.1.call-done = f32[1408,256]{1,0:T(8,128)} async-done(((f32[1408,2048]{1,0:T(8,128)}), f32[1408,256]{1,0:T(8,128)}) %reduce-scatter.11.cloned.1.call-update) | async-done | bytes 1441808 | tf_op jit(solution)/shard_map/reduce_scatter | solution.py:1276
  1206.5 4.8 copy.44
  (61 shorter events, 0.6 us)
Async XLA Ops:
  7.2 3.3 copy-start.15
  7.2 901.8 %reduce-scatter.5.cloned.1.call-start = ((), (), s32[]{:S(2)}) async-start(), calls=%async_computation.4 | async-start | bytes 8699904 | tf_op jit(solution)/shard_map/reduce_scatter | solution.py:1339
  7.2 3.5 copy-start
  10.7 8.0 copy-start.14
  10.7 2.7 copy-start.4
  17.9 4.2 copy-start.1
  17.9 0.7 copy-start.17
  18.0 2.0 copy-start.10
  20.0 7.8 copy-start.13
  20.0 2.1 copy-start.18
  20.0 3.3 copy-start.16
  22.2 8.1 copy-start.11
  22.5 5.3 copy-start.2
  27.8 2.5 copy-start.9
  30.3 4.4 copy-start.3
  252.9 11.8 copy-start.5
  252.9 26.0 %slice-start = ((s8[5767168]{0:T(1024)(128)(4,1)}), s8[4194304]{0:T(1024)(128)(4,1)S(1)}, s32[]{:S(2)}) async-start(s8[5767168]{0:T(1024)(128)(4,1)} %bitcast.46), calls=%async_computation.8 | async-start | bytes 8388608
  264.7 14.2 %slice-start.1 = ((s8[5767168]{0:T(1024)(128)(4,1)}), s8[1572864]{0:T(1024)(128)(4,1)S(1)}, s32[]{:S(2)}) async-start(s8[5767168]{0:T(1024)(128)(4,1)} %bitcast.46), calls=%async_computation.9 | async-start | bytes 3145728
  278.9 9.0 copy-start.6
  278.9 13.4 %copy-start.7 = (bf16[1024,1408]{1,0:T(8,128)(2,1)}, bf16[1024,1408]{1,0:T(8,128)(2,1)S(1)}, u32[]{:S(2)}) copy-start(bf16[1024,1408]{1,0:T(8,128)(2,1)S(1)} %get-tuple-element.61.up_hbm) | copy-start | bytes 8650756
  655.3 165.7 %copy-start.12 = (f32[8,2048]{1,0:T(8,128)S(1)}, f32[8,2048]{1,0:T(8,128)}, u32[]{:S(2)}) copy-start(f32[8,2048]{1,0:T(8,128)} %get-tuple-element.52) | copy-start | bytes 196612
  822.8 217.5 %reduce-scatter.9.cloned.1.call-start = ((), (), s32[]{:S(2)}) async-start(), calls=%async_computation.6 | async-start | bytes 25952256 | tf_op jit(solution)/shard_map/reduce_scatter | solution.py:1275
  823.6 292.1 %reduce-scatter.7.cloned.1.call-start = ((), (), s32[]{:S(2)}) async-start(), calls=%async_computation.5 | async-start | bytes 9437184 | tf_op jit(solution)/shard_map/reduce_scatter | solution.py:1298
  824.3 382.2 %reduce-scatter.11.cloned.1.call-start = ((), (), s32[]{:S(2)}) async-start(), calls=%async_computation.7 | async-start | bytes 12976128 | tf_op jit(solution)/shard_map/reduce_scatter | solution.py:1276
  824.9 79.2 %copy-start.8 = (bf16[640,2048]{1,0:T(8,128)(2,1)S(1)}, bf16[640,2048]{1,0:T(8,128)(2,1)}, u32[]{:S(2)}) copy-start(bf16[640,2048]{1,0:T(8,128)(2,1)} %get-tuple-element.44) | copy-start | bytes 7864324
Sparse Core Ops, SparseCore 0:
  822.9 67.3 reduce-scatter.4
  893.9 146.3 reduce-scatter.8
  1044.4 71.2 reduce-scatter.6
  1119.6 86.8 reduce-scatter.10

commit v9 on v8

--- a/solution.py
+++ b/solution.py
@@ -201,15 +201,16 @@
     n,
     chunks,
     lag,
-    x_ref,
     scale_ref,
     gain_ref,
-    mid_hbm,
-    act_hbm,
     gate_hbm,
     up_hbm,
+    gate_w_hbm,
+    up_w_hbm,
+    act_hbm,
     cot_hbm,
     down_hbm,
+    mid_hbm,
     hidden_hbm,
     d_hidden_ref,
     d_low_ref,
@@ -218,14 +219,17 @@
     grad_down_ref,
     one_ref,
     two_ref,
+    part,
     held,
     red,
-    mid_ref,
-    act_ref,
     gate_ref,
     up_ref,
+    gate_w_ref,
+    up_w_ref,
+    act_ref,
     cot_ref,
     down_ref,
+    mid_tile,
     wide_tile,
     row_tile,
     base_tile,
@@ -233,6 +237,7 @@
     d_tile,
     low_tile,
     load_sem,
+    mid_sem,
     wide_sem,
     row_sem,
     base_sem,
@@ -255,9 +260,10 @@
         pltpu.make_async_copy(src, dst, load_sem.at[i])
         for i, (src, dst) in enumerate(
             (
-                (mid_hbm, mid_ref),
                 (gate_hbm, gate_ref),
                 (up_hbm, up_ref),
+                (gate_w_hbm, gate_w_ref),
+                (up_w_hbm, up_w_ref),
                 (act_hbm, act_ref),
                 (cot_hbm, cot_ref),
                 (down_hbm, down_ref),
@@ -266,6 +272,30 @@
     ]
     for load in loads:
         load.start()
+
+    def take_mid(t):
+        cols = pl.ds(pl.multiple_of(t * wide, wide), wide)
+        slot = lax.rem(t, 2)
+        return pltpu.make_async_copy(mid_hbm.at[:, cols], mid_tile.at[slot], mid_sem.at[slot])
+
+    take_mid(0).start()
+    made = min(128, rows // 2)
+    pairs = rows // (2 * made)
+    pair_steps = chunks // pairs
+
+    def produce(i, carry):
+        side = lax.rem(i, 2)
+        side = jnp.where(2 * me >= n, side, 1 - side)
+        row_block = side * pairs + lax.div(i, 2)
+        own = pl.ds(pl.multiple_of(row_block * made, made), made)
+        part[own, :] = right_dot(gate_ref[own, :], gate_w_ref[...]) + right_dot(
+            up_ref[own, :], up_w_ref[...]
+        )
+        return carry
+
+    for load in loads[:4]:
+        load.wait()
+    produce(0, 0)
 
     def block(t):
         return pl.ds(pl.multiple_of(t * tile, tile), tile)
@@ -301,7 +331,7 @@
     def job(j, carry):
         @pl.when(j == 0)
         def _():
-            for load in loads:
+            for load in loads[4:]:
                 load.wait()
 
         for which, src in enumerate((gate_ref, up_ref)):
@@ -309,8 +339,14 @@
 
             @pl.when((j < tall_from) & (lax.rem(j, 2) == which))
             def _():
-                cols = pl.ds(pl.multiple_of(t * wide, wide), wide)
-                value = left_dot(mid_ref[:, cols], src[...])
+                if which == 0:
+                    take_mid(t).wait()
+
+                    @pl.when(t + 1 < wide_count)
+                    def _():
+                        take_mid(t + 1).start()
+
+                value = left_dot(mid_tile[lax.rem(t, 2)], src[...])
                 if which:
                     wide_copy(0, t).wait()
                 else:
@@ -373,6 +409,11 @@
         return carry
 
     def after_step(s, steps):
+        made_bounds = tuple(
+            jnp.minimum(1 + (at + 2) * 2 // pair_steps, 2 * pairs) for at in (s, s + 1)
+        )
+        made_from = jnp.where(s == 0, 1, made_bounds[0])
+        lax.fori_loop(made_from, made_bounds[1], produce, 0)
         late = steps - 4
         bounds = tuple(jnp.clip(at - 2, 0, late) * job_count // late for at in (s, s + 1))
         lax.fori_loop(*bounds, job, 0)
@@ -431,7 +472,7 @@
         for item in puts(half, c):
             item.start()
 
-    line_steps(axis, n, chunks, lag, x_ref, held, red, sems, lambda at: None, after_step)
+    line_steps(axis, n, chunks, lag, part, held, red, sems, lambda at: None, after_step)
     for half in (0, 1):
         for c in range(max(chunks - 2, 0), chunks):
             for item in puts(half, c):
@@ -440,31 +481,34 @@
     out_copy(two_ref, out_counts[1] - 1).wait()
 
 
-def mid_sum(x, scale, gain, mid, act, d_gate, d_up, cot, w_down, hidden, axis, n, parts, cid):
-    rows, width = x.shape
+def mid_sum(
+    scale, gain, d_gate, d_up, w_gate, w_up, act, cot, w_down, mid, hidden, axis, n, parts, cid
+):
+    rows, width = hidden.shape
     units = act.shape[1]
     tile = min(256, rows // 2)
     chunks = chunk_count(rows, 32, 16)
     vmem = pl.BlockSpec(memory_space=pltpu.VMEM)
     anywhere = pl.BlockSpec(memory_space=pl.ANY)
-    loaded = (mid, act, d_gate, d_up, cot, w_down)
+    loaded = (d_gate, d_up, w_gate, w_up, act, cot, w_down)
     tall = tile if units % 128 == 0 and units >= tile else max(tile, units)
     return pl.pallas_call(
         functools.partial(mid_kernel, axis, n, chunks, 2),
         out_shape=(
-            jax.ShapeDtypeStruct(x.shape, jnp.float32),
-            jax.ShapeDtypeStruct(x.shape, jnp.bfloat16),
+            jax.ShapeDtypeStruct(hidden.shape, jnp.float32),
+            jax.ShapeDtypeStruct(hidden.shape, jnp.bfloat16),
             jax.ShapeDtypeStruct((8, width), jnp.float32),
             jax.ShapeDtypeStruct((2 * width, units), jnp.float32),
             jax.ShapeDtypeStruct((units, width), jnp.float32),
             jax.ShapeDtypeStruct((rows * 5 // 8, width), jnp.float32),
             jax.ShapeDtypeStruct((rows - rows * 5 // 8, width), jnp.float32),
         ),
-        in_specs=[vmem] * 3 + [anywhere] * 7,
+        in_specs=[vmem] * 2 + [anywhere] * 9,
         out_specs=(anywhere, anywhere, vmem) + (anywhere,) * 4,
-        scratch_shapes=[pltpu.VMEM(x.shape, jnp.float32)] * 2
+        scratch_shapes=[pltpu.VMEM(hidden.shape, jnp.float32)] * 3
         + [pltpu.VMEM(item.shape, item.dtype) for item in loaded]
         + [
+            pltpu.VMEM((2, rows, width // parts), mid.dtype),
             pltpu.VMEM((width // parts, units), jnp.float32),
             pltpu.VMEM((tall, width), jnp.float32),
             pltpu.VMEM((rows // 8, width), jnp.float32),
@@ -472,15 +516,16 @@
             pltpu.VMEM((2, 2, rows // (2 * chunks), width), jnp.float32),
             pltpu.VMEM((2, 2, rows // (2 * chunks), width), jnp.bfloat16),
             pltpu.SemaphoreType.DMA((len(loaded),)),
+            pltpu.SemaphoreType.DMA((2,)),
         ]
         + [pltpu.SemaphoreType.DMA((1,))] * 3
         + [pltpu.SemaphoreType.DMA((2, 2))] * 3
         + [pltpu.SemaphoreType.DMA((2, chunks))] * 4,
         compiler_params=pltpu.CompilerParams(
-            collective_id=cid, has_side_effects=True, vmem_limit_bytes=62 << 20
+            collective_id=cid, has_side_effects=True, vmem_limit_bytes=67043328
         ),
         name="mid_sum",
-    )(x, scale, gain, *loaded, hidden)
+    )(scale, gain, *loaded, mid, hidden)
 
 
 def tail_kernel(
@@ -1141,7 +1186,7 @@
     cid,
 ):
     chunks = chunk_count(x.shape[0], 32, 16)
-    block = min(128, seq_len)
+    block = min(256, seq_len)
     vmem = pl.BlockSpec(memory_space=pltpu.VMEM)
     anywhere = pl.BlockSpec(memory_space=pl.ANY)
     loaded = (q, d_low, out_proj, q_up, mixed)
@@ -1255,17 +1300,17 @@
     hidden_act = (gate_pre * gate_sig * up_pre).astype(jnp.bfloat16)
     d_gate = (d_act * up_pre * gate_sig * (1.0 + gate_pre * (1.0 - gate_sig))).astype(jnp.bfloat16)
     d_up = (d_act * gate_pre * gate_sig).astype(jnp.bfloat16)
-    d_mid_part = right_dot(d_gate, w_gate) + right_dot(d_up, w_up)
     d_hidden, d_hidden_low, acc_two, grad_wide, grad_down, out_part_one, out_part_two = mid_sum(
-        d_mid_part,
         scale_two,
         gain_mlp.reshape(1, -1),
-        normed_mid,
-        hidden_act,
         d_gate,
         d_up,
+        w_gate,
+        w_up,
+        hidden_act,
         d_output,
         w_down,
+        normed_mid,
         hidden_in,
         "tensor",
         tp_count,

time: 1230 us -> 1210 us (0.984)
  matrix products: 61.5 us -> 39.9 us
    dot_general x2 -> x0, matrix products: 21.8 us -> none  [right_dot(): lax.dot_general(left, right, (((1,), (1,)), ((), ())), preferred_element_...]
  transfers between devices with their start and end apart: 4 -> 4, of which waited for: 3 -> 3; matrix products, arithmetic and copies ran while one was open for 1% -> 1% of each run, Pallas kernels for 6% -> 7%
where the time goes in v9:
time: 1210 us; the launch traced here: 1200 us
  Pallas kernels  817 us (68%)
  waiting for transfers between devices  283 us (23%)
  matrix products  39.9 us (3%)
  other arithmetic  24.4 us (2%)
  local copies, waits for them, and re-layouts  21 us (2%)
  between operations  14.3 us (1%)
    pallas_call x1, Pallas kernels, attend(): pl.pallas_call(functools.partial(attend_kernel, axis, n, chunks, 2, seq_l...  218 us
    pallas_call x1, Pallas kernels, mid_sum(): pl.pallas_call(functools.partial(mid_kernel, axis, n, chunks, 2), out_sha...  212 us
    pallas_call x1, Pallas kernels, tail_sum(): pl.pallas_call(functools.partial(tail_kernel, axis, n, chunks, 2, block),...  164 us
    pallas_call x1, Pallas kernels, attend_back(): pl.pallas_call(functools.partial(attend_back_kernel, axis, n, chunks, 2,...  140 us
    reduce_scatter x1, waiting for transfers between devices, shards(): lax.psum_scatter(grad_wide, 'dp', scatter_dimension=0, tiled=True)  119 us
    reduce_scatter x1, waiting for transfers between devices, shards(): lax.psum_scatter(grad_down, 'dp', scatter_dimension=1, tiled=True)  90.8 us
    pallas_call x1, Pallas kernels, line_sum(): pl.pallas_call(functools.partial(line_low_kernel, axis, n, chunks, 2), ou...  83.7 us
    reduce_scatter x1, waiting for transfers between devices, shards(): grad_out = lax.psum_scatter(grad_out, 'dp', scatter_dimension=1, tiled=True)  71.8 us
  transfers between devices with their start and end apart: 4, of which 3 were waited for; matrix products, arithmetic and copies ran while one was open for 1% of the time, Pallas kernels for 7%

profile of v9, /device:TPU:0, one launch (start us, length us, event | category | flops | bytes accessed | tf_op | source)
XLA Modules:
  0.0 1200.3 jit_solution(11883979203919181014)
XLA Ops:
  7.3 3.2 fusion
  10.5 0.2 copy-done
  10.7 2.7 fusion.19
  13.4 4.5 fusion.21
  18.0 0.3 multiply_reduce_fusion
  18.3 0.3 copy-done.13
  18.6 1.3 copy-done.6
  20.0 2.1 convolution_convert_fusion.v_ref
  22.1 0.1 fusion.6
  22.2 0.2 copy.37
  22.4 0.8 compare_select_fusion.own_ref
  23.3 0.6 reshape.251
  23.9 4.7 multiply_convert_fusion.3
  28.6 1.2 copy.40.scale_mid_ref
  29.8 2.3 fusion.3.pick_hbm
  32.2 1.0 copy.39.scale_one_ref
  33.2 3.2 subtract_convert_fusion
  36.4 0.8 pad_maximum_fusion.1.k_ref
  37.2 5.9 fusion.27.raw_ref
  43.2 218.1 %attend.1 = (f32[1024,2048]{1,0:T(8,128)}, bf16[1024,1024]{1,0:T(8,128)(2,1)}, bf16[1024,1024]{1,0:T(8,128)(2,1)}, f32[4,1024,1]{2,1,0:T(8,128)}, bf16[1024,2048...) custom-call(f32[1024,1024]{1,0:T(8,128)} %fusion.27.raw_ref, bf16[1024,256]{1,0:T(8,128)(2,1)} %pad_maximum_fusion.1.k_ref, ...), custom_call_target="tpu_custom_call" | custom-call | tf_op jit(solution)/shard_map/attend/pallas_call | solution.py:968
  261.3 11.9 fusion.28
  273.2 12.8 %multiply_convert_fusion = (bf16[1024,1408]{1,0:T(8,128)(2,1)}, bf16[1024,1408]{1,0:T(8,128)(2,1)}, bf16[1024,1408]{1,0:T(8,128)(2,1)}) fusion(f32[1024,1408]{1,0:T(8,128)} %fusion.28, f32[1024,1408]{1,0:T(8,128)S(1)} %copy-done.15, bf16[1024,2048]{1,0:T(8,128)(2,1)S(1)} %copy-done.3, bf16[2048,1408]{1,0:T(8,128)(2,1)S(1)} %bitcast.30), kind=kOutput, calls=%fused_computation.5 | convolution fusion | flops 5928648704 | bytes 30146560 | tf_op jit(solution)/shard_map/dot_general | solution.py:1298
  286.0 211.9 %mid_sum.1 = (f32[1024,2048]{1,0:T(8,128)}, bf16[1024,2048]{1,0:T(8,128)(2,1)}, f32[8,2048]{1,0:T(8,128)}, f32[4096,1408]{1,0:T(8,128)}, f32[1408,2048]{1,0:T(8,...) custom-call(f32[1024,1]{1,0:T(8,128)} %get-tuple-element.35.scale_ref, f32[1,2048]{1,0:T(1,128)} %bitcast.32, ...), custom_call_target="tpu_custom_call" | custom-call | tf_op jit(solution)/shard_map/mid_sum/pallas_call | solution.py:495
  497.9 139.6 %attend_back.1 = (bf16[640,2048]{1,0:T(8,128)(2,1)}, bf16[1024,1024]{1,0:T(8,128)(2,1)}, f32[1024,1536]{1,0:T(8,128)}, f32[1024,2048]{1,0:T(8,128)}) custom-call(f32[640,2048]{1,0:T(8,128)} %get-tuple-element.39.x_ref, bf16[1024,256]{1,0:T(8,128)(2,1)} %pad_maximum_fusion.1.k_ref, bf16[1024,256]{1,0:T(8,128)(2,1)} %convolution_convert_fusion.v_ref, ...), custom_call_target="tpu_custom_call" | custom-call | tf_op jit(solution)/shard_map/attend_back/pallas_call | solution.py:1193
  637.6 163.8 %tail_sum.1 = (bf16[1024,2048]{1,0:T(8,128)(2,1)}, f32[8,472,512]{2,1,0:T(8,128)}, f32[8,2048]{1,0:T(8,128)}, f32[8,1024]{1,0:T(8,128)}) custom-call(f32[1024,1536]{1,0:T(8,128)} %get-tuple-element.46.x_ref, f32[1024,1]{1,0:T(8,128)} %copy.39.scale_one_ref, f32[1024,1]{1,0:T(8,128)} %copy.40.scale_mid_ref, f32[1024,128]{1,0:T(8,128)} %get-tuple-element.75.cos_ref, ...), custom_call_target="tpu_custom_call" | custom-call | tf_op jit(solution)/shard_map/tail_sum/pallas_call | solution.py:732
  801.4 0.9 reduce_sum.63
  802.2 0.1 reshape.247
  802.3 0.8 reduce_sum.65
  803.1 0.1 reshape.249
  803.2 0.1 reshape.248
  803.4 1.6 dynamic_update_slice.3
  805.1 0.7 reduce-scatter.9.cloned.1.call-update
  805.9 0.7 reduce-scatter.7.cloned.1.call-update
  806.6 0.5 reduce-scatter.11.cloned.1.call-update
  807.2 83.7 %line_sum.1 = bf16[384,2048]{1,0:T(8,128)(2,1)} custom-call(f32[384,2048]{1,0:T(8,128)} %get-tuple-element.45.x_ref), custom_call_target="tpu_custom_call" | custom-call | tf_op jit(solution)/shard_map/line_sum/pallas_call | solution.py:183
  890.9 4.9 pad_maximum_fusion
  895.8 1.1 fusion.26
  896.9 0.7 pad_maximum_fusion.3
  897.6 1.1 fusion.25
  898.8 0.8 pad_maximum_fusion.2
  899.6 1.2 slice_bitcast_fusion.1
  900.8 1.3 slice_bitcast_fusion
  902.1 1.6 fusion.24
  903.7 118.9 %reduce-scatter.9.cloned.1.call-done = f32[512,1408]{1,0:T(8,128)} async-done(((f32[4096,1408]{1,0:T(8,128)}), f32[512,1408]{1,0:T(8,128)}) %reduce-scatter.9.cloned.1.call-update) | async-done | bytes 2883600 | tf_op jit(solution)/shard_map/reduce_scatter | solution.py:1320
  1022.6 3.6 fusion.23
  1026.2 71.8 %reduce-scatter.7.cloned.1.call-done = f32[1024,256]{1,0:T(8,128)} async-done(((f32[1024,2048]{1,0:T(8,128)}), f32[1024,256]{1,0:T(8,128)}) %reduce-scatter.7.cloned.1.call-update) | async-done | bytes 1048592 | tf_op jit(solution)/shard_map/reduce_scatter | solution.py:1343
  1098.0 90.8 %reduce-scatter.11.cloned.1.call-done = f32[1408,256]{1,0:T(8,128)} async-done(((f32[1408,2048]{1,0:T(8,128)}), f32[1408,256]{1,0:T(8,128)}) %reduce-scatter.11.cloned.1.call-update) | async-done | bytes 1441808 | tf_op jit(solution)/shard_map/reduce_scatter | solution.py:1321
  1188.7 4.8 copy.44
  (53 shorter events, 0.4 us)
Async XLA Ops:
  7.2 3.3 copy-start.11
  7.2 888.6 %reduce-scatter.5.cloned.1.call-start = ((), (), s32[]{:S(2)}) async-start(), calls=%async_computation.4 | async-start | bytes 8699904 | tf_op jit(solution)/shard_map/reduce_scatter | solution.py:1384
  7.2 3.5 copy-start
  10.7 8.0 copy-start.10
  10.7 2.7 copy-start.4
  17.9 4.2 copy-start.1
  17.9 0.7 copy-start.13
  17.9 2.0 copy-start.6
  20.0 3.9 copy-start.9
  20.0 2.1 copy-start.14
  20.0 3.3 copy-start.12
  22.2 6.4 copy-start.7
  28.6 14.6 %copy-start.2 = (bf16[1024,1024]{1,0:T(8,128)(2,1)}, bf16[1024,1024]{1,0:T(8,128)(2,1)S(1)}, u32[]{:S(2)}) copy-start(bf16[1024,1024]{1,0:T(8,128)(2,1)S(1)} %get-tuple-element.57.q_hbm) | copy-start | bytes 6291460
  43.2 230.1 %slice-start = ((s8[5767168]{0:T(1024)(128)(4,1)}), s8[1572864]{0:T(1024)(128)(4,1)S(1)}, s32[]{:S(2)}) async-start(s8[5767168]{0:T(1024)(128)(4,1)} %bitcast.29), calls=%async_computation.8 | async-start | bytes 3145728
  261.3 11.9 slice-start.1
  261.3 11.9 copy-start.3
  261.3 11.9 copy-start.15
  637.6 165.7 %copy-start.8 = (f32[8,2048]{1,0:T(8,128)S(1)}, f32[8,2048]{1,0:T(8,128)}, u32[]{:S(2)}) copy-start(f32[8,2048]{1,0:T(8,128)} %get-tuple-element.52) | copy-start | bytes 196612
  805.1 217.5 %reduce-scatter.9.cloned.1.call-start = ((), (), s32[]{:S(2)}) async-start(), calls=%async_computation.6 | async-start | bytes 25952256 | tf_op jit(solution)/shard_map/reduce_scatter | solution.py:1320
  805.8 292.1 %reduce-scatter.7.cloned.1.call-start = ((), (), s32[]{:S(2)}) async-start(), calls=%async_computation.5 | async-start | bytes 9437184 | tf_op jit(solution)/shard_map/reduce_scatter | solution.py:1343
  806.6 382.2 %reduce-scatter.11.cloned.1.call-start = ((), (), s32[]{:S(2)}) async-start(), calls=%async_computation.7 | async-start | bytes 12976128 | tf_op jit(solution)/shard_map/reduce_scatter | solution.py:1321
  807.1 83.7 %copy-start.5 = (bf16[640,2048]{1,0:T(8,128)(2,1)S(1)}, bf16[640,2048]{1,0:T(8,128)(2,1)}, u32[]{:S(2)}) copy-start(bf16[640,2048]{1,0:T(8,128)(2,1)} %get-tuple-element.44) | copy-start | bytes 7864324
Sparse Core Ops, SparseCore 0:
  805.2 67.3 reduce-scatter.4
  876.2 146.3 reduce-scatter.8
  1026.6 71.2 reduce-scatter.6
  1101.9 86.8 reduce-scatter.10
